TPU v7x, 32 devices: a whole 2x2x4 slice. The times are simulated.
32 devices in a mesh: parts: 2 (over y), row: 4 (over x, core), col: 4 (over z).
Axes of the slice: x: 2, y: 2, z: 4, core: 2. Of those that a mesh axis runs over, the one named last changes fastest.
Arguments:
- alignment_tensor: bfloat16 [256, 256, 256], P(('parts', 'col'), 'row'), parts along dimension 0, may hold values from -6 to 6
- standardizer_scaling: float32 [256], replicated, may hold values from 0.25 to 1.75
- standardizer_offset: float32 [256], replicated, may hold values from -3 to 3
- first_projector: bfloat16 [256, 32], replicated, may hold values from -0.375 to 0.375
- second_projector: bfloat16 [256, 32], replicated, may hold values from -0.375 to 0.375
- final_projector: bfloat16 [1024, 128], replicated, may hold values from -1 to 1
- final_offset: float32 [128], replicated, may hold values from -3 to 3
- amino_strand_label: int32 [512], P('parts'), parts along dimension 0, may hold values from 0 to 7, never falling along the last dimension, each value on 1 to 128 neighbouring positions
- matched_strand_count: int32 [16, 8], P('parts'), parts along dimension 0, may hold values from 32 to 128, as said below
- couple_delta_adjoint: bfloat16 [512, 256, 128], P(('parts', 'row'), 'col'), parts along dimension 0, may hold values from -6 to 6
Outputs:
- pair_update: bfloat16 [512, 256, 128], P(('parts', 'row'), 'col'), parts along dimension 0
- adjoint_first_factor: bfloat16 [256, 8192], P(('parts', 'col'), 'row'), parts along dimension 0
- grad_right: bfloat16 [256, 8192], P(('parts', 'col'), 'row'), parts along dimension 0
- grad_w_out: float32 [2048, 128], P('parts'), parts along dimension 0
There are 2 independent parts, one for each index of `parts`. A program takes and returns all parts, laid end to end along the dimension named above; an argument that names none is the same for every part. Nothing has to cross between parts.
Inputs may be any that keep to these rules, and one draw needn't show every extreme that they name: `amino_strand_label`: chain numbers never fall along the residues; a chain has 1 to 128 residues. `matched_strand_count`: every entry is a multiple of 32.
All inputs are finite; a program needn't handle non-finite values.
Results may differ from a plain program's by a relative error of at most 0.018.
Values may be sent and summed in bfloat16 or wider, within the bound.
A program may use at most 256 MiB of HBM per device.

v0:
```python
import functools

import jax
import jax.numpy as jnp
from jax import lax
from jax.experimental import pallas as pl
from jax.experimental.pallas import tpu as pltpu
from jax.sharding import PartitionSpec as P

PROJECTED_SIZE = 32
CZ = 128
WINDOW_AMINOS = 256
DEPTH_STEP = 32
CHAINS = 8
LEVELS = 4


def standardize_entries(alignment_tensor, standard_multiplier, additive_offset):
    incoming_entries = alignment_tensor.astype(jnp.float32)
    center = incoming_entries - jnp.mean(incoming_entries, axis=-1, keepdims=True)
    spread = jnp.mean(center * center, axis=-1, keepdims=True)
    return (center * lax.rsqrt(spread + 1e-05) * standard_multiplier + additive_offset).astype(
        jnp.bfloat16
    )


def pair_kernel(
    group, cols, seqs, levels,
    left_ref, right_ref, depth_ref, grad_ref, weight_ref, weight_t_ref, bias_ref, left_t_ref,
    tall_ref,
    pair_ref, left_grad_ref, right_grad_ref, weight_grad_ref,
    outer_ref, scaled_ref, back_ref,
):
    step = pl.program_id(0)
    width = group * cols
    size = PROJECTED_SIZE
    chunk = 4
    depth = depth_ref[0]
    inverse = 1.0 / depth
    row = lax.broadcasted_iota(jnp.int32, (group * seqs, width), 0)
    lane = lax.broadcasted_iota(jnp.int32, (group * seqs, width), 1)
    seq = (row % seqs).astype(jnp.float32)
    keep = jnp.where(
        jnp.logical_and(row // seqs == lane // cols, seq < depth), 1.0, 0.0
    ).astype(jnp.bfloat16)
    keep = jnp.concatenate([keep] * chunk, axis=1)
    grad = grad_ref[...]
    back = lax.dot_general(
        weight_ref[...], grad, (((1,), (1,)), ((), ())), preferred_element_type=jnp.float32
    )
    back_ref[...] = (back * inverse).astype(jnp.bfloat16)
    left = left_ref[0]
    left_grad = jnp.zeros((size, group * seqs), jnp.float32)
    rows_here = pl.ds(pl.multiple_of(step * size, size), size)
    for first in range(0, size, chunk):
        lanes = slice(first * width, (first + chunk) * width)
        right = right_ref[:, lanes] * keep
        prod = jnp.dot(left, right, preferred_element_type=jnp.float32)
        for e in range(chunk):
            outer_ref[(first + e) * size : (first + e + 1) * size, :] = (
                prod[:, e * width : (e + 1) * width] * inverse
            ).astype(jnp.bfloat16)
        scaled = jnp.concatenate(
            [back_ref[(first + e) * size : (first + e + 1) * size, :] for e in range(chunk)], axis=1
        )
        scaled_ref[rows_here, lanes] = scaled
        left_grad = left_grad + lax.dot_general(
            scaled, right, (((1,), (1,)), ((), ())), preferred_element_type=jnp.float32
        )
    left_grad_ref[0] = left_grad.astype(jnp.bfloat16)
    outer = outer_ref[...]
    pair = jnp.dot(weight_t_ref[...], outer, preferred_element_type=jnp.float32).T
    pair_ref[...] = (pair + bias_ref[...]).astype(jnp.bfloat16)
    weight_part = jnp.dot(outer, grad, preferred_element_type=jnp.float32)

    @pl.when(step == 0)
    def _():
        weight_grad_ref[...] = weight_part

    @pl.when(step > 0)
    def _():
        weight_grad_ref[...] += weight_part

    @pl.when(step == pl.num_programs(0) - 1)
    def _():
        span = 2
        part = lax.broadcasted_iota(jnp.int32, (DEPTH_STEP, span * width), 1) % width // cols
        for level in range(levels):
            wanted = jnp.where(tall_ref[...] > level * DEPTH_STEP, 1.0, 0.0).astype(jnp.bfloat16)
            wanted = jnp.concatenate([wanted] * span, axis=1)

            def piece(index, carry, level=level, wanted=wanted):
                lanes = pl.ds(pl.multiple_of(index * span * width, span * width), span * width)
                masked = scaled_ref[:, lanes] * wanted
                out = jnp.dot(left_t_ref[level], masked, preferred_element_type=jnp.float32)
                total = jnp.zeros((DEPTH_STEP, span * width), jnp.float32)
                for g in range(group):
                    total = jnp.where(part == g, out[g * DEPTH_STEP : (g + 1) * DEPTH_STEP], total)
                right_grad_ref[level * DEPTH_STEP : (level + 1) * DEPTH_STEP, lanes] = total
                return carry

            lax.fori_loop(0, size // span, piece, 0)


def to(source, target, send, recv, row, col):
    return pltpu.make_async_remote_copy(
        src_ref=source,
        dst_ref=target,
        send_sem=send,
        recv_sem=recv,
        device_id={"row": row, "col": col},
        device_id_type=pl.DeviceIdType.MESH,
    )


def arrived(ref, sem):
    pltpu.make_async_copy(ref, ref, sem).wait()


def greet(n_row, n_col, me):
    peers = n_row * n_col
    barrier = pltpu.get_barrier_semaphore()

    def signal(off, carry):
        peer = (me + off) % peers
        pl.semaphore_signal(
            barrier,
            inc=1,
            device_id={"row": peer // n_col, "col": peer % n_col},
            device_id_type=pl.DeviceIdType.MESH,
        )
        return carry

    lax.fori_loop(1, peers, signal, 0)
    pl.semaphore_wait(barrier, peers - 1)


def sum_kernel(
    n_row, n_col, ratio,
    left_ref, right_ref, weight_ref,
    left_out, right_out, weight_out,
    left_in, right_in, weight_in, reduced, total,
    left_send, left_recv, right_send, right_recv,
    weight_send, weight_recv, total_send, total_recv,
):
    row, col = lax.axis_index("row"), lax.axis_index("col")
    me = row * n_col + col
    peers = n_row * n_col
    part = weight_ref.shape[0] // peers
    greet(n_row, n_col, me)

    def weight_copy(off):
        peer = (me + off) % peers
        source = weight_ref.at[pl.ds(pl.multiple_of(peer * part, part), part)]
        return to(
            source, weight_in.at[me], weight_send.at[off], weight_recv.at[me],
            peer // n_col, peer % n_col,
        )

    def total_copy(off):
        peer = (me + off) % peers
        return to(
            reduced, total.at[me], total_send.at[off], total_recv.at[me],
            peer // n_col, peer % n_col,
        )

    def left_copy(off):
        peer = (col + off) % n_col
        return to(
            left_ref.at[peer], left_in.at[col], left_send.at[off], left_recv.at[col], row, peer
        )

    owner = col // ratio
    slot = row * ratio + col % ratio

    def right_copy(off):
        peer = (col + off) % n_col
        return to(
            right_ref.at[peer], right_in.at[slot], right_send.at[off], right_recv.at[slot],
            owner, peer,
        )

    def start(make):
        def body(off, carry):
            make(off).start()
            return carry

        return body

    def sent(make):
        def body(off, carry):
            make(off).wait_send()
            return carry

        return body

    lax.fori_loop(1, peers, start(weight_copy), 0)
    lax.fori_loop(1, n_col, start(right_copy), 0)

    @pl.when(owner == row)
    def _():
        pltpu.make_async_copy(right_ref.at[col], right_in.at[slot], right_recv.at[slot]).start()

    @pl.when(owner != row)
    def _():
        right_copy(0).start()

    lax.fori_loop(1, n_col, start(left_copy), 0)

    def add_weight(off, acc):
        peer = (me + off) % peers
        arrived(weight_in.at[peer], weight_recv.at[peer])
        return acc + weight_in[peer]

    own = weight_ref[pl.ds(pl.multiple_of(me * part, part), part), :]
    mine = lax.fori_loop(1, peers, add_weight, own)
    reduced[...] = mine
    total[me] = mine
    lax.fori_loop(1, peers, sent(weight_copy), 0)
    lax.fori_loop(1, peers, start(total_copy), 0)

    def wait_left(off, carry):
        peer = (col + off) % n_col
        arrived(left_in.at[peer], left_recv.at[peer])
        return carry

    lax.fori_loop(1, n_col, wait_left, 0)
    left_total = left_ref[col].astype(jnp.float32)
    for off in range(1, n_col):
        left_total = left_total + left_in[(col + off) % n_col].astype(jnp.float32)
    left_out[...] = left_total.astype(jnp.bfloat16)
    width = right_in.shape[2]
    for t in range(ratio):
        right_total = jnp.zeros(right_in.shape[1:], jnp.float32)
        for r in range(n_row):
            arrived(right_in.at[r * ratio + t], right_recv.at[r * ratio + t])
            right_total = right_total + right_in[r * ratio + t].astype(jnp.float32)
        right_out[:, t * width : (t + 1) * width] = right_total.astype(jnp.bfloat16)

    def wait_total(off, carry):
        peer = (me + off) % peers
        arrived(total.at[peer], total_recv.at[peer])
        return carry

    lax.fori_loop(1, peers, wait_total, 0)
    weight_out[...] = total[...].reshape(weight_out.shape)
    lax.fori_loop(1, peers, sent(total_copy), 0)
    lax.fori_loop(1, n_col, sent(left_copy), 0)
    lax.fori_loop(1, n_col, sent(right_copy), 0)

    @pl.when(owner != row)
    def _():
        right_copy(0).wait_send()


def shards(
    alignment_tensor,
    standardizer_scaling,
    standardizer_offset,
    first_projector,
    second_projector,
    final_projector,
    final_offset,
    amino_strand_label,
    matched_strand_count,
    couple_delta_adjoint,
):
    homolog_portion, rows, embedding_extent = alignment_tensor.shape
    cols = couple_delta_adjoint.shape[1]
    size = PROJECTED_SIZE
    entries = standardize_entries(
        alignment_tensor, standardizer_scaling, standardizer_offset
    ).reshape(-1, embedding_extent)
    both = jnp.dot(
        entries,
        jnp.concatenate([first_projector, second_projector], axis=1),
        preferred_element_type=jnp.float32,
    ).astype(jnp.bfloat16)
    first_factor = both[:, :size].reshape(homolog_portion, rows * size)
    second_factor = both[:, size:].reshape(homolog_portion, rows * size)
    left_panel = lax.all_gather(first_factor, "col", axis=0, tiled=True)
    right_rows = lax.all_gather(second_factor, "row", axis=1, tiled=True)
    right_panel = lax.all_to_all(right_rows, "col", split_axis=1, concat_axis=0, tiled=True)
    seqs = left_panel.shape[0]
    levels = seqs // DEPTH_STEP
    row_start = lax.axis_index("row") * rows
    col_start = lax.axis_index("col") * cols
    chains = jnp.arange(CHAINS, dtype=jnp.int32)
    row_hot = (
        lax.dynamic_slice_in_dim(amino_strand_label, row_start, rows, 0)[:, None] == chains[None, :]
    ).astype(jnp.float32)
    col_hot = (
        lax.dynamic_slice_in_dim(amino_strand_label, col_start, cols, 0)[:, None] == chains[None, :]
    ).astype(jnp.float32)
    table = matched_strand_count.astype(jnp.float32)
    depth = jnp.dot(
        jnp.dot(row_hot, table, precision=lax.Precision.HIGHEST),
        col_hot.T,
        precision=lax.Precision.HIGHEST,
    )
    group = max(1, 128 // cols)
    width = group * cols
    steps = rows // group
    left4 = left_panel.reshape(seqs, steps, group, size)
    left_groups = left4.transpose(1, 3, 2, 0).reshape(steps, size, group * seqs)
    left_levels = (
        left_panel.reshape(levels, DEPTH_STEP, steps, group, size)
        .transpose(0, 3, 1, 2, 4)
        .reshape(levels, group * DEPTH_STEP, steps * size)
    )
    right_turned = right_panel.reshape(seqs, cols, size).transpose(0, 2, 1)
    right_wide = jnp.broadcast_to(
        right_turned[None, :, :, None, :], (group, seqs, size, group, cols)
    ).reshape(group * seqs, size * width)
    depth_rows = depth.reshape(steps, 1, width)
    depth_tall = jnp.broadcast_to(depth_rows, (steps, size, width)).reshape(steps * size, width)
    weight = final_projector.reshape(size, size, CZ).transpose(1, 0, 2).reshape(size * size, CZ)
    flat_grad = couple_delta_adjoint.reshape(-1, CZ)
    whole = lambda shape: pl.BlockSpec(shape, lambda g: (0,) * len(shape))
    pair, left_grad, right_grad, weight_part = pl.pallas_call(
        functools.partial(pair_kernel, group, cols, seqs, levels),
        grid=(steps,),
        in_specs=[
            pl.BlockSpec((1, size, group * seqs), lambda g: (g, 0, 0)),
            whole((group * seqs, size * width)),
            pl.BlockSpec((1, 1, width), lambda g: (g, 0, 0)),
            pl.BlockSpec((width, CZ), lambda g: (g, 0)),
            whole((size * size, CZ)),
            whole((CZ, size * size)),
            whole((1, CZ)),
            whole((levels, group * DEPTH_STEP, steps * size)),
            whole((steps * size, width)),
        ],
        out_specs=[
            pl.BlockSpec((width, CZ), lambda g: (g, 0)),
            pl.BlockSpec((1, size, group * seqs), lambda g: (g, 0, 0)),
            whole((seqs, size * width)),
            whole((size * size, CZ)),
        ],
        out_shape=[
            jax.ShapeDtypeStruct((steps * width, CZ), jnp.bfloat16),
            jax.ShapeDtypeStruct((steps, size, group * seqs), jnp.bfloat16),
            jax.ShapeDtypeStruct((seqs, size * width), jnp.float32),
            jax.ShapeDtypeStruct((size * size, CZ), jnp.float32),
        ],
        scratch_shapes=[
            pltpu.VMEM((size * size, width), jnp.bfloat16),
            pltpu.VMEM((steps * size, size * width), jnp.bfloat16),
            pltpu.VMEM((size * size, width), jnp.bfloat16),
        ],
        compiler_params=pltpu.CompilerParams(
            dimension_semantics=("arbitrary",), vmem_limit_bytes=56 * 1024 * 1024
        ),
    )(
        left_groups,
        right_wide,
        depth_rows,
        flat_grad,
        weight,
        weight.T,
        final_offset[None, :],
        left_levels,
        depth_tall,
    )
    pair_update = pair.reshape(rows, cols, CZ)
    left_sum = (
        left_grad.reshape(steps, size, group, seqs).transpose(3, 0, 2, 1).reshape(seqs, rows * size)
    )
    right_sum = (
        right_grad.reshape(seqs, size, group, cols)
        .sum(axis=2)
        .astype(jnp.bfloat16)
        .transpose(0, 2, 1)
        .reshape(seqs, cols * size)
    )
    n_row, n_col = lax.axis_size("row"), lax.axis_size("col")
    ratio = rows // cols
    peers = n_row * n_col
    vmem = pl.BlockSpec(memory_space=pltpu.VMEM)
    share = seqs // n_col
    part = weight_part.shape[0] // peers
    dma = pltpu.SemaphoreType.DMA
    adjoint_first_factor, grad_right, weight_total = pl.pallas_call(
        functools.partial(sum_kernel, n_row, n_col, ratio),
        in_specs=[vmem] * 3,
        out_specs=[vmem] * 3,
        out_shape=[
            jax.ShapeDtypeStruct((share, rows * size), jnp.bfloat16),
            jax.ShapeDtypeStruct((share, rows * size), jnp.bfloat16),
            jax.ShapeDtypeStruct(weight_part.shape, jnp.float32),
        ],
        scratch_shapes=[
            pltpu.VMEM((n_col, share, rows * size), jnp.bfloat16),
            pltpu.VMEM((n_row * ratio, share, cols * size), jnp.bfloat16),
            pltpu.VMEM((peers, part, CZ), jnp.float32),
            pltpu.VMEM((part, CZ), jnp.float32),
            pltpu.VMEM((peers, part, CZ), jnp.float32),
            dma((n_col,)),
            dma((n_col,)),
            dma((n_col,)),
            dma((n_row * ratio,)),
            dma((peers,)),
            dma((peers,)),
            dma((peers,)),
            dma((peers,)),
        ],
        compiler_params=pltpu.CompilerParams(collective_id=0, has_side_effects=True),
    )(
        left_sum.reshape(n_col, share, rows * size),
        right_sum.reshape(n_col, share, cols * size),
        weight_part,
    )
    grad_w_out = (
        weight_total.reshape(size, size, CZ).transpose(1, 0, 2).reshape(size * size, CZ)
        / WINDOW_AMINOS
    )
    return (pair_update, adjoint_first_factor, grad_right, grad_w_out)


def solution(mesh):
    in_specs = (
        P(("parts", "col"), "row", None),
        P(),
        P(),
        P(),
        P(),
        P(),
        P(),
        P("parts"),
        P("parts", None),
        P(("parts", "row"), "col", None),
    )
    out_specs = (
        P(("parts", "row"), "col", None),
        P(("parts", "col"), "row"),
        P(("parts", "col"), "row"),
        P("parts", None),
    )
    return jax.shard_map(shards, mesh=mesh, in_specs=in_specs, out_specs=out_specs, check_vma=False)
```

profile of v0, /device:TPU:1, one launch (start us, length us, event | category | flops | bytes accessed | tf_op | source)
XLA Modules:
  0.0 201.8 jit_solution(13278679215754601313)
XLA Ops:
  0.6 0.0 copy-start
  0.7 1.6 convert_reduce_fusion
  2.3 1.9 fusion.2
  4.3 0.7 fusion.5
  5.0 0.4 convolution_convert_fusion
  5.5 0.0 copy-start.9
  5.5 0.0 copy-start.10
  5.5 0.3 copy.46
  5.8 0.5 reshape.91
  6.3 8.5 %all_gather.7 = bf16[32,8192]{1,0:T(8,128)(2,1)S(1)} all-gather(bf16[32,2048]{1,0:T(8,128)(2,1)S(1)} %reshape.91), channel_id=1, replica_groups=mesh['parts'=2,'row'=4,'col'=4] {'row'}, dimensions={1}, use_global_device_ids=true | all-gather | bytes 655360 | tf_op jit(solution)/shard_map/all_gather | solution.py:282
  14.8 0.8 copy.65
  15.7 4.6 %all-to-all-start = ((bf16[32,4,2048]{2,0,1:T(8,128)(2,1)}), bf16[32,4,2048]{2,0,1:T(8,128)(2,1)S(1)}, u32[]{:S(2)}, u32[]{:S(2)}) async-start(bf16[32,4,2048]{2,0,1:T(8,128)(2,1)} %bitcast.43), calls=%async_computation | async-start | bytes 1048576 | tf_op jit(solution)/shard_map/all_to_all | solution.py:283
  20.3 0.1 fusion.16
  20.3 0.2 fusion.9
  20.5 0.3 fusion.10
  20.8 0.1 broadcast_in_dim.10
  20.9 0.7 reshape.94.depth_ref
  21.6 0.3 copy.43
  21.9 0.5 reshape.88
  22.4 0.0 copy-start.2
  22.4 19.8 %all_gather.6 = bf16[128,2048]{1,0:T(8,128)(2,1)S(1)} all-gather(bf16[32,2048]{1,0:T(8,128)(2,1)S(1)} %reshape.88), channel_id=1, replica_groups=mesh['parts'=2,'row'=4,'col'=4] {'col'}, dimensions={0}, use_global_device_ids=true | all-gather | bytes 655360 | tf_op jit(solution)/shard_map/all_gather | solution.py:281
  42.2 1.0 copy.44
  43.2 1.6 reshape.98
  44.8 0.1 copy.49
  45.0 0.8 copy.50
  45.8 1.9 copy.64
  47.7 1.7 copy.51
  49.5 4.2 %reshape.99.left_t_ref = bf16[4,64,1024]{2,1,0:T(8,128)(2,1)} reshape(bf16[4,2,32,32,32]{4,3,2,1,0:T(8,128)(2,1)} %copy.51) | data formatting | bytes 1048576 | tf_op jit(solution)/shard_map/reshape | solution.py:309
  53.7 0.0 all-to-all-done
  53.7 1.6 reshape.92
  55.3 2.6 %copy.48 = bf16[128,32,64]{0,2,1:T(8,128)(2,1)S(1)} copy(bf16[128,32,64]{1,2,0:T(8,128)(2,1)S(1)} %bitcast.44) | data formatting | bytes 1048576 | tf_op jit(solution)/shard_map/transpose | solution.py:311
  57.9 2.0 %broadcast_in_dim.8 = bf16[2,128,32,2,64]{1,0,4,3,2:T(2,128)(2,1)S(1)} broadcast(bf16[128,32,64]{0,2,1:T(8,128)(2,1)S(1)} %copy.48), dimensions={1,2,4} | broadcast | bytes 2621440 | tf_op jit(solution)/shard_map/broadcast_in_dim | solution.py:312
  60.0 0.3 copy.63
  60.2 3.0 %copy.52.right_ref = bf16[256,4096]{1,0:T(8,128)(2,1)} copy(bf16[256,4096]{0,1:T(8,128)(2,1)S(1)} %bitcast.49) | data formatting | bytes 4194304 | tf_op jit(solution)/shard_map/reshape | solution.py:314
  63.2 0.9 broadcast_in_dim.11
  64.1 63.5 %shard_map.129 = (bf16[4096,128]{1,0:T(8,128)(2,1)}, bf16[32,32,256]{2,1,0:T(8,128)(2,1)}, f32[128,4096]{1,0:T(8,128)}, f32[1024,128]{1,0:T(8,128)}) custom-call(bf16[32,32,256]{2,1,0:T(8,128)(2,1)} %bitcast.58, bf16[256,4096]{1,0:T(8,128)(2,1)} %copy.52.right_ref, f32[32,1,128]{2,1,0:T(1,128)} %reshape.94.depth_ref, bf16[4096,128]{1,0:T(8,128)(2,1)} %bitcast.60, ...), custom_call_target="tpu_custom_call" | custom-call | tf_op jit(solution)/shard_map/pallas_call | solution.py:320
  127.6 1.2 reshape.102
  128.8 2.0 copy.53
  130.8 3.0 %reshape_reshape.6.left_ref = bf16[4,32,2048]{2,1,0:T(8,128)(2,1)} reshape(bf16[128,32,2,32]{3,2,1,0:T(2,128)(2,1)S(1)} %bitcast.45) | data formatting | bytes 1048576 | tf_op jit(solution)/shard_map/reshape;reshape | solution.py:409
  133.7 1.9 copy.54
  135.7 0.2 reduce_sum.29
  135.8 3.2 %copy.55 = bf16[128,64,32]{2,1,0:T(8,128)(2,1)S(1)} copy(bf16[128,64,32]{0,1,2:T(8,128)(2,1)S(1)} %bitcast.56) | data formatting | bytes 1048576 | tf_op jit(solution)/shard_map/convert_element_type | solution.py:372
  139.1 3.0 %reshape_reshape.7.right_ref = bf16[4,32,2048]{2,1,0:T(8,128)(2,1)} reshape(bf16[128,64,32]{2,1,0:T(8,128)(2,1)S(1)} %copy.55) | data formatting | bytes 1048576 | tf_op jit(solution)/shard_map/reshape;reshape | solution.py:410
  142.1 56.1 %shard_map.130 = (bf16[32,2048]{1,0:T(8,128)(2,1)}, bf16[32,2048]{1,0:T(8,128)(2,1)}, f32[1024,128]{1,0:T(8,128)}) custom-call(bf16[4,32,2048]{2,1,0:T(8,128)(2,1)} %reshape_reshape.6.left_ref, bf16[4,32,2048]{2,1,0:T(8,128)(2,1)} %reshape_reshape.7.right_ref, f32[1024,128]{1,0:T(8,128)} %get-tuple-element.14.weight_ref), custom_call_target="tpu_custom_call" | custom-call | tf_op jit(solution)/shard_map/pallas_call | solution.py:383
  198.2 1.1 broadcast_multiply_fusion
  199.3 1.1 copy.56
  200.4 0.7 copy.68
  201.1 0.7 copy.69
  (21 shorter events, 0.1 us)
Async XLA Ops:
  0.6 3.6 %copy-start = (bf16[32,64,256]{2,1,0:T(8,128)(2,1)S(1)}, bf16[32,64,256]{2,1,0:T(8,128)(2,1)}, u32[]{:S(2)}) copy-start(bf16[32,64,256]{2,1,0:T(8,128)(2,1)} %param.10) | copy-start | bytes 3145732
  0.6 3.6 %copy-start.7 = (f32[256]{0:T(256)S(1)}, f32[256]{0:T(256)}, u32[]{:S(2)}) copy-start(f32[256]{0:T(256)} %param.12) | copy-start | bytes 3076
  0.7 3.6 %copy-start.8 = (f32[256]{0:T(256)S(1)}, f32[256]{0:T(256)}, u32[]{:S(2)}) copy-start(f32[256]{0:T(256)} %param.11) | copy-start | bytes 3076
  0.7 4.3 %copy-start.5 = (bf16[256,32]{0,1:T(8,128)(2,1)S(1)}, bf16[256,32]{0,1:T(8,128)(2,1)}, u32[]{:S(2)}) copy-start(bf16[256,32]{0,1:T(8,128)(2,1)} %param.14) | copy-start | bytes 49156
  0.7 4.3 %copy-start.6 = (bf16[256,32]{0,1:T(8,128)(2,1)S(1)}, bf16[256,32]{0,1:T(8,128)(2,1)}, u32[]{:S(2)}) copy-start(bf16[256,32]{0,1:T(8,128)(2,1)} %param.13) | copy-start | bytes 49156
  5.5 14.8 %copy-start.9 = (s32[256]{0:T(256)S(1)}, s32[256]{0:T(256)}, u32[]{:S(2)}) copy-start(s32[256]{0:T(256)} %param.17) | copy-start | bytes 3076
  5.5 14.8 %copy-start.10 = (s32[8,8]{1,0:T(8,128)S(1)}, s32[8,8]{1,0:T(8,128)}, u32[]{:S(2)}) copy-start(s32[8,8]{1,0:T(8,128)} %param.18) | copy-start | bytes 772
  15.7 38.0 %all-to-all-start = ((bf16[32,4,2048]{2,0,1:T(8,128)(2,1)}), bf16[32,4,2048]{2,0,1:T(8,128)(2,1)S(1)}, u32[]{:S(2)}, u32[]{:S(2)}) async-start(bf16[32,4,2048]{2,0,1:T(8,128)(2,1)} %bitcast.43), calls=%async_computation | async-start | bytes 1048576 | tf_op jit(solution)/shard_map/all_to_all | solution.py:283
  22.4 22.4 %copy-start.2 = (bf16[1024,128]{1,0:T(8,128)(2,1)S(1)}, bf16[1024,128]{1,0:T(8,128)(2,1)}, u32[]{:S(2)}) copy-start(bf16[1024,128]{1,0:T(8,128)(2,1)} %param.15) | copy-start | bytes 786436
  45.0 4.5 %copy-start.1 = (bf16[32,32,128]{2,1,0:T(8,128)(2,1)}, bf16[32,32,128]{2,1,0:T(8,128)(2,1)S(1)}, u32[]{:S(2)}) copy-start(bf16[32,32,128]{2,1,0:T(8,128)(2,1)S(1)} %copy.49) | copy-start | bytes 786436
  198.2 2.2 %copy-start.4 = (bf16[32,2048]{1,0:T(8,128)(2,1)S(1)}, bf16[32,2048]{1,0:T(8,128)(2,1)}, u32[]{:S(2)}) copy-start(bf16[32,2048]{1,0:T(8,128)(2,1)} %get-tuple-element.27) | copy-start | bytes 393220
  198.2 2.9 %copy-start.3 = (bf16[32,2048]{1,0:T(8,128)(2,1)S(1)}, bf16[32,2048]{1,0:T(8,128)(2,1)}, u32[]{:S(2)}) copy-start(bf16[32,2048]{1,0:T(8,128)(2,1)} %get-tuple-element.28) | copy-start | bytes 393220
where the time goes:
time: 203 us; the launch traced here: 202 us
  Pallas kernels  120 us (59%)
  local copies, waits for them, and re-layouts  41.8 us (21%)
  blocking collectives  28.3 us (14%)
  other arithmetic  5.56 us (3%)
  starting transfers between devices  4.59 us (2%)
    pallas_call x1, Pallas kernels, shards(): pl.pallas_call(functools.partial(pair_kernel, group, cols, seqs, levels),...  63.5 us
    pallas_call x1, Pallas kernels, shards(): pl.pallas_call(functools.partial(sum_kernel, n_row, n_col, ratio), in_spe...  56.1 us
    all_gather x1, blocking collectives, shards(): left_panel = lax.all_gather(first_factor, 'col', axis=0, tiled=True)  19.8 us
    all_gather x1, blocking collectives, shards(): right_rows = lax.all_gather(second_factor, 'row', axis=1, tiled=True)  8.5 us
    all_to_all x1, starting transfers between devices, shards(): lax.all_to_all(right_rows, 'col', split_axis=1, concat_axis=0, tiled=True)  4.59 us
    reshape x1, local copies, waits for them, and re-layouts, shards(): left_levels = left_panel.reshape(levels, DEPTH_STEP, steps, group, size)....  4.23 us
  transfers between devices with their start and end apart: 1, of which 0 were waited for; matrix products, arithmetic and copies ran while one was open for 7% of the time, Pallas kernels for 0%

commit v1 on v0

v1 whole, which is shorter than its diff:
```python
import functools

import jax
import jax.numpy as jnp
from jax import lax
from jax.experimental import pallas as pl
from jax.experimental.pallas import tpu as pltpu
from jax.sharding import PartitionSpec as P

PROJECTED_SIZE = 32
CZ = 128
WINDOW_AMINOS = 256
CHAINS = 8
LANES = 128
MESH = pl.DeviceIdType.MESH


def standardize_entries(alignment_tensor, standard_multiplier, additive_offset):
    incoming_entries = alignment_tensor.astype(jnp.float32)
    center = incoming_entries - jnp.mean(incoming_entries, axis=-1, keepdims=True)
    spread = jnp.mean(center * center, axis=-1, keepdims=True)
    return (center * lax.rsqrt(spread + 1e-05) * standard_multiplier + additive_offset).astype(
        jnp.bfloat16
    )


def to(source, target, send, recv, row, col):
    return pltpu.make_async_remote_copy(
        src_ref=source,
        dst_ref=target,
        send_sem=send,
        recv_sem=recv,
        device_id={"row": row, "col": col},
        device_id_type=MESH,
    )


def arrived(ref, sem):
    pltpu.make_async_copy(ref, ref, sem).wait()


def greet(n_row, n_col, me):
    peers = n_row * n_col
    barrier = pltpu.get_barrier_semaphore()

    def signal(off, carry):
        peer = (me + off) % peers
        pl.semaphore_signal(
            barrier,
            inc=1,
            device_id={"row": peer // n_col, "col": peer % n_col},
            device_id_type=MESH,
        )
        return carry

    lax.fori_loop(1, peers, signal, 0)
    pl.semaphore_wait(barrier, peers - 1)


def gather_kernel(
    n_row, n_col, ratio,
    left_ref, right_ref,
    left_out, right_out,
    left_send, left_recv, right_send, right_recv, hop_send, twin_send, own_sem,
):
    row, col = lax.axis_index("row"), lax.axis_index("col")
    share = left_ref.shape[0]
    greet(n_row, n_col, row * n_col + col)
    block = lambda ref, index: ref.at[pl.ds(pl.multiple_of(index * share, share), share)]
    owner = col // ratio
    twin = row + 1 - 2 * (row % 2)
    chips = n_row // 2

    def right_copy(t):
        return to(
            right_ref.at[t], block(right_out, col), right_send.at[t], right_recv.at[col],
            row, row * ratio + t,
        )

    def left_copy(off):
        peer = (col + off) % n_col
        return to(left_ref, block(left_out, col), left_send.at[off], left_recv.at[col], row, peer)

    def hop_copy(source, index, hop):
        return to(
            source, block(right_out, index), hop_send.at[index, hop], right_recv.at[index],
            (row + 2 * hop) % n_row, col,
        )

    def twin_copy(source, index):
        return to(
            source, block(right_out, index), twin_send.at[index], right_recv.at[index], twin, col
        )

    own_left = pltpu.make_async_copy(left_ref, block(left_out, col), own_sem.at[0])
    own_left.start()
    for t in range(ratio):
        pl.when(row * ratio + t != col)(right_copy(t).start)
    mine = right_ref.at[col % ratio]
    own_right = pltpu.make_async_copy(mine, block(right_out, col), own_sem.at[1])

    @pl.when(row == owner)
    def _():
        own_right.start()
        for hop in range(1, chips):
            hop_copy(mine, col, hop).start()
        twin_copy(mine, col).start()

    for off in range(1, n_col):
        left_copy(off).start()

    @pl.when(row == owner)
    def _():
        own_right.wait()
        for off in range(1, n_col):
            peer = (col + off) % n_col
            source = block(right_out, peer)
            arrived(source, right_recv.at[peer])
            for hop in range(1, chips):
                hop_copy(source, peer, hop).start()
            twin_copy(source, peer).start()

    relays = jnp.logical_and(row != owner, row % 2 == owner % 2)

    @pl.when(relays)
    def _():
        for off in range(n_col):
            peer = (col + off) % n_col
            source = block(right_out, peer)
            arrived(source, right_recv.at[peer])
            twin_copy(source, peer).start()

    @pl.when(row % 2 != owner % 2)
    def _():
        for off in range(n_col):
            peer = (col + off) % n_col
            arrived(block(right_out, peer), right_recv.at[peer])

    own_left.wait()
    for off in range(1, n_col):
        peer = (col + off) % n_col
        arrived(block(left_out, peer), left_recv.at[peer])
    for off in range(1, n_col):
        left_copy(off).wait_send()
    for t in range(ratio):
        pl.when(row * ratio + t != col)(right_copy(t).wait_send)

    @pl.when(row == owner)
    def _():
        for off in range(n_col):
            peer = (col + off) % n_col
            for hop in range(1, chips):
                hop_copy(block(right_out, peer), peer, hop).wait_send()

    @pl.when(row % 2 == owner % 2)
    def _():
        for off in range(n_col):
            peer = (col + off) % n_col
            twin_copy(block(right_out, peer), peer).wait_send()


def pair_kernel(
    tile, cols, seqs,
    labels_ref,
    left_ref, right_ref, table_ref, chain_ref, inverse_ref, grad_ref, weight_ref, weight_t_ref,
    bias_ref,
    pair_ref, left_grad_ref, right_grad_ref, weight_grad_ref,
    kept, kept_t, spread, scaled, outer, acc, left_acc, right_acc, weight_acc, slots,
):
    step = pl.program_id(0)
    size = PROJECTED_SIZE
    inner = LANES // cols
    blocks = size // inner
    width = 2 * LANES if blocks % 2 == 0 else LANES
    f32, bf16 = jnp.float32, jnp.bfloat16
    seq = lax.broadcasted_iota(jnp.int32, (seqs, LANES), 0).astype(f32)

    @pl.when(step == 0)
    def _():
        spread[...] = jnp.zeros_like(spread)
        right_acc[...] = jnp.zeros_like(right_acc)
        weight_acc[...] = jnp.zeros_like(weight_acc)

        def fill(chain, carry):
            keep = jnp.where(seq < table_ref[pl.ds(chain, 1), :], 1.0, 0.0).astype(bf16)
            for b in range(blocks):
                lanes = slice(b * LANES, (b + 1) * LANES)
                piece = right_ref[:, lanes] * keep
                kept[chain, :, lanes] = piece
                kept_t[chain, lanes, :] = piece.T
            return carry

        lax.fori_loop(labels_ref[0], labels_ref[labels_ref.shape[0] - 1] + 2, fill, 0)

    for i in range(tile):
        grad = grad_ref[i * cols : (i + 1) * cols, :]
        for e in range(inner):
            spread[i * LANES + e * cols : i * LANES + (e + 1) * cols, e * CZ : (e + 1) * CZ] = grad
    inverse = [inverse_ref[i : i + 1, :] for i in range(tile)]
    for i in range(0, tile, 2):
        back = lax.dot_general(
            weight_ref[...], spread[i * LANES : (i + 2) * LANES, :], (((1,), (1,)), ((), ())),
            preferred_element_type=f32,
        )
        for k in range(2):
            part = (back[:, k * LANES : (k + 1) * LANES] * inverse[i + k]).astype(bf16)
            for b in range(blocks):
                scaled[(i + k) * size : (i + k + 1) * size, b * LANES : (b + 1) * LANES] = part[
                    b * size : (b + 1) * size
                ]

    low = labels_ref[step * tile]
    high = labels_ref[step * tile + tile - 1]

    def chain_pair(first, chain):
        left = left_ref[...]
        lane = chain_ref[0]
        for k in range(2):
            slots[k * seqs : (k + 1) * seqs, :] = left * jnp.where(
                lane == (chain + k).astype(f32), 1.0, 0.0
            ).astype(bf16)
        both = slots[...]
        both_t = both.T
        keep = [seq < table_ref[pl.ds(chain + k, 1), :] for k in range(2)]
        for start in range(0, blocks * LANES, width):
            lanes = slice(start, start + width)
            right = kept[pl.ds(chain, 2), :, lanes].reshape(2 * seqs, width)
            prod = jnp.dot(both_t, right, preferred_element_type=f32)
            if first:
                acc[:, lanes] = prod
            else:
                acc[:, lanes] += prod
            out = jnp.dot(both, scaled[:, lanes], preferred_element_type=f32)
            for b in range(width // LANES):
                part = slice(b * LANES, (b + 1) * LANES)
                right_acc[:, start + b * LANES : start + (b + 1) * LANES] += jnp.where(
                    keep[0], out[:seqs, part], 0.0
                ) + jnp.where(keep[1], out[seqs:, part], 0.0)
        right_t = jnp.concatenate([kept_t[chain], kept_t[chain + 1]], axis=1)
        out = jnp.dot(scaled[...], right_t, preferred_element_type=f32)
        for i in range(tile):
            label = labels_ref[step * tile + i]
            rows = slice(i * size, (i + 1) * size)
            part = jnp.where(label == chain, out[rows, :seqs], 0.0) + jnp.where(
                label == chain + 1, out[rows, seqs:], 0.0
            )
            if first:
                left_acc[rows, :] = part
            else:
                left_acc[rows, :] += part

    chain_pair(True, low)

    def more(p, carry):
        chain_pair(False, low + 2 * p)
        return carry

    lax.fori_loop(1, (high - low) // 2 + 1, more, 0)
    left_grad_ref[...] = left_acc[...].T.astype(bf16)
    for i in range(tile):
        for b in range(blocks):
            outer[b * size : (b + 1) * size, i * LANES : (i + 1) * LANES] = (
                acc[i * size : (i + 1) * size, b * LANES : (b + 1) * LANES] * inverse[i]
            ).astype(bf16)
    lane = lax.broadcasted_iota(jnp.int32, (CZ, LANES), 1) // cols
    for i in range(0, tile, 2):
        both = jnp.dot(
            weight_t_ref[...], outer[:, i * LANES : (i + 2) * LANES], preferred_element_type=f32
        )
        for k in range(2):
            lanes = slice(k * LANES, (k + 1) * LANES)
            total = both[:CZ, lanes]
            for e in range(1, inner):
                total = jnp.where(lane == e, both[e * CZ : (e + 1) * CZ, lanes], total)
            turned = total.T
            pair = turned[:cols]
            for e in range(1, inner):
                pair = pair + turned[e * cols : (e + 1) * cols]
            pair_ref[(i + k) * cols : (i + k + 1) * cols, :] = (pair + bias_ref[...]).astype(bf16)
    weight_acc[...] += jnp.dot(outer[...], spread[...], preferred_element_type=f32)

    @pl.when(step == pl.num_programs(0) - 1)
    def _():
        right_grad_ref[...] = right_acc[...].astype(bf16)
        rows = blocks * size
        for e in range(inner):
            weight_grad_ref[e * rows : (e + 1) * rows, :] = weight_acc[
                :, e * CZ : (e + 1) * CZ
            ].astype(bf16)


def sum_kernel(
    n_row, n_col, ratio,
    left_ref, right_ref, weight_ref,
    left_out, right_out, weight_out,
    left_in, right_mid, right_sum, right_in, weight_mid, weight_sum, weight_in, weight_part,
    weight_all,
    left_send, left_recv, mid_send, mid_recv, right_send, right_recv,
    w1_send, w1_recv, w2_send, w2_recv, w3_send, w3_recv, w4_send, w4_recv,
):
    f32, bf16 = jnp.float32, jnp.bfloat16
    row, col = lax.axis_index("row"), lax.axis_index("col")
    greet(n_row, n_col, row * n_col + col)
    many = n_col // n_row
    quarter = weight_ref.shape[0] // n_row
    piece = quarter // n_col
    owner, slot = col // ratio, col % ratio
    rows_of = lambda index, extent: pl.ds(pl.multiple_of(index * extent, extent), extent)

    def w1_copy(off):
        peer = (row + off) % n_row
        return to(
            weight_ref.at[rows_of(peer, quarter)], weight_mid.at[row], w1_send.at[off],
            w1_recv.at[row], peer, col,
        )

    def mid_copy(off):
        peer = (row + off) % n_row
        return to(
            right_ref.at[rows_of(peer, many)], right_mid.at[row], mid_send.at[off],
            mid_recv.at[row], peer, col,
        )

    def left_copy(off):
        peer = (col + off) % n_col
        return to(
            left_ref.at[peer], left_in.at[col], left_send.at[off], left_recv.at[col], row, peer
        )

    def right_copy(b):
        return to(
            right_sum.at[b], right_in.at[slot, row], right_send.at[b],
            right_recv.at[slot, row], owner, row * many + b,
        )

    def w2_copy(off):
        peer = (col + off) % n_col
        return to(
            weight_sum.at[rows_of(peer, piece)], weight_in.at[col], w2_send.at[off],
            w2_recv.at[col], row, peer,
        )

    def w3_copy(off):
        peer = (col + off) % n_col
        return to(
            weight_part, weight_all.at[rows_of(row * n_col + col, piece)], w3_send.at[off],
            w3_recv.at[col], row, peer,
        )

    def w4_copy(off):
        peer = (row + off) % n_row
        mine = weight_all.at[rows_of(row, quarter)]
        return to(mine, mine, w4_send.at[off], w4_recv.at[row], peer, col)

    for off in range(1, n_row):
        w1_copy(off).start()
    for off in range(1, n_row):
        mid_copy(off).start()
    late = n_col - 1
    for off in range(1, late):
        left_copy(off).start()

    own = weight_ref[rows_of(row, quarter), :].astype(f32)
    for off in range(1, n_row):
        peer = (row + off) % n_row
        arrived(weight_mid.at[peer], w1_recv.at[peer])
        own = own + weight_mid[peer].astype(f32)
    weight_sum[...] = own.astype(bf16)
    for off in range(1, n_col):
        w2_copy(off).start()
    left_copy(late).start()

    total = right_ref[rows_of(row, many)].astype(f32)
    for off in range(1, n_row):
        peer = (row + off) % n_row
        arrived(right_mid.at[peer], mid_recv.at[peer])
        total = total + right_mid[peer].astype(f32)
    right_sum[...] = total.astype(bf16)
    for b in range(many):
        here = jnp.logical_and(owner == row, row * many + b == col)
        pl.when(jnp.logical_not(here))(right_copy(b).start)
        pl.when(here)(
            pltpu.make_async_copy(
                right_sum.at[b], right_in.at[slot, row], right_recv.at[slot, row]
            ).start
        )

    own = weight_sum[rows_of(col, piece), :].astype(f32)
    for off in range(1, n_col):
        peer = (col + off) % n_col
        arrived(weight_in.at[peer], w2_recv.at[peer])
        own = own + weight_in[peer].astype(f32)
    weight_part[...] = own.astype(bf16)
    weight_all[rows_of(row * n_col + col, piece), :] = own.astype(bf16)
    for off in range(1, n_col):
        w3_copy(off).start()
    for off in range(1, n_col):
        peer = (col + off) % n_col
        arrived(weight_all.at[rows_of(row * n_col + peer, piece)], w3_recv.at[peer])
    for off in range(1, n_row):
        w4_copy(off).start()

    total = left_ref[col].astype(f32)
    for off in range(1, n_col):
        peer = (col + off) % n_col
        arrived(left_in.at[peer], left_recv.at[peer])
        total = total + left_in[peer].astype(f32)
    left_out[...] = total.astype(bf16)
    for t in range(ratio):
        source = col // many
        arrived(right_in.at[t, source], right_recv.at[t, source])
        right_out[t] = right_in[t, source]
    for off in range(1, n_row):
        peer = (row + off) % n_row
        arrived(weight_all.at[rows_of(peer, quarter)], w4_recv.at[peer])
    weight_out[...] = weight_all[...].astype(f32) * (1.0 / WINDOW_AMINOS)

    for off in range(1, n_row):
        w1_copy(off).wait_send()
        mid_copy(off).wait_send()
        w4_copy(off).wait_send()
    for off in range(1, n_col):
        left_copy(off).wait_send()
        w2_copy(off).wait_send()
        w3_copy(off).wait_send()
    for b in range(many):
        here = jnp.logical_and(owner == row, row * many + b == col)
        pl.when(jnp.logical_not(here))(right_copy(b).wait_send)


def shards(
    alignment_tensor,
    standardizer_scaling,
    standardizer_offset,
    first_projector,
    second_projector,
    final_projector,
    final_offset,
    amino_strand_label,
    matched_strand_count,
    couple_delta_adjoint,
):
    f32, bf16 = jnp.float32, jnp.bfloat16
    share, rows, feats = alignment_tensor.shape
    cols = couple_delta_adjoint.shape[1]
    size = PROJECTED_SIZE
    n_row, n_col = lax.axis_size("row"), lax.axis_size("col")
    ratio = rows // cols
    seqs = share * n_col
    inner = LANES // cols
    blocks = size // inner
    wide = size * cols
    vmem = pl.BlockSpec(memory_space=pltpu.VMEM)
    dma = pltpu.SemaphoreType.DMA

    entries = standardize_entries(
        alignment_tensor, standardizer_scaling, standardizer_offset
    ).reshape(-1, feats)
    both = jnp.dot(
        entries,
        jnp.concatenate([first_projector, second_projector], axis=1),
        preferred_element_type=f32,
    ).astype(bf16)
    left_own = both[:, :size].reshape(share, rows * size)
    right_own = (
        both[:, size:]
        .reshape(share, ratio, cols, size)
        .transpose(1, 0, 3, 2)
        .reshape(ratio, share, wide)
    )
    left_panel, right_panel = pl.pallas_call(
        functools.partial(gather_kernel, n_row, n_col, ratio),
        in_specs=[vmem] * 2,
        out_specs=[vmem] * 2,
        out_shape=[
            jax.ShapeDtypeStruct((seqs, rows * size), bf16),
            jax.ShapeDtypeStruct((seqs, wide), bf16),
        ],
        scratch_shapes=[
            dma((n_col,)), dma((n_col,)), dma((ratio,)), dma((n_col,)),
            dma((n_col, n_row // 2)), dma((n_col,)), dma((2,)),
        ],
        compiler_params=pltpu.CompilerParams(collective_id=0, has_side_effects=True),
    )(left_own, right_own)

    row_labels = lax.dynamic_slice_in_dim(
        amino_strand_label, lax.axis_index("row") * rows, rows, 0
    )
    col_labels = lax.dynamic_slice_in_dim(
        amino_strand_label, lax.axis_index("col") * cols, cols, 0
    )
    chains = jnp.arange(CHAINS, dtype=jnp.int32)
    row_hot = (row_labels[:, None] == chains[None, :]).astype(f32)
    col_hot = (col_labels[:, None] == chains[None, :]).astype(f32)
    by_chain = jnp.dot(
        matched_strand_count.astype(f32), col_hot.T, precision=lax.Precision.HIGHEST
    )
    depth = jnp.dot(row_hot, by_chain, precision=lax.Precision.HIGHEST)
    table = jnp.pad(jnp.tile(by_chain, (1, inner)), ((0, CHAINS), (0, 0)))
    inverse = jnp.tile(1.0 / depth, (1, inner))
    tile = 8
    steps = rows // tile
    chain_lanes = jnp.repeat(row_labels.astype(f32), size).reshape(steps, 1, tile * size)
    weight = (
        final_projector.reshape(size, blocks, inner, CZ)
        .transpose(1, 0, 2, 3)
        .reshape(blocks * size, inner * CZ)
    )
    flat_grad = couple_delta_adjoint.reshape(-1, CZ)
    whole = lambda shape: pl.BlockSpec(shape, lambda g, labels: (0,) * len(shape))
    pair, left_grad, right_grad, weight_part = pl.pallas_call(
        functools.partial(pair_kernel, tile, cols, seqs),
        grid_spec=pltpu.PrefetchScalarGridSpec(
            num_scalar_prefetch=1,
            grid=(steps,),
            in_specs=[
                pl.BlockSpec((seqs, tile * size), lambda g, labels: (0, g)),
                whole((seqs, wide)),
                whole((2 * CHAINS, LANES)),
                pl.BlockSpec((1, 1, tile * size), lambda g, labels: (g, 0, 0)),
                pl.BlockSpec((tile, LANES), lambda g, labels: (g, 0)),
                pl.BlockSpec((tile * cols, CZ), lambda g, labels: (g, 0)),
                whole((blocks * size, inner * CZ)),
                whole((inner * CZ, blocks * size)),
                whole((1, CZ)),
            ],
            out_specs=[
                pl.BlockSpec((tile * cols, CZ), lambda g, labels: (g, 0)),
                pl.BlockSpec((seqs, tile * size), lambda g, labels: (0, g)),
                whole((seqs, wide)),
                whole((size * size, CZ)),
            ],
            scratch_shapes=[
                pltpu.VMEM((CHAINS + 1, seqs, wide), bf16),
                pltpu.VMEM((CHAINS + 1, wide, seqs), bf16),
                pltpu.VMEM((tile * LANES, inner * CZ), bf16),
                pltpu.VMEM((tile * size, wide), bf16),
                pltpu.VMEM((blocks * size, tile * LANES), bf16),
                pltpu.VMEM((tile * size, wide), f32),
                pltpu.VMEM((tile * size, seqs), f32),
                pltpu.VMEM((seqs, wide), f32),
                pltpu.VMEM((blocks * size, inner * CZ), f32),
                pltpu.VMEM((2 * seqs, tile * size), bf16),
            ],
        ),
        out_shape=[
            jax.ShapeDtypeStruct((rows * cols, CZ), bf16),
            jax.ShapeDtypeStruct((seqs, rows * size), bf16),
            jax.ShapeDtypeStruct((seqs, wide), bf16),
            jax.ShapeDtypeStruct((size * size, CZ), bf16),
        ],
        compiler_params=pltpu.CompilerParams(
            dimension_semantics=("arbitrary",), vmem_limit_bytes=56 * 1024 * 1024
        ),
    )(
        row_labels,
        left_panel,
        right_panel,
        table,
        chain_lanes,
        inverse,
        flat_grad,
        weight,
        weight.T,
        final_offset[None, :],
    )
    pair_update = pair.reshape(rows, cols, CZ)
    many = n_col // n_row
    quarter = size * size // n_row
    piece = quarter // n_col
    adjoint_first_factor, right_sum, weight_total = pl.pallas_call(
        functools.partial(sum_kernel, n_row, n_col, ratio),
        in_specs=[vmem] * 3,
        out_specs=[vmem] * 3,
        out_shape=[
            jax.ShapeDtypeStruct((share, rows * size), bf16),
            jax.ShapeDtypeStruct((ratio, share, wide), bf16),
            jax.ShapeDtypeStruct((size * size, CZ), f32),
        ],
        scratch_shapes=[
            pltpu.VMEM((n_col, share, rows * size), bf16),
            pltpu.VMEM((n_row, many, share, wide), bf16),
            pltpu.VMEM((many, share, wide), bf16),
            pltpu.VMEM((ratio, n_row, share, wide), bf16),
            pltpu.VMEM((n_row, quarter, CZ), bf16),
            pltpu.VMEM((quarter, CZ), bf16),
            pltpu.VMEM((n_col, piece, CZ), bf16),
            pltpu.VMEM((piece, CZ), bf16),
            pltpu.VMEM((size * size, CZ), bf16),
            dma((n_col,)), dma((n_col,)),
            dma((n_row,)), dma((n_row,)),
            dma((many,)), dma((ratio, n_row)),
            dma((n_row,)), dma((n_row,)),
            dma((n_col,)), dma((n_col,)),
            dma((n_col,)), dma((n_col,)),
            dma((n_row,)), dma((n_row,)),
        ],
        compiler_params=pltpu.CompilerParams(collective_id=1, has_side_effects=True),
    )(
        left_grad.reshape(n_col, share, rows * size),
        right_grad.reshape(n_col, share, wide),
        weight_part,
    )
    grad_right = (
        right_sum.reshape(ratio, share, size, cols)
        .transpose(1, 0, 3, 2)
        .reshape(share, rows * size)
    )
    grad_w_out = (
        weight_total.reshape(inner, blocks, size, CZ).transpose(2, 1, 0, 3).reshape(size * size, CZ)
    )
    return (pair_update, adjoint_first_factor, grad_right, grad_w_out)


def solution(mesh):
    in_specs = (
        P(("parts", "col"), "row", None),
        P(),
        P(),
        P(),
        P(),
        P(),
        P(),
        P("parts"),
        P("parts", None),
        P(("parts", "row"), "col", None),
    )
    out_specs = (
        P(("parts", "row"), "col", None),
        P(("parts", "col"), "row"),
        P(("parts", "col"), "row"),
        P("parts", None),
    )
    return jax.shard_map(shards, mesh=mesh, in_specs=in_specs, out_specs=out_specs, check_vma=False)
```

time: 203 us -> 96.6 us (0.48)
  Pallas kernels: 120 us -> 78.9 us
  local copies, waits for them, and re-layouts: 41.8 us -> 10.8 us
  blocking collectives: 28.3 us -> 0 us
  starting transfers between devices: 4.59 us -> 0 us
    all_gather x2 -> x0, blocking collectives: 28.3 us -> none  [the longest x1 19.8 us: shards(): left_panel = lax.all_gather(first_factor, 'col', axis=0, tiled=True)]
    pallas_call x1, Pallas kernels: 56.1 us -> 33.4 us  [shards(): pl.pallas_call(functools.partial(sum_kernel, n_row, n_col, ratio), in_spe...]
    pallas_call x1 -> x2, Pallas kernels: 63.5 us -> 45.4 us  [the longest x1 23.5 us: shards(): pl.pallas_call(functools.partial(gather_kernel, n_row, n_col, ratio), in_...]
    reshape x11 -> x9, local copies, waits for them, and re-layouts: 18.1 us -> 6.26 us  [the longest x2 1.51 us: shards(): right_sum.reshape(ratio, share, size, cols).transpose(1, 0, 3, 2)]
    another operation x2 -> x4, local copies, waits for them, and re-layouts: 5.94 us -> 0.85 us  [the longest x2 0.73 us: shards(): inverse = jnp.tile(1.0 / depth, (1, inner))]
    all_to_all x1 -> x0, starting transfers between devices: 4.59 us -> none  [shards(): lax.all_to_all(right_rows, 'col', split_axis=1, concat_axis=0, tiled=True)]
    transpose x3 -> x1, local copies, waits for them, and re-layouts: 4.42 us -> 1.2 us  [shards(): weight_total.reshape(inner, blocks, size, CZ).transpose(2, 1, 0, 3)]
    convert_element_type x1 -> x0, local copies, waits for them, and re-layouts: 3.22 us -> none  [shards(): right_sum = right_grad.reshape(seqs, size, group, cols).sum(axis=2).astyp...]
  transfers between devices with their start and end apart: 1 -> 0, of which waited for: 0 -> 0; matrix products, arithmetic and copies ran while one was open for 7% -> 0% of each run, Pallas kernels for 0% -> 0%
where the time goes in v1:
time: 96.6 us; the launch traced here: 95.9 us
  Pallas kernels  78.9 us (82%)
  local copies, waits for them, and re-layouts  10.8 us (11%)
  other arithmetic  3.85 us (4%)
  matrix products  1.52 us (2%)
    pallas_call x1, Pallas kernels, shards(): pl.pallas_call(functools.partial(sum_kernel, n_row, n_col, ratio), in_spe...  33.4 us
    pallas_call x1, Pallas kernels, shards(): pl.pallas_call(functools.partial(gather_kernel, n_row, n_col, ratio), in_...  23.5 us
    pallas_call x1, Pallas kernels, shards(): pl.pallas_call(functools.partial(pair_kernel, tile, cols, seqs), grid_spe...  22 us

profile of v1, /device:TPU:1, one launch (start us, length us, event | category | flops | bytes accessed | tf_op | source)
XLA Modules:
  0.0 95.9 jit_solution(9995003461409804127)
XLA Ops:
  0.6 0.0 copy-start
  0.6 0.9 fusion.14
  1.5 0.0 copy-start.7
  1.5 0.1 broadcast_in_dim.8
  1.6 0.9 fusion.9
  2.5 0.1 tile.9
  2.6 0.6 pad.4.table_ref
  3.2 0.0 copy-start.3
  3.2 1.6 %convert_reduce_fusion = f32[32,64]{1,0:T(8,128)S(1)} fusion(bf16[32,64,256]{2,1,0:T(8,128)(2,1)} %param.10), kind=kLoop, calls=%fused_computation.1 | loop fusion | flops 1046528 | bytes 1056768 | tf_op jit(solution)/shard_map/reduce_sum | solution.py:20
  4.8 0.0 copy-done
  4.8 0.6 fusion.2
  5.5 0.0 copy-start.8
  5.5 0.0 copy-start.9
  5.5 0.1 broadcast_in_dim.9
  5.6 0.7 broadcast_in_dim.20.chain_ref
  6.3 0.0 copy-done.7
  6.3 0.2 convolution_divide_fusion
  6.5 0.7 tile.21.inverse_ref
  7.2 0.0 copy-done.3
  7.2 0.2 copy.22
  7.5 0.0 copy-start.1
  7.5 0.8 copy.23
  8.4 0.0 copy-done.8
  8.4 0.0 copy-done.9
  8.4 0.0 copy-start.5
  8.4 0.0 copy-start.6
  8.4 0.7 fusion.5
  9.1 0.0 copy-done.1
  9.1 0.0 copy-done.5
  9.1 0.0 copy-done.6
  9.2 0.4 convolution_convert_fusion
  9.6 0.2 reshape.83
  9.9 0.1 copy.30
  10.0 0.9 reshape.84.right_ref
  10.9 0.3 copy.20
  11.2 1.2 %reshape.82.left_ref = bf16[32,2048]{1,0:T(8,128)(2,1)} reshape(bf16[2048,32]{1,0:T(8,128)(2,1)S(1)} %copy.20) | data formatting | bytes 262144 | tf_op jit(solution)/shard_map/reshape | solution.py:464
  12.4 23.5 %shard_map.129 = (bf16[128,2048]{1,0:T(8,128)(2,1)}, bf16[128,2048]{1,0:T(8,128)(2,1)}) custom-call(bf16[32,2048]{1,0:T(8,128)(2,1)} %reshape.82.left_ref, bf16[1,32,2048]{2,1,0:T(8,128)(2,1)} %reshape.84.right_ref), custom_call_target="tpu_custom_call" | custom-call | tf_op jit(solution)/shard_map/pallas_call | solution.py:471
  35.9 22.0 %shard_map.130 = (bf16[4096,128]{1,0:T(8,128)(2,1)}, bf16[128,2048]{1,0:T(8,128)(2,1)}, bf16[128,2048]{1,0:T(8,128)(2,1)}, bf16[1024,128]{1,0:T(8,128)(2,1)}) custom-call(s32[64]{0:T(128)} %copy-done.7, bf16[128,2048]{1,0:T(8,128)(2,1)} %get-tuple-element.13.left_ref, bf16[128,2048]{1,0:T(8,128)(2,1)} %get-tuple-element.14.right_ref, ...), custom_call_target="tpu_custom_call" | custom-call | tf_op jit(solution)/shard_map/pallas_call | solution.py:511
  57.8 33.4 %shard_map.131 = (bf16[32,2048]{1,0:T(8,128)(2,1)}, bf16[1,32,2048]{2,1,0:T(8,128)(2,1)}, f32[1024,128]{1,0:T(8,128)}) custom-call(bf16[4,32,2048]{2,1,0:T(8,128)(2,1)} %bitcast.41, bf16[4,32,2048]{2,1,0:T(8,128)(2,1)} %bitcast.42, bf16[1024,128]{1,0:T(8,128)(2,1)} %get-tuple-element.18.weight_ref), custom_call_target="tpu_custom_call" | custom-call | tf_op jit(solution)/shard_map/pallas_call | solution.py:571
  91.3 0.0 copy-start.2
  91.3 1.2 %reshape.91 = bf16[1,32,32,64]{3,2,1,0:T(8,128)(2,1)S(1)} reshape(bf16[1,32,2048]{2,1,0:T(8,128)(2,1)} %get-tuple-element.20) | data formatting | bytes 262144 | tf_op jit(solution)/shard_map/reshape | solution.py:605
  92.5 0.3 copy.24
  92.8 0.0 copy-start.4
  92.8 1.2 %reshape.92 = bf16[32,2048]{1,0:T(8,128)(2,1)} reshape(bf16[32,1,64,32]{3,2,0,1:T(8,128)(2,1)S(1)} %bitcast.36) | data formatting | bytes 262144 | tf_op jit(solution)/shard_map/reshape | solution.py:607
  94.0 0.0 copy-done.2
  94.0 1.2 %copy.25 = f32[32,16,2,128]{3,2,1,0:T(2,128)} copy(f32[32,16,2,128]{3,0,1,2:T(8,128)S(1)} %bitcast.44) | data formatting | bytes 1048576 | tf_op jit(solution)/shard_map/transpose | solution.py:610
  95.2 0.0 copy-done.4
  95.2 0.7 copy.32
  (6 shorter events, 0.1 us)
Async XLA Ops:
  0.6 4.2 %copy-start = (bf16[32,64,256]{2,1,0:T(8,128)(2,1)S(1)}, bf16[32,64,256]{2,1,0:T(8,128)(2,1)}, u32[]{:S(2)}) copy-start(bf16[32,64,256]{2,1,0:T(8,128)(2,1)} %param.10) | copy-start | bytes 3145732
  1.5 4.8 %copy-start.7 = (s32[64]{0:T(128)}, s32[64]{0:T(128)S(1)}, u32[]{:S(2)}) copy-start(s32[64]{0:T(128)S(1)} %get-tuple-element.23.labels_ref) | copy-start | bytes 772
  3.2 4.0 %copy-start.3 = (bf16[1024,128]{1,0:T(8,128)(2,1)S(1)}, bf16[1024,128]{1,0:T(8,128)(2,1)}, u32[]{:S(2)}) copy-start(bf16[1024,128]{1,0:T(8,128)(2,1)} %param.15) | copy-start | bytes 786436
  5.5 2.9 %copy-start.8 = (f32[256]{0:T(256)S(1)}, f32[256]{0:T(256)}, u32[]{:S(2)}) copy-start(f32[256]{0:T(256)} %param.12) | copy-start | bytes 3076
  5.5 2.9 %copy-start.9 = (f32[256]{0:T(256)S(1)}, f32[256]{0:T(256)}, u32[]{:S(2)}) copy-start(f32[256]{0:T(256)} %param.11) | copy-start | bytes 3076
  7.5 1.6 %copy-start.1 = (bf16[64,8,2,128]{3,1,2,0:T(8,128)(2,1)}, bf16[64,8,2,128]{3,1,2,0:T(8,128)(2,1)S(1)}, u32[]{:S(2)}) copy-start(bf16[64,8,2,128]{3,1,2,0:T(8,128)(2,1)S(1)} %copy.29) | copy-start | bytes 786436
  8.4 0.8 copy-start.5
  8.4 0.8 copy-start.6
  91.3 2.7 %copy-start.2 = (f32[1024,128]{1,0:T(8,128)S(1)}, f32[1024,128]{1,0:T(8,128)}, u32[]{:S(2)}) copy-start(f32[1024,128]{1,0:T(8,128)} %get-tuple-element.21) | copy-start | bytes 1572868
  92.8 2.4 %copy-start.4 = (bf16[32,2048]{1,0:T(8,128)(2,1)S(1)}, bf16[32,2048]{1,0:T(8,128)(2,1)}, u32[]{:S(2)}) copy-start(bf16[32,2048]{1,0:T(8,128)(2,1)} %get-tuple-element.32) | copy-start | bytes 393220

commit v2 on v1

--- a/solution.py
+++ b/solution.py
@@ -61,15 +61,20 @@
     n_row, n_col, ratio,
     left_ref, right_ref,
     left_out, right_out,
-    left_send, left_recv, right_send, right_recv, hop_send, twin_send, own_sem,
+    up_send, down_send, left_recv, right_send, right_recv, hop_send, twin_send, own_sem,
 ):
     row, col = lax.axis_index("row"), lax.axis_index("col")
     share = left_ref.shape[0]
+    parts = left_recv.shape[1]
+    part = left_ref.shape[1] // parts
     greet(n_row, n_col, row * n_col + col)
-    block = lambda ref, index: ref.at[pl.ds(pl.multiple_of(index * share, share), share)]
+    rows_of = lambda index: pl.ds(pl.multiple_of(index * share, share), share)
+    block = lambda ref, index: ref.at[rows_of(index)]
     owner = col // ratio
     twin = row + 1 - 2 * (row % 2)
     chips = n_row // 2
+    is_owner = row == owner
+    same_side = row % 2 == owner % 2
 
     def right_copy(t):
         return to(
@@ -77,9 +82,16 @@
             row, row * ratio + t,
         )
 
-    def left_copy(off):
-        peer = (col + off) % n_col
-        return to(left_ref, block(left_out, col), left_send.at[off], left_recv.at[col], row, peer)
+    def left_part(index, h):
+        return left_out.at[rows_of(index), h * part : (h + 1) * part]
+
+    def left_copy(index, h, step, own=False):
+        sends = up_send if step > 0 else down_send
+        source = left_ref.at[:, h * part : (h + 1) * part] if own else left_part(index, h)
+        return to(
+            source, left_part(index, h), sends.at[index, h], left_recv.at[index, h],
+            row, (col + step) % n_col,
+        )
 
     def hop_copy(source, index, hop):
         return to(
@@ -92,71 +104,80 @@
             source, block(right_out, index), twin_send.at[index], right_recv.at[index], twin, col
         )
 
+    has_up, has_down = col + 1 < n_col, col > 0
+    for t in range(ratio):
+        pl.when(row * ratio + t != col)(right_copy(t).start)
+    for h in range(parts):
+        pl.when(has_up)(left_copy(col, h, 1, True).start)
+        pl.when(has_down)(left_copy(col, h, -1, True).start)
     own_left = pltpu.make_async_copy(left_ref, block(left_out, col), own_sem.at[0])
     own_left.start()
-    for t in range(ratio):
-        pl.when(row * ratio + t != col)(right_copy(t).start)
     mine = right_ref.at[col % ratio]
     own_right = pltpu.make_async_copy(mine, block(right_out, col), own_sem.at[1])
 
-    @pl.when(row == owner)
+    @pl.when(is_owner)
     def _():
         own_right.start()
         for hop in range(1, chips):
             hop_copy(mine, col, hop).start()
         twin_copy(mine, col).start()
 
-    for off in range(1, n_col):
-        left_copy(off).start()
-
-    @pl.when(row == owner)
-    def _():
-        own_right.wait()
-        for off in range(1, n_col):
-            peer = (col + off) % n_col
-            source = block(right_out, peer)
-            arrived(source, right_recv.at[peer])
-            for hop in range(1, chips):
-                hop_copy(source, peer, hop).start()
-            twin_copy(source, peer).start()
-
-    relays = jnp.logical_and(row != owner, row % 2 == owner % 2)
-
-    @pl.when(relays)
-    def _():
-        for off in range(n_col):
-            peer = (col + off) % n_col
-            source = block(right_out, peer)
-            arrived(source, right_recv.at[peer])
-            twin_copy(source, peer).start()
-
-    @pl.when(row % 2 != owner % 2)
-    def _():
-        for off in range(n_col):
-            peer = (col + off) % n_col
-            arrived(block(right_out, peer), right_recv.at[peer])
+    def pass_left(k):
+        for h in range(parts):
+            for step, there in ((1, col - k), (-1, col + k)):
+                here = there >= 0 if step > 0 else there < n_col
+                index = there % n_col
+
+                @pl.when(here)
+                def _(index=index, h=h):
+                    arrived(left_part(index, h), left_recv.at[index, h])
+
+                on = jnp.logical_and(here, has_up if step > 0 else has_down)
+                pl.when(on)(left_copy(index, h, step).start)
+
+    def pass_right(k):
+        for there in (col - k, col + k) if k else (col,):
+            index = there % n_col
+            source = block(right_out, index)
+            here = jnp.logical_and(there >= 0, there < n_col)
+
+            @pl.when(jnp.logical_and(here, jnp.logical_not(jnp.logical_and(is_owner, k == 0))))
+            def _(index=index, source=source):
+                arrived(source, right_recv.at[index])
+
+            if k:
+
+                @pl.when(jnp.logical_and(here, is_owner))
+                def _(index=index, source=source):
+                    for hop in range(1, chips):
+                        hop_copy(source, index, hop).start()
+
+            relay = same_side if k else jnp.logical_and(same_side, jnp.logical_not(is_owner))
+            pl.when(jnp.logical_and(here, relay))(twin_copy(source, index).start)
+
+    for k in range(1, n_col - 1):
+        pass_left(k)
+        if k == 1:
+            pass_right(0)
+        pass_right(k)
+    pass_right(n_col - 1)
+    pass_left(n_col - 1)
 
     own_left.wait()
-    for off in range(1, n_col):
-        peer = (col + off) % n_col
-        arrived(block(left_out, peer), left_recv.at[peer])
-    for off in range(1, n_col):
-        left_copy(off).wait_send()
+    pl.when(is_owner)(own_right.wait)
     for t in range(ratio):
         pl.when(row * ratio + t != col)(right_copy(t).wait_send)
-
-    @pl.when(row == owner)
-    def _():
-        for off in range(n_col):
-            peer = (col + off) % n_col
+    for index in range(n_col):
+        for h in range(parts):
+            pl.when(jnp.logical_and(has_up, index <= col))(left_copy(index, h, 1).wait_send)
+            pl.when(jnp.logical_and(has_down, index >= col))(left_copy(index, h, -1).wait_send)
+
+        @pl.when(is_owner)
+        def _(index=index):
             for hop in range(1, chips):
-                hop_copy(block(right_out, peer), peer, hop).wait_send()
-
-    @pl.when(row % 2 == owner % 2)
-    def _():
-        for off in range(n_col):
-            peer = (col + off) % n_col
-            twin_copy(block(right_out, peer), peer).wait_send()
+                hop_copy(block(right_out, index), index, hop).wait_send()
+
+        pl.when(same_side)(twin_copy(block(right_out, index), index).wait_send)
 
 
 def pair_kernel(
@@ -293,19 +314,28 @@
     n_row, n_col, ratio,
     left_ref, right_ref, weight_ref,
     left_out, right_out, weight_out,
-    left_in, right_mid, right_sum, right_in, weight_mid, weight_sum, weight_in, weight_part,
-    weight_all,
-    left_send, left_recv, mid_send, mid_recv, right_send, right_recv,
+    up_in, down_in, right_twin, right_half, right_mid, right_sum, right_in,
+    weight_mid, weight_sum, weight_in, weight_part, weight_all,
+    up_send, up_recv, down_send, down_recv, twin_send, twin_recv, mid_send, mid_recv,
+    right_send, right_recv,
     w1_send, w1_recv, w2_send, w2_recv, w3_send, w3_recv, w4_send, w4_recv,
 ):
     f32, bf16 = jnp.float32, jnp.bfloat16
     row, col = lax.axis_index("row"), lax.axis_index("col")
     greet(n_row, n_col, row * n_col + col)
+    chips = n_row // 2
+    chip, side = row // 2, row % 2
+    twin = row + 1 - 2 * side
     many = n_col // n_row
+    half = n_col // 2
     quarter = weight_ref.shape[0] // n_row
     piece = quarter // n_col
+    parts = up_recv.shape[1]
+    part = left_ref.shape[2] // parts
     owner, slot = col // ratio, col % ratio
     rows_of = lambda index, extent: pl.ds(pl.multiple_of(index * extent, extent), extent)
+    mine = side * chips + chip
+    has_up, has_down = col + 1 < n_col, col > 0
 
     def w1_copy(off):
         peer = (row + off) % n_row
@@ -314,23 +344,32 @@
             w1_recv.at[row], peer, col,
         )
 
+    twin_copy = to(
+        right_ref.at[rows_of(1 - side, half)], right_twin, twin_send, twin_recv, twin, col
+    )
+
     def mid_copy(off):
-        peer = (row + off) % n_row
-        return to(
-            right_ref.at[rows_of(peer, many)], right_mid.at[row], mid_send.at[off],
-            mid_recv.at[row], peer, col,
-        )
-
-    def left_copy(off):
-        peer = (col + off) % n_col
-        return to(
-            left_ref.at[peer], left_in.at[col], left_send.at[off], left_recv.at[col], row, peer
+        peer = (chip + off) % chips
+        return to(
+            right_half.at[rows_of(peer, many)], right_mid.at[chip], mid_send.at[off],
+            mid_recv.at[chip], 2 * peer + side, col,
         )
 
     def right_copy(b):
         return to(
-            right_sum.at[b], right_in.at[slot, row], right_send.at[b],
-            right_recv.at[slot, row], owner, row * many + b,
+            right_sum.at[b], right_in.at[slot], right_send.at[b], right_recv.at[slot],
+            owner, mine * many + b,
+        )
+
+    def left_copy(index, h, step, own=False):
+        lanes = slice(h * part, (h + 1) * part)
+        buffer, send, recv = (
+            (up_in, up_send, up_recv) if step > 0 else (down_in, down_send, down_recv)
+        )
+        source = (left_ref if own else buffer).at[index, :, lanes]
+        return to(
+            source, buffer.at[index, :, lanes], send.at[index, h], recv.at[index, h],
+            row, (col + step) % n_col,
         )
 
     def w2_copy(off):
@@ -349,16 +388,44 @@
 
     def w4_copy(off):
         peer = (row + off) % n_row
-        mine = weight_all.at[rows_of(row, quarter)]
-        return to(mine, mine, w4_send.at[off], w4_recv.at[row], peer, col)
-
+        own = weight_all.at[rows_of(row, quarter)]
+        return to(own, own, w4_send.at[off], w4_recv.at[row], peer, col)
+
+    def left_own(index, step):
+        end = col == 0 if step > 0 else col == n_col - 1
+        for h in range(parts):
+            pl.when(end)(left_copy(index, h, step, True).start)
+
+    def left_pass(index, step):
+        buffer, recv = (up_in, up_recv) if step > 0 else (down_in, down_recv)
+        if step > 0:
+            on = jnp.logical_and(col > 0, col < index)
+        else:
+            on = jnp.logical_and(col < n_col - 1, col > index)
+        for h in range(parts):
+            lanes = slice(h * part, (h + 1) * part)
+
+            @pl.when(on)
+            def _(h=h, lanes=lanes):
+                arrived(buffer.at[index, :, lanes], recv.at[index, h])
+                buffer[index, :, lanes] = (
+                    buffer[index, :, lanes].astype(f32) + left_ref[index, :, lanes].astype(f32)
+                ).astype(bf16)
+                left_copy(index, h, step).start()
+
+    twin_copy.start()
     for off in range(1, n_row):
         w1_copy(off).start()
-    for off in range(1, n_row):
+    for k in range(n_col - 1, 1, -1):
+        left_own(k, 1)
+        left_own(n_col - 1 - k, -1)
+
+    arrived(right_twin, twin_recv)
+    right_half[...] = (
+        right_ref[rows_of(side, half)].astype(f32) + right_twin[...].astype(f32)
+    ).astype(bf16)
+    for off in range(1, chips):
         mid_copy(off).start()
-    late = n_col - 1
-    for off in range(1, late):
-        left_copy(off).start()
 
     own = weight_ref[rows_of(row, quarter), :].astype(f32)
     for off in range(1, n_row):
@@ -368,22 +435,27 @@
     weight_sum[...] = own.astype(bf16)
     for off in range(1, n_col):
         w2_copy(off).start()
-    left_copy(late).start()
-
-    total = right_ref[rows_of(row, many)].astype(f32)
-    for off in range(1, n_row):
-        peer = (row + off) % n_row
+    left_own(1, 1)
+    left_own(n_col - 2, -1)
+    left_pass(n_col - 1, 1)
+    left_pass(0, -1)
+
+    total = right_half[rows_of(chip, many)].astype(f32)
+    for off in range(1, chips):
+        peer = (chip + off) % chips
         arrived(right_mid.at[peer], mid_recv.at[peer])
         total = total + right_mid[peer].astype(f32)
     right_sum[...] = total.astype(bf16)
     for b in range(many):
-        here = jnp.logical_and(owner == row, row * many + b == col)
+        here = jnp.logical_and(owner == row, mine * many + b == col)
         pl.when(jnp.logical_not(here))(right_copy(b).start)
         pl.when(here)(
-            pltpu.make_async_copy(
-                right_sum.at[b], right_in.at[slot, row], right_recv.at[slot, row]
-            ).start
-        )
+            pltpu.make_async_copy(right_sum.at[b], right_in.at[slot], right_recv.at[slot]).start
+        )
+
+    for k in range(n_col - 2, 1, -1):
+        left_pass(k, 1)
+        left_pass(n_col - 1 - k, -1)
 
     own = weight_sum[rows_of(col, piece), :].astype(f32)
     for off in range(1, n_col):
@@ -394,37 +466,62 @@
     weight_all[rows_of(row * n_col + col, piece), :] = own.astype(bf16)
     for off in range(1, n_col):
         w3_copy(off).start()
+
+    for h in range(parts):
+        lanes = slice(h * part, (h + 1) * part)
+        left_out[:, lanes] = left_ref[col, :, lanes]
+
+        for on, buffer, recv in ((has_down, up_in, up_recv), (has_up, down_in, down_recv)):
+            both = jnp.logical_and(has_up, has_down)
+
+            @pl.when(on)
+            def _(buffer=buffer, recv=recv, h=h, lanes=lanes):
+                arrived(buffer.at[col, :, lanes], recv.at[col, h])
+
+        @pl.when(both)
+        def _(lanes=lanes):
+            left_out[:, lanes] = (
+                left_ref[col, :, lanes].astype(f32)
+                + up_in[col, :, lanes].astype(f32)
+                + down_in[col, :, lanes].astype(f32)
+            ).astype(bf16)
+
+        for on, buffer in ((jnp.logical_not(has_up), up_in), (jnp.logical_not(has_down), down_in)):
+
+            @pl.when(on)
+            def _(buffer=buffer, lanes=lanes):
+                left_out[:, lanes] = (
+                    left_ref[col, :, lanes].astype(f32) + buffer[col, :, lanes].astype(f32)
+                ).astype(bf16)
+
     for off in range(1, n_col):
         peer = (col + off) % n_col
         arrived(weight_all.at[rows_of(row * n_col + peer, piece)], w3_recv.at[peer])
     for off in range(1, n_row):
         w4_copy(off).start()
-
-    total = left_ref[col].astype(f32)
-    for off in range(1, n_col):
-        peer = (col + off) % n_col
-        arrived(left_in.at[peer], left_recv.at[peer])
-        total = total + left_in[peer].astype(f32)
-    left_out[...] = total.astype(bf16)
     for t in range(ratio):
-        source = col // many
-        arrived(right_in.at[t, source], right_recv.at[t, source])
-        right_out[t] = right_in[t, source]
+        arrived(right_in.at[t], right_recv.at[t])
+        right_out[t] = right_in[t]
     for off in range(1, n_row):
         peer = (row + off) % n_row
         arrived(weight_all.at[rows_of(peer, quarter)], w4_recv.at[peer])
     weight_out[...] = weight_all[...].astype(f32) * (1.0 / WINDOW_AMINOS)
 
+    twin_copy.wait_send()
+    for off in range(1, chips):
+        mid_copy(off).wait_send()
     for off in range(1, n_row):
         w1_copy(off).wait_send()
-        mid_copy(off).wait_send()
         w4_copy(off).wait_send()
     for off in range(1, n_col):
-        left_copy(off).wait_send()
         w2_copy(off).wait_send()
         w3_copy(off).wait_send()
+    for index in range(n_col):
+        for h in range(parts):
+            pl.when(col < index)(left_copy(index, h, 1).wait_send)
+            pl.when(col > index)(left_copy(index, h, -1).wait_send)
     for b in range(many):
-        here = jnp.logical_and(owner == row, row * many + b == col)
+        here = jnp.logical_and(owner == row, mine * many + b == col)
         pl.when(jnp.logical_not(here))(right_copy(b).wait_send)
 
 
@@ -477,7 +574,7 @@
             jax.ShapeDtypeStruct((seqs, wide), bf16),
         ],
         scratch_shapes=[
-            dma((n_col,)), dma((n_col,)), dma((ratio,)), dma((n_col,)),
+            dma((n_col, 2)), dma((n_col, 2)), dma((n_col, 2)), dma((ratio,)), dma((n_col,)),
             dma((n_col, n_row // 2)), dma((n_col,)), dma((2,)),
         ],
         compiler_params=pltpu.CompilerParams(collective_id=0, has_side_effects=True),
@@ -579,17 +676,21 @@
         ],
         scratch_shapes=[
             pltpu.VMEM((n_col, share, rows * size), bf16),
-            pltpu.VMEM((n_row, many, share, wide), bf16),
+            pltpu.VMEM((n_col, share, rows * size), bf16),
+            pltpu.VMEM((n_col // 2, share, wide), bf16),
+            pltpu.VMEM((n_col // 2, share, wide), bf16),
+            pltpu.VMEM((n_row // 2, many, share, wide), bf16),
             pltpu.VMEM((many, share, wide), bf16),
-            pltpu.VMEM((ratio, n_row, share, wide), bf16),
+            pltpu.VMEM((ratio, share, wide), bf16),
             pltpu.VMEM((n_row, quarter, CZ), bf16),
             pltpu.VMEM((quarter, CZ), bf16),
             pltpu.VMEM((n_col, piece, CZ), bf16),
             pltpu.VMEM((piece, CZ), bf16),
             pltpu.VMEM((size * size, CZ), bf16),
-            dma((n_col,)), dma((n_col,)),
-            dma((n_row,)), dma((n_row,)),
-            dma((many,)), dma((ratio, n_row)),
+            dma((n_col, 2)), dma((n_col, 2)), dma((n_col, 2)), dma((n_col, 2)),
+            dma, dma,
+            dma((n_row // 2,)), dma((n_row // 2,)),
+            dma((many,)), dma((ratio,)),
             dma((n_row,)), dma((n_row,)),
             dma((n_col,)), dma((n_col,)),
             dma((n_col,)), dma((n_col,)),

time: 96.6 us -> 98.7 us (1.022)
  Pallas kernels: 78.9 us -> 80.1 us
    pallas_call x1, Pallas kernels: 33.4 us -> 35.8 us  [shards(): pl.pallas_call(functools.partial(sum_kernel, n_row, n_col, ratio), in_spe...]
where the time goes in v2:
time: 98.7 us; the launch traced here: 97.1 us
  Pallas kernels  80.1 us (81%)
  local copies, waits for them, and re-layouts  10.8 us (11%)
  other arithmetic  3.85 us (4%)
  matrix products  1.52 us (2%)
    pallas_call x1, Pallas kernels, shards(): pl.pallas_call(functools.partial(sum_kernel, n_row, n_col, ratio), in_spe...  35.8 us
    pallas_call x1, Pallas kernels, shards(): pl.pallas_call(functools.partial(gather_kernel, n_row, n_col, ratio), in_...  23 us
    pallas_call x1, Pallas kernels, shards(): pl.pallas_call(functools.partial(pair_kernel, tile, cols, seqs), grid_spe...  21.2 us

profile of v2, /device:TPU:1, one launch (start us, length us, event | category | flops | bytes accessed | tf_op | source)
XLA Modules:
  0.0 97.1 jit_solution(2310163448450075852)
XLA Ops:
  0.6 0.0 copy-start
  0.6 0.9 fusion.14
  1.5 0.0 copy-start.7
  1.5 0.1 broadcast_in_dim.8
  1.6 0.9 fusion.9
  2.5 0.1 tile.9
  2.6 0.6 pad.4.table_ref
  3.2 0.0 copy-start.3
  3.2 1.6 %convert_reduce_fusion = f32[32,64]{1,0:T(8,128)S(1)} fusion(bf16[32,64,256]{2,1,0:T(8,128)(2,1)} %param.10), kind=kLoop, calls=%fused_computation.1 | loop fusion | flops 1046528 | bytes 1056768 | tf_op jit(solution)/shard_map/reduce_sum | solution.py:20
  4.8 0.0 copy-done
  4.8 0.6 fusion.2
  5.5 0.0 copy-start.8
  5.5 0.0 copy-start.9
  5.5 0.1 broadcast_in_dim.9
  5.6 0.7 broadcast_in_dim.20.chain_ref
  6.3 0.0 copy-done.7
  6.3 0.2 convolution_divide_fusion
  6.5 0.7 tile.21.inverse_ref
  7.2 0.0 copy-done.3
  7.2 0.2 copy.22
  7.5 0.0 copy-start.1
  7.5 0.8 copy.23
  8.4 0.0 copy-done.8
  8.4 0.0 copy-done.9
  8.4 0.0 copy-start.5
  8.4 0.0 copy-start.6
  8.4 0.7 fusion.5
  9.1 0.0 copy-done.1
  9.1 0.0 copy-done.5
  9.1 0.0 copy-done.6
  9.2 0.4 convolution_convert_fusion
  9.6 0.2 reshape.83
  9.9 0.1 copy.30
  10.0 0.9 reshape.84.right_ref
  10.9 0.3 copy.20
  11.2 1.2 %reshape.82.left_ref = bf16[32,2048]{1,0:T(8,128)(2,1)} reshape(bf16[2048,32]{1,0:T(8,128)(2,1)S(1)} %copy.20) | data formatting | bytes 262144 | tf_op jit(solution)/shard_map/reshape | solution.py:561
  12.4 23.0 %shard_map.129 = (bf16[128,2048]{1,0:T(8,128)(2,1)}, bf16[128,2048]{1,0:T(8,128)(2,1)}) custom-call(bf16[32,2048]{1,0:T(8,128)(2,1)} %reshape.82.left_ref, bf16[1,32,2048]{2,1,0:T(8,128)(2,1)} %reshape.84.right_ref), custom_call_target="tpu_custom_call" | custom-call | tf_op jit(solution)/shard_map/pallas_call | solution.py:568
  35.4 21.2 %shard_map.130 = (bf16[4096,128]{1,0:T(8,128)(2,1)}, bf16[128,2048]{1,0:T(8,128)(2,1)}, bf16[128,2048]{1,0:T(8,128)(2,1)}, bf16[1024,128]{1,0:T(8,128)(2,1)}) custom-call(s32[64]{0:T(128)} %copy-done.7, bf16[128,2048]{1,0:T(8,128)(2,1)} %get-tuple-element.13.left_ref, bf16[128,2048]{1,0:T(8,128)(2,1)} %get-tuple-element.14.right_ref, ...), custom_call_target="tpu_custom_call" | custom-call | tf_op jit(solution)/shard_map/pallas_call | solution.py:608
  56.6 35.8 %shard_map.131 = (bf16[32,2048]{1,0:T(8,128)(2,1)}, bf16[1,32,2048]{2,1,0:T(8,128)(2,1)}, f32[1024,128]{1,0:T(8,128)}) custom-call(bf16[4,32,2048]{2,1,0:T(8,128)(2,1)} %bitcast.41, bf16[4,32,2048]{2,1,0:T(8,128)(2,1)} %bitcast.42, bf16[1024,128]{1,0:T(8,128)(2,1)} %get-tuple-element.18.weight_ref), custom_call_target="tpu_custom_call" | custom-call | tf_op jit(solution)/shard_map/pallas_call | solution.py:668
  92.5 0.0 copy-start.2
  92.5 1.2 %reshape.91 = bf16[1,32,32,64]{3,2,1,0:T(8,128)(2,1)S(1)} reshape(bf16[1,32,2048]{2,1,0:T(8,128)(2,1)} %get-tuple-element.20) | data formatting | bytes 262144 | tf_op jit(solution)/shard_map/reshape | solution.py:706
  93.7 0.3 copy.24
  94.0 0.0 copy-start.4
  94.0 1.2 %reshape.92 = bf16[32,2048]{1,0:T(8,128)(2,1)} reshape(bf16[32,1,64,32]{3,2,0,1:T(8,128)(2,1)S(1)} %bitcast.36) | data formatting | bytes 262144 | tf_op jit(solution)/shard_map/reshape | solution.py:708
  95.2 0.0 copy-done.2
  95.2 1.2 %copy.25 = f32[32,16,2,128]{3,2,1,0:T(2,128)} copy(f32[32,16,2,128]{3,0,1,2:T(8,128)S(1)} %bitcast.44) | data formatting | bytes 1048576 | tf_op jit(solution)/shard_map/transpose | solution.py:711
  96.4 0.0 copy-done.4
  96.4 0.7 copy.32
  (6 shorter events, 0.1 us)
Async XLA Ops:
  0.6 4.2 %copy-start = (bf16[32,64,256]{2,1,0:T(8,128)(2,1)S(1)}, bf16[32,64,256]{2,1,0:T(8,128)(2,1)}, u32[]{:S(2)}) copy-start(bf16[32,64,256]{2,1,0:T(8,128)(2,1)} %param.10) | copy-start | bytes 3145732
  1.5 4.8 %copy-start.7 = (s32[64]{0:T(128)}, s32[64]{0:T(128)S(1)}, u32[]{:S(2)}) copy-start(s32[64]{0:T(128)S(1)} %get-tuple-element.23.labels_ref) | copy-start | bytes 772
  3.2 4.0 %copy-start.3 = (bf16[1024,128]{1,0:T(8,128)(2,1)S(1)}, bf16[1024,128]{1,0:T(8,128)(2,1)}, u32[]{:S(2)}) copy-start(bf16[1024,128]{1,0:T(8,128)(2,1)} %param.15) | copy-start | bytes 786436
  5.5 2.9 %copy-start.8 = (f32[256]{0:T(256)S(1)}, f32[256]{0:T(256)}, u32[]{:S(2)}) copy-start(f32[256]{0:T(256)} %param.12) | copy-start | bytes 3076
  5.5 2.9 %copy-start.9 = (f32[256]{0:T(256)S(1)}, f32[256]{0:T(256)}, u32[]{:S(2)}) copy-start(f32[256]{0:T(256)} %param.11) | copy-start | bytes 3076
  7.5 1.6 %copy-start.1 = (bf16[64,8,2,128]{3,1,2,0:T(8,128)(2,1)}, bf16[64,8,2,128]{3,1,2,0:T(8,128)(2,1)S(1)}, u32[]{:S(2)}) copy-start(bf16[64,8,2,128]{3,1,2,0:T(8,128)(2,1)S(1)} %copy.29) | copy-start | bytes 786436
  8.4 0.8 copy-start.5
  8.4 0.8 copy-start.6
  92.5 2.7 %copy-start.2 = (f32[1024,128]{1,0:T(8,128)S(1)}, f32[1024,128]{1,0:T(8,128)}, u32[]{:S(2)}) copy-start(f32[1024,128]{1,0:T(8,128)} %get-tuple-element.21) | copy-start | bytes 1572868
  94.0 2.4 %copy-start.4 = (bf16[32,2048]{1,0:T(8,128)(2,1)S(1)}, bf16[32,2048]{1,0:T(8,128)(2,1)}, u32[]{:S(2)}) copy-start(bf16[32,2048]{1,0:T(8,128)(2,1)} %get-tuple-element.32) | copy-start | bytes 393220

commit v3 on v1

v3 whole, which is shorter than its diff:
```python
import functools

import jax
import jax.numpy as jnp
from jax import lax
from jax.experimental import pallas as pl
from jax.experimental.pallas import tpu as pltpu
from jax.sharding import PartitionSpec as P

PROJECTED_SIZE = 32
CZ = 128
WINDOW_AMINOS = 256
CHAINS = 8
LANES = 128
MESH = pl.DeviceIdType.MESH


def standardize_entries(alignment_tensor, standard_multiplier, additive_offset):
    incoming_entries = alignment_tensor.astype(jnp.float32)
    center = incoming_entries - jnp.mean(incoming_entries, axis=-1, keepdims=True)
    spread = jnp.mean(center * center, axis=-1, keepdims=True)
    return (center * lax.rsqrt(spread + 1e-05) * standard_multiplier + additive_offset).astype(
        jnp.bfloat16
    )


def to(source, target, send, recv, row, col):
    return pltpu.make_async_remote_copy(
        src_ref=source,
        dst_ref=target,
        send_sem=send,
        recv_sem=recv,
        device_id={"row": row, "col": col},
        device_id_type=MESH,
    )


def arrived(ref, sem):
    pltpu.make_async_copy(ref, ref, sem).wait()


def greet(n_row, n_col, me):
    peers = n_row * n_col
    barrier = pltpu.get_barrier_semaphore()

    def signal(off, carry):
        peer = (me + off) % peers
        pl.semaphore_signal(
            barrier,
            inc=1,
            device_id={"row": peer // n_col, "col": peer % n_col},
            device_id_type=MESH,
        )
        return carry

    lax.fori_loop(1, peers, signal, 0)
    return lambda: pl.semaphore_wait(barrier, peers - 1)


def fill_tables(rows, cols, labels_ref, counts_ref, row, col, table_ref, inverse_ref):
    f32 = jnp.float32
    inner = LANES // cols
    lane = lax.broadcasted_iota(jnp.int32, (1, LANES), 1) % cols
    label = jnp.zeros((1, LANES), jnp.int32)
    for j in range(cols):
        label = jnp.where(lane == j, labels_ref[col * cols + j], label)
    table_ref[...] = jnp.zeros_like(table_ref)
    for a in range(CHAINS):
        line = jnp.zeros((1, LANES), jnp.int32)
        for b in range(CHAINS):
            line = jnp.where(label == b, counts_ref[a, b], line)
        table_ref[a : a + 1, :] = line.astype(f32)

    def divide(i, carry):
        inverse_ref[pl.ds(i, 1), :] = 1.0 / table_ref[pl.ds(labels_ref[row * rows + i], 1), :]
        return carry

    lax.fori_loop(0, rows, divide, 0)


def fill_weights(blocks, final_ref, wide_ref, weight_ref, weight_t_ref):
    size = PROJECTED_SIZE
    inner = size // blocks
    wide_ref[...] = final_ref[...].astype(jnp.float32)
    for b in range(blocks):
        for e in range(inner):
            weight_ref[b * size : (b + 1) * size, e * CZ : (e + 1) * CZ] = wide_ref[
                pl.ds(b * inner + e, size, stride=size), :
            ].astype(jnp.bfloat16)
    weight_t_ref[...] = weight_ref[...].T


def project(
    share, rows, align_ref, gain_ref, shift_ref, first_ref, second_ref,
    normed_ref, line_ref, turn_ref, left_own, right_own,
):
    f32, bf16 = jnp.float32, jnp.bfloat16
    size = PROJECTED_SIZE
    feats = align_ref.shape[2]
    gain, shift = gain_ref[...], shift_ref[...]

    def normalise(k, carry):
        x = align_ref[pl.ds(k * 4, 4)].reshape(4 * rows, feats).astype(f32)
        center = x - jnp.mean(x, axis=-1, keepdims=True)
        var = jnp.mean(center * center, axis=-1, keepdims=True)
        normed_ref[pl.ds(pl.multiple_of(k * 4 * rows, 4 * rows), 4 * rows), :] = (
            center * lax.rsqrt(var + 1e-05) * gain + shift
        ).astype(bf16)
        return carry

    lax.fori_loop(0, share // 4, normalise, 0)
    low = share // 2
    second = second_ref[...]
    for p in range(low):
        pair = jnp.concatenate(
            [normed_ref[p * rows : (p + 1) * rows], normed_ref[(p + low) * rows : (p + low + 1) * rows]],
            axis=0,
        )
        turn_ref[p * size : (p + 1) * size, :] = lax.dot_general(
            second, pair, (((1,), (1,)), ((), ())), preferred_element_type=f32
        )
    near = lax.broadcasted_iota(jnp.int32, (low, LANES), 1) < rows
    for b in range(size // 2):
        even = turn_ref[pl.ds(2 * b, low, stride=size), :]
        odd = turn_ref[pl.ds(2 * b + 1, low, stride=size), :]
        lanes = slice(b * LANES, (b + 1) * LANES)
        right_own[0, :low, lanes] = jnp.where(near, even, pltpu.roll(odd, rows, 1)).astype(bf16)
        right_own[0, low:, lanes] = jnp.where(near, pltpu.roll(even, rows, 1), odd).astype(bf16)
    yield
    fold = LANES // size
    first = jnp.concatenate([first_ref[...]] * fold, axis=1)
    line_ref[...] = jnp.dot(normed_ref[...], first, preferred_element_type=f32)
    place = lax.broadcasted_iota(jnp.int32, (share, LANES), 1) // size
    for g in range(rows // fold):
        total = line_ref[pl.ds(g * fold, share, stride=rows), :]
        for k in range(1, fold):
            total = jnp.where(
                place == k, line_ref[pl.ds(g * fold + k, share, stride=rows), :], total
            )
        left_own[:, g * LANES : (g + 1) * LANES] = total.astype(bf16)
    yield


def gather_kernel(
    n_row, n_col, ratio, rows, cols, tile, fused, *refs
):
    f32, bf16 = jnp.float32, jnp.bfloat16
    size = PROJECTED_SIZE
    inner = LANES // cols
    blocks = size // inner
    labels_ref, counts_ref, final_ref, grad_ref = refs[:4]
    count = 9 if fused else 6
    source_refs = refs[4:count]
    left_out, right_out, table_ref, inverse_ref, weight_ref, weight_t_ref, scaled_out = refs[
        count : count + 7
    ]
    grad, spread, scaled, wide_ref = refs[count + 7 : count + 11]
    refs = refs[count + 11 :]
    if fused:
        normed_ref, line_ref, turn_ref, left_ref, right_ref = refs[:5]
        refs = refs[5:]
    else:
        left_ref, right_ref = source_refs
    (
        left_send, left_recv, right_send, right_recv, hop_send, twin_send, own_sem, grad_sem,
        scaled_sem,
    ) = refs
    row, col = lax.axis_index("row"), lax.axis_index("col")
    share = left_ref.shape[0]
    ready = greet(n_row, n_col, row * n_col + col)
    grad_copy = pltpu.make_async_copy(grad_ref, grad, grad_sem)
    grad_copy.start()
    block = lambda ref, index: ref.at[pl.ds(pl.multiple_of(index * share, share), share)]
    owner = col // ratio
    twin = row + 1 - 2 * (row % 2)
    chips = n_row // 2
    is_owner = row == owner
    same_side = row % 2 == owner % 2

    def right_copy(t):
        return to(
            right_ref.at[t], block(right_out, col), right_send.at[t], right_recv.at[col],
            row, row * ratio + t,
        )

    def left_copy(off):
        peer = (col + off) % n_col
        return to(left_ref, block(left_out, col), left_send.at[off], left_recv.at[col], row, peer)

    def hop_copy(source, index, hop):
        return to(
            source, block(right_out, index), hop_send.at[index, hop], right_recv.at[index],
            (row + 2 * hop) % n_row, col,
        )

    def twin_copy(source, index):
        return to(
            source, block(right_out, index), twin_send.at[index], right_recv.at[index], twin, col
        )

    work = project(share, rows, *source_refs, *((normed_ref, line_ref, turn_ref, left_ref, right_ref))) if fused else None
    if fused:
        next(work)
    ready()
    for t in range(ratio):
        pl.when(row * ratio + t != col)(right_copy(t).start)
    mine = right_ref.at[col % ratio]
    own_right = pltpu.make_async_copy(mine, block(right_out, col), own_sem.at[1])

    @pl.when(is_owner)
    def _():
        own_right.start()
        for hop in range(1, chips):
            hop_copy(mine, col, hop).start()
        twin_copy(mine, col).start()

    if fused:
        next(work)
    own_left = pltpu.make_async_copy(left_ref, block(left_out, col), own_sem.at[0])
    own_left.start()
    for off in range(1, n_col):
        left_copy(off).start()

    def pass_right(off):
        peer = (col + off) % n_col
        source = block(right_out, peer)
        if off:
            arrived(source, right_recv.at[peer])

            @pl.when(is_owner)
            def _():
                for hop in range(1, chips):
                    hop_copy(source, peer, hop).start()

            pl.when(same_side)(twin_copy(source, peer).start)
        else:

            @pl.when(jnp.logical_not(is_owner))
            def _():
                arrived(source, right_recv.at[peer])

            pl.when(jnp.logical_and(same_side, jnp.logical_not(is_owner)))(
                twin_copy(source, peer).start
            )

    fill_weights(blocks, final_ref, wide_ref, weight_ref, weight_t_ref)
    fill_tables(rows, cols, labels_ref, counts_ref, row, col, table_ref, inverse_ref)
    spread[...] = jnp.zeros_like(spread)
    grad_copy.wait()
    steps = rows // tile

    def scaled_copy(step, slot):
        extent = tile * size
        return pltpu.make_async_copy(
            scaled.at[slot],
            scaled_out.at[pl.ds(pl.multiple_of(step * extent, extent), extent)],
            scaled_sem.at[slot],
        )

    def scale(step, carry):
        slot = step % 2
        first = pl.multiple_of(step * tile * cols, tile * cols)
        part = grad[pl.ds(first, tile * cols), :]
        for i in range(tile):
            for e in range(inner):
                spread[i * LANES + e * cols : i * LANES + (e + 1) * cols, e * CZ : (e + 1) * CZ] = (
                    part[i * cols : (i + 1) * cols]
                )
        inverse = inverse_ref[pl.ds(pl.multiple_of(step * tile, tile), tile), :]

        @pl.when(step >= 2)
        def _():
            scaled_copy(step - 2, slot).wait()

        for i in range(0, tile, 2):
            back = lax.dot_general(
                weight_ref[...], spread[i * LANES : (i + 2) * LANES, :], (((1,), (1,)), ((), ())),
                preferred_element_type=f32,
            )
            for k in range(2):
                piece = (
                    back[:, k * LANES : (k + 1) * LANES] * inverse[i + k : i + k + 1]
                ).astype(bf16)
                for b in range(blocks):
                    scaled[
                        slot, (i + k) * size : (i + k + 1) * size, b * LANES : (b + 1) * LANES
                    ] = piece[b * size : (b + 1) * size]
        scaled_copy(step, slot).start()
        for off in range(n_col - 1):
            pl.when(step == min(2 * off + 1, steps - 1))(functools.partial(pass_right, off))
        return carry

    lax.fori_loop(0, steps, scale, 0)
    pass_right(n_col - 1)
    for step in range(max(0, steps - 2), steps):
        scaled_copy(step, step % 2).wait()

    own_left.wait()
    pl.when(is_owner)(own_right.wait)
    for off in range(1, n_col):
        peer = (col + off) % n_col
        arrived(block(left_out, peer), left_recv.at[peer])
    for off in range(1, n_col):
        left_copy(off).wait_send()
    for t in range(ratio):
        pl.when(row * ratio + t != col)(right_copy(t).wait_send)

    @pl.when(is_owner)
    def _():
        for off in range(n_col):
            peer = (col + off) % n_col
            for hop in range(1, chips):
                hop_copy(block(right_out, peer), peer, hop).wait_send()

    @pl.when(same_side)
    def _():
        for off in range(n_col):
            peer = (col + off) % n_col
            twin_copy(block(right_out, peer), peer).wait_send()


def pair_kernel(
    tile, cols, seqs,
    labels_ref,
    left_ref, right_ref, table_ref, inverse_ref, grad_ref, scaled, weight_t_ref, bias_ref,
    pair_ref, left_grad_ref, right_grad_ref, weight_grad_ref,
    kept, kept_t, spread, outer, acc, left_acc, right_acc, weight_acc, slots,
):
    step = pl.program_id(0)
    size = PROJECTED_SIZE
    inner = LANES // cols
    blocks = size // inner
    width = 2 * LANES if blocks % 2 == 0 else LANES
    f32, bf16 = jnp.float32, jnp.bfloat16
    seq = lax.broadcasted_iota(jnp.int32, (seqs, LANES), 0).astype(f32)

    @pl.when(step == 0)
    def _():
        spread[...] = jnp.zeros_like(spread)
        right_acc[...] = jnp.zeros_like(right_acc)
        weight_acc[...] = jnp.zeros_like(weight_acc)

        def fill(chain, carry):
            keep = jnp.where(seq < table_ref[pl.ds(chain, 1), :], 1.0, 0.0).astype(bf16)
            for b in range(blocks):
                lanes = slice(b * LANES, (b + 1) * LANES)
                piece = right_ref[:, lanes] * keep
                kept[chain, :, lanes] = piece
                kept_t[chain, lanes, :] = piece.T
            return carry

        extent = pl.num_programs(0) * tile
        first = lax.axis_index("row") * extent
        lax.fori_loop(labels_ref[first], labels_ref[first + extent - 1] + 2, fill, 0)

    for i in range(tile):
        grad = grad_ref[i * cols : (i + 1) * cols, :]
        for e in range(inner):
            spread[i * LANES + e * cols : i * LANES + (e + 1) * cols, e * CZ : (e + 1) * CZ] = grad
    inverse = [inverse_ref[i : i + 1, :] for i in range(tile)]
    offset = lax.axis_index("row") * (pl.num_programs(0) * tile)
    label = [labels_ref[offset + step * tile + i] for i in range(tile)]
    place = lax.broadcasted_iota(jnp.int32, (1, tile * size), 1) // size
    lane = jnp.zeros((1, tile * size), jnp.int32)
    for i in range(tile):
        lane = jnp.where(place == i, label[i], lane)
    low, high = label[0], label[tile - 1]

    def chain_pair(first, chain):
        left = left_ref[...]
        for k in range(2):
            slots[k * seqs : (k + 1) * seqs, :] = left * jnp.where(
                lane == chain + k, 1.0, 0.0
            ).astype(bf16)
        both = slots[...]
        both_t = both.T
        keep = [seq < table_ref[pl.ds(chain + k, 1), :] for k in range(2)]
        for start in range(0, blocks * LANES, width):
            lanes = slice(start, start + width)
            right = kept[pl.ds(chain, 2), :, lanes].reshape(2 * seqs, width)
            prod = jnp.dot(both_t, right, preferred_element_type=f32)
            if first:
                acc[:, lanes] = prod
            else:
                acc[:, lanes] += prod
            out = jnp.dot(both, scaled[:, lanes], preferred_element_type=f32)
            for b in range(width // LANES):
                part = slice(b * LANES, (b + 1) * LANES)
                right_acc[:, start + b * LANES : start + (b + 1) * LANES] += jnp.where(
                    keep[0], out[:seqs, part], 0.0
                ) + jnp.where(keep[1], out[seqs:, part], 0.0)
        right_t = jnp.concatenate([kept_t[chain], kept_t[chain + 1]], axis=1)
        out = jnp.dot(scaled[...], right_t, preferred_element_type=f32)
        for i in range(tile):
            rows = slice(i * size, (i + 1) * size)
            part = jnp.where(label[i] == chain, out[rows, :seqs], 0.0) + jnp.where(
                label[i] == chain + 1, out[rows, seqs:], 0.0
            )
            if first:
                left_acc[rows, :] = part
            else:
                left_acc[rows, :] += part

    chain_pair(True, low)

    def more(p, carry):
        chain_pair(False, low + 2 * p)
        return carry

    lax.fori_loop(1, (high - low) // 2 + 1, more, 0)
    left_grad_ref[...] = left_acc[...].T.astype(bf16)
    for i in range(tile):
        for b in range(blocks):
            outer[b * size : (b + 1) * size, i * LANES : (i + 1) * LANES] = (
                acc[i * size : (i + 1) * size, b * LANES : (b + 1) * LANES] * inverse[i]
            ).astype(bf16)
    group = lax.broadcasted_iota(jnp.int32, (CZ, LANES), 1) // cols
    for i in range(0, tile, 2):
        both = jnp.dot(
            weight_t_ref[...], outer[:, i * LANES : (i + 2) * LANES], preferred_element_type=f32
        )
        for k in range(2):
            lanes = slice(k * LANES, (k + 1) * LANES)
            total = both[:CZ, lanes]
            for e in range(1, inner):
                total = jnp.where(group == e, both[e * CZ : (e + 1) * CZ, lanes], total)
            turned = total.T
            pair = turned[:cols]
            for e in range(1, inner):
                pair = pair + turned[e * cols : (e + 1) * cols]
            pair_ref[(i + k) * cols : (i + k + 1) * cols, :] = (pair + bias_ref[...]).astype(bf16)
    weight_acc[...] += jnp.dot(outer[...], spread[...], preferred_element_type=f32)

    @pl.when(step == pl.num_programs(0) - 1)
    def _():
        right_grad_ref[...] = right_acc[...].astype(bf16)
        rows = blocks * size
        for e in range(inner):
            weight_grad_ref[e * rows : (e + 1) * rows, :] = weight_acc[
                :, e * CZ : (e + 1) * CZ
            ].astype(bf16)


def sum_kernel(
    n_row, n_col, ratio, blocks,
    left_ref, right_ref, weight_ref,
    left_out, right_out, weight_out,
    left_in, right_twin, right_half, right_mid, right_sum, right_in,
    weight_mid, weight_sum, weight_in, weight_part, weight_all,
    up_send, down_send, left_recv, twin_send, twin_recv, mid_send, mid_recv,
    right_send, right_recv,
    w1_send, w1_recv, w2_send, w2_recv, w3_send, w3_recv, w4_send, w4_recv,
):
    f32, bf16 = jnp.float32, jnp.bfloat16
    row, col = lax.axis_index("row"), lax.axis_index("col")
    greet(n_row, n_col, row * n_col + col)()
    chips = n_row // 2
    chip, side = row // 2, row % 2
    twin = row + 1 - 2 * side
    many = n_col // n_row
    half = n_col // 2
    quarter = weight_ref.shape[0] // n_row
    piece = quarter // n_col
    parts = left_recv.shape[1]
    part = left_ref.shape[2] // parts
    owner, slot = col // ratio, col % ratio
    rows_of = lambda index, extent: pl.ds(pl.multiple_of(index * extent, extent), extent)
    mine = side * chips + chip

    def w1_copy(off):
        peer = (row + off) % n_row
        return to(
            weight_ref.at[rows_of(peer, quarter)], weight_mid.at[row], w1_send.at[off],
            w1_recv.at[row], peer, col,
        )

    twin_copy = to(
        right_ref.at[rows_of(1 - side, half)], right_twin, twin_send, twin_recv, twin, col
    )

    def mid_copy(off):
        peer = (chip + off) % chips
        return to(
            right_half.at[rows_of(peer, many)], right_mid.at[chip], mid_send.at[off],
            mid_recv.at[chip], 2 * peer + side, col,
        )

    def right_copy(b):
        return to(
            right_sum.at[b], right_in.at[slot], right_send.at[b], right_recv.at[slot],
            owner, mine * many + b,
        )

    def left_copies(d, h):
        lanes = slice(h * part, (h + 1) * part)
        for step, sends in ((d, up_send), (-d, down_send)):
            there = col + step
            peer = there % n_col
            copy = to(
                left_ref.at[peer, :, lanes], left_in.at[col, :, lanes], sends.at[d, h],
                left_recv.at[col, h], row, peer,
            )
            yield jnp.logical_and(there >= 0, there < n_col), copy

    def left_start(d, h):
        for on, copy in left_copies(d, h):
            pl.when(on)(copy.start)

    def w2_copy(off):
        peer = (col + off) % n_col
        return to(
            weight_sum.at[rows_of(peer, piece)], weight_in.at[col], w2_send.at[off],
            w2_recv.at[col], row, peer,
        )

    def w3_copy(off):
        peer = (col + off) % n_col
        return to(
            weight_part, weight_all.at[rows_of(row * n_col + col, piece)], w3_send.at[off],
            w3_recv.at[col], row, peer,
        )

    def w4_copy(off):
        peer = (row + off) % n_row
        own = weight_all.at[rows_of(row, quarter)]
        return to(own, own, w4_send.at[off], w4_recv.at[row], peer, col)

    for off in range(1, n_row):
        w1_copy(off).start()
    twin_copy.start()
    for h in range(parts):
        left_start(1, h)
    left_start(2, 0)

    arrived(right_twin, twin_recv)
    right_half[...] = (
        right_ref[rows_of(side, half)].astype(f32) + right_twin[...].astype(f32)
    ).astype(bf16)
    for off in range(1, chips):
        mid_copy(off).start()

    own = weight_ref[rows_of(row, quarter), :].astype(f32)
    for off in range(1, n_row):
        peer = (row + off) % n_row
        arrived(weight_mid.at[peer], w1_recv.at[peer])
        own = own + weight_mid[peer].astype(f32)
    weight_sum[...] = own.astype(bf16)
    for off in range(1, n_col):
        w2_copy(off).start()
    for h in range(1, parts):
        left_start(2, h)

    total = right_half[rows_of(chip, many)].astype(f32)
    for off in range(1, chips):
        peer = (chip + off) % chips
        arrived(right_mid.at[peer], mid_recv.at[peer])
        total = total + right_mid[peer].astype(f32)
    right_sum[...] = total.astype(bf16)
    for b in range(many):
        here = jnp.logical_and(owner == row, mine * many + b == col)
        pl.when(jnp.logical_not(here))(right_copy(b).start)
        pl.when(here)(
            pltpu.make_async_copy(right_sum.at[b], right_in.at[slot], right_recv.at[slot]).start
        )

    own = weight_sum[rows_of(col, piece), :].astype(f32)
    for off in range(1, n_col):
        peer = (col + off) % n_col
        arrived(weight_in.at[peer], w2_recv.at[peer])
        own = own + weight_in[peer].astype(f32)
    weight_part[...] = own.astype(bf16)
    weight_all[rows_of(row * n_col + col, piece), :] = own.astype(bf16)
    for off in range(1, n_col):
        w3_copy(off).start()
    for d in range(3, n_col):
        for h in range(parts):
            left_start(d, h)

    for off in range(1, n_col):
        peer = (col + off) % n_col
        arrived(weight_all.at[rows_of(row * n_col + peer, piece)], w3_recv.at[peer])
    for off in range(1, n_row):
        w4_copy(off).start()

    total = left_ref[col].astype(f32)
    for off in range(1, n_col):
        peer = (col + off) % n_col
        for h in range(parts):
            arrived(left_in.at[peer, :, h * part : (h + 1) * part], left_recv.at[peer, h])
        total = total + left_in[peer].astype(f32)
    left_out[...] = total.astype(bf16)
    for t in range(ratio):
        arrived(right_in.at[t], right_recv.at[t])
        right_out[t] = right_in[t]
    for off in range(1, n_row):
        peer = (row + off) % n_row
        arrived(weight_all.at[rows_of(peer, quarter)], w4_recv.at[peer])
    size = PROJECTED_SIZE
    for g in range(size):
        e = (g % blocks) * (size // blocks) + g // blocks
        weight_out[pl.ds(e, size, stride=size), :] = weight_all[
            g * size : (g + 1) * size, :
        ].astype(f32) * (1.0 / WINDOW_AMINOS)

    twin_copy.wait_send()
    for off in range(1, chips):
        mid_copy(off).wait_send()
    for off in range(1, n_row):
        w1_copy(off).wait_send()
        w4_copy(off).wait_send()
    for off in range(1, n_col):
        w2_copy(off).wait_send()
        w3_copy(off).wait_send()
        for h in range(parts):
            for on, copy in left_copies(off, h):
                pl.when(on)(copy.wait_send)
    for b in range(many):
        here = jnp.logical_and(owner == row, mine * many + b == col)
        pl.when(jnp.logical_not(here))(right_copy(b).wait_send)


def shards(
    alignment_tensor,
    standardizer_scaling,
    standardizer_offset,
    first_projector,
    second_projector,
    final_projector,
    final_offset,
    amino_strand_label,
    matched_strand_count,
    couple_delta_adjoint,
):
    f32, bf16 = jnp.float32, jnp.bfloat16
    share, rows, feats = alignment_tensor.shape
    cols = couple_delta_adjoint.shape[1]
    size = PROJECTED_SIZE
    n_row, n_col = lax.axis_size("row"), lax.axis_size("col")
    ratio = rows // cols
    seqs = share * n_col
    inner = LANES // cols
    blocks = size // inner
    wide = size * cols
    vmem = pl.BlockSpec(memory_space=pltpu.VMEM)
    dma = pltpu.SemaphoreType.DMA

    tile = 8
    steps = rows // tile
    fused = ratio == 1 and 2 * rows == LANES and share % 16 == 0
    if fused:
        sources = (
            alignment_tensor, standardizer_scaling[None, :], standardizer_offset[None, :],
            first_projector, second_projector.T,
        )
        extra = [
            pltpu.VMEM((share * rows, feats), bf16),
            pltpu.VMEM((share * rows, LANES), f32),
            pltpu.VMEM((share // 2 * size, LANES), f32),
            pltpu.VMEM((share, rows * size), bf16),
            pltpu.VMEM((ratio, share, wide), bf16),
        ]
    else:
        entries = standardize_entries(
            alignment_tensor, standardizer_scaling, standardizer_offset
        ).reshape(-1, feats)
        both = jnp.dot(
            entries,
            jnp.concatenate([first_projector, second_projector], axis=1),
            preferred_element_type=f32,
        ).astype(bf16)
        left_own = both[:, :size].reshape(share, rows * size)
        right_own = (
            both[:, size:]
            .reshape(share, ratio, cols, size)
            .transpose(1, 0, 3, 2)
            .reshape(ratio, share, wide)
        )
        sources, extra = (left_own, right_own), []
    flat_grad = couple_delta_adjoint.reshape(-1, CZ)
    smem = pl.BlockSpec(memory_space=pltpu.SMEM)
    hbm = pl.BlockSpec(memory_space=pl.ANY)
    left_panel, right_panel, table, inverse, weight, weight_t, scaled = pl.pallas_call(
        functools.partial(gather_kernel, n_row, n_col, ratio, rows, cols, tile, fused),
        in_specs=[smem, smem, vmem, hbm] + [vmem] * len(sources),
        out_specs=[vmem] * 6 + [hbm],
        out_shape=[
            jax.ShapeDtypeStruct((seqs, rows * size), bf16),
            jax.ShapeDtypeStruct((seqs, wide), bf16),
            jax.ShapeDtypeStruct((2 * CHAINS, LANES), f32),
            jax.ShapeDtypeStruct((rows, LANES), f32),
            jax.ShapeDtypeStruct((blocks * size, inner * CZ), bf16),
            jax.ShapeDtypeStruct((inner * CZ, blocks * size), bf16),
            jax.ShapeDtypeStruct((rows * size, wide), bf16),
        ],
        scratch_shapes=[
            pltpu.VMEM((rows * cols, CZ), bf16),
            pltpu.VMEM((tile * LANES, inner * CZ), bf16),
            pltpu.VMEM((2, tile * size, wide), bf16),
            pltpu.VMEM((size * size, CZ), f32),
            *extra,
            dma((n_col,)), dma((n_col,)), dma((ratio,)), dma((n_col,)),
            dma((n_col, n_row // 2)), dma((n_col,)), dma((2,)), dma, dma((2,)),
        ],
        compiler_params=pltpu.CompilerParams(
            collective_id=0, has_side_effects=True, vmem_limit_bytes=56 * 1024 * 1024
        ),
    )(amino_strand_label, matched_strand_count, final_projector, flat_grad, *sources)

    whole = lambda shape: pl.BlockSpec(shape, lambda g, labels: (0,) * len(shape))
    pair, left_grad, right_grad, weight_part = pl.pallas_call(
        functools.partial(pair_kernel, tile, cols, seqs),
        grid_spec=pltpu.PrefetchScalarGridSpec(
            num_scalar_prefetch=1,
            grid=(steps,),
            in_specs=[
                pl.BlockSpec((seqs, tile * size), lambda g, labels: (0, g)),
                whole((seqs, wide)),
                whole((2 * CHAINS, LANES)),
                pl.BlockSpec((tile, LANES), lambda g, labels: (g, 0)),
                pl.BlockSpec((tile * cols, CZ), lambda g, labels: (g, 0)),
                pl.BlockSpec((tile * size, wide), lambda g, labels: (g, 0)),
                whole((inner * CZ, blocks * size)),
                whole((1, CZ)),
            ],
            out_specs=[
                pl.BlockSpec((tile * cols, CZ), lambda g, labels: (g, 0)),
                pl.BlockSpec((seqs, tile * size), lambda g, labels: (0, g)),
                whole((seqs, wide)),
                whole((size * size, CZ)),
            ],
            scratch_shapes=[
                pltpu.VMEM((CHAINS + 1, seqs, wide), bf16),
                pltpu.VMEM((CHAINS + 1, wide, seqs), bf16),
                pltpu.VMEM((tile * LANES, inner * CZ), bf16),
                pltpu.VMEM((blocks * size, tile * LANES), bf16),
                pltpu.VMEM((tile * size, wide), f32),
                pltpu.VMEM((tile * size, seqs), f32),
                pltpu.VMEM((seqs, wide), f32),
                pltpu.VMEM((blocks * size, inner * CZ), f32),
                pltpu.VMEM((2 * seqs, tile * size), bf16),
            ],
        ),
        out_shape=[
            jax.ShapeDtypeStruct((rows * cols, CZ), bf16),
            jax.ShapeDtypeStruct((seqs, rows * size), bf16),
            jax.ShapeDtypeStruct((seqs, wide), bf16),
            jax.ShapeDtypeStruct((size * size, CZ), bf16),
        ],
        compiler_params=pltpu.CompilerParams(
            dimension_semantics=("arbitrary",), vmem_limit_bytes=56 * 1024 * 1024
        ),
    )(
        amino_strand_label,
        left_panel,
        right_panel,
        table,
        inverse,
        flat_grad,
        scaled,
        weight_t,
        final_offset[None, :],
    )
    pair_update = pair.reshape(rows, cols, CZ)
    many = n_col // n_row
    quarter = size * size // n_row
    piece = quarter // n_col
    adjoint_first_factor, right_sum, weight_total = pl.pallas_call(
        functools.partial(sum_kernel, n_row, n_col, ratio, blocks),
        in_specs=[vmem] * 3,
        out_specs=[vmem] * 3,
        out_shape=[
            jax.ShapeDtypeStruct((share, rows * size), bf16),
            jax.ShapeDtypeStruct((ratio, share, wide), bf16),
            jax.ShapeDtypeStruct((size * size, CZ), f32),
        ],
        scratch_shapes=[
            pltpu.VMEM((n_col, share, rows * size), bf16),
            pltpu.VMEM((n_col // 2, share, wide), bf16),
            pltpu.VMEM((n_col // 2, share, wide), bf16),
            pltpu.VMEM((n_row // 2, many, share, wide), bf16),
            pltpu.VMEM((many, share, wide), bf16),
            pltpu.VMEM((ratio, share, wide), bf16),
            pltpu.VMEM((n_row, quarter, CZ), bf16),
            pltpu.VMEM((quarter, CZ), bf16),
            pltpu.VMEM((n_col, piece, CZ), bf16),
            pltpu.VMEM((piece, CZ), bf16),
            pltpu.VMEM((size * size, CZ), bf16),
            dma((n_col, 2)), dma((n_col, 2)), dma((n_col, 2)),
            dma, dma,
            dma((n_row // 2,)), dma((n_row // 2,)),
            dma((many,)), dma((ratio,)),
            dma((n_row,)), dma((n_row,)),
            dma((n_col,)), dma((n_col,)),
            dma((n_col,)), dma((n_col,)),
            dma((n_row,)), dma((n_row,)),
        ],
        compiler_params=pltpu.CompilerParams(collective_id=1, has_side_effects=True),
    )(
        left_grad.reshape(n_col, share, rows * size),
        right_grad.reshape(n_col, share, wide),
        weight_part,
    )
    grad_right = (
        right_sum.reshape(ratio, share, size, cols)
        .transpose(1, 0, 3, 2)
        .reshape(share, rows * size)
    )
    return (pair_update, adjoint_first_factor, grad_right, weight_total)


def solution(mesh):
    in_specs = (
        P(("parts", "col"), "row", None),
        P(),
        P(),
        P(),
        P(),
        P(),
        P(),
        P("parts"),
        P("parts", None),
        P(("parts", "row"), "col", None),
    )
    out_specs = (
        P(("parts", "row"), "col", None),
        P(("parts", "col"), "row"),
        P(("parts", "col"), "row"),
        P("parts", None),
    )
    return jax.shard_map(shards, mesh=mesh, in_specs=in_specs, out_specs=out_specs, check_vma=False)
```

time: 96.6 us -> 84.7 us (0.88)
  other arithmetic: 3.85 us -> 0 us
  local copies, waits for them, and re-layouts: 10.8 us -> 7.54 us
  Pallas kernels: 78.9 us -> 75.8 us
  matrix products: 1.52 us -> 0 us
    unnamed x22 -> x3, local copies, waits for them, and re-layouts: 0.74 us -> 4.89 us
    reshape x6 -> x0, local copies, waits for them, and re-layouts: 3.55 us -> none  [the longest x3 1.28 us: shards(): right_own = both[:, size:].reshape(share, ratio, cols, size).transpose(1,...]
    reduce_sum x2 -> x0, other arithmetic: 2.25 us -> none  [the longest x1 1.61 us: standardize_entries(): jnp.mean(incoming_entries, axis=-1, keepdims=True)]
    pallas_call x1, Pallas kernels: 22 us -> 20 us  [shards(): pl.pallas_call(functools.partial(pair_kernel, tile, cols, seqs), grid_spe...]
    convert_element_type x2 -> x0, other arithmetic: 1.58 us -> none  [the longest x1 0.86 us: shards(): row_labels.astype(f32)]
    dot_general x3 -> x0, matrix products: 1.52 us -> none  [the longest x1 0.87 us: shards(): jnp.dot(matched_strand_count.astype(f32), col_hot.T, precision=lax.Precis...]
    transpose x1 -> x0, local copies, waits for them, and re-layouts: 1.2 us -> none  [shards(): weight_total.reshape(inner, blocks, size, CZ).transpose(2, 1, 0, 3)]
    pallas_call x2, Pallas kernels: 56.9 us -> 55.8 us  [the longest x1 30.4 us: shards(): pl.pallas_call(functools.partial(sum_kernel, n_row, n_col, ratio, blocks)...]
where the time goes in v3:
time: 84.7 us; the launch traced here: 84 us
  Pallas kernels  75.8 us (89%)
  local copies, waits for them, and re-layouts  7.54 us (9%)
    pallas_call x1, Pallas kernels, shards(): pl.pallas_call(functools.partial(sum_kernel, n_row, n_col, ratio, blocks)...  30.4 us
    pallas_call x1, Pallas kernels, shards(): pl.pallas_call(functools.partial(gather_kernel, n_row, n_col, ratio, rows...  25.4 us
    pallas_call x1, Pallas kernels, shards(): pl.pallas_call(functools.partial(pair_kernel, tile, cols, seqs), grid_spe...  20 us
    unnamed x3, local copies, waits for them, and re-layouts  4.89 us

profile of v3, /device:TPU:1, one launch (start us, length us, event | category | flops | bytes accessed | tf_op | source)
XLA Modules:
  0.0 84.0 jit_solution(9131703410618580873)
XLA Ops:
  0.6 1.5 %copy.16.refs_7_ = bf16[256,32]{1,0:T(8,128)(2,1)} copy(bf16[256,32]{0,1:T(8,128)(2,1)} %param.13) | data formatting | bytes 32768 | tf_op args[3]
  2.1 25.4 %shard_map.129 = (bf16[128,2048]{1,0:T(8,128)(2,1)}, bf16[128,2048]{1,0:T(8,128)(2,1)}, f32[16,128]{1,0:T(8,128)}, f32[64,128]{1,0:T(8,128)}, bf16[512,256]{1,0:...) custom-call(s32[256]{0:T(256)} %labels_ref.1, s32[8,8]{1,0:T(8,128)} %refs_1_.1, ...), custom_call_target="tpu_custom_call" | custom-call | tf_op jit(solution)/shard_map/pallas_call | solution.py:682
  27.5 20.0 %shard_map.130 = (bf16[4096,128]{1,0:T(8,128)(2,1)}, bf16[128,2048]{1,0:T(8,128)(2,1)}, bf16[128,2048]{1,0:T(8,128)(2,1)}, bf16[1024,128]{1,0:T(8,128)(2,1)}) custom-call(s32[256]{0:T(256)} %labels_ref.1, bf16[128,2048]{1,0:T(8,128)(2,1)} %get-tuple-element.17.left_ref, bf16[128,2048]{1,0:T(8,128)(2,1)} %get-tuple-element.18.right_ref, ...), custom_call_target="tpu_custom_call" | custom-call | tf_op jit(solution)/shard_map/pallas_call | solution.py:710
  47.5 30.4 %shard_map.131 = (bf16[32,2048]{1,0:T(8,128)(2,1)}, bf16[1,32,2048]{2,1,0:T(8,128)(2,1)}, f32[1024,128]{1,0:T(8,128)}) custom-call(bf16[4,32,2048]{2,1,0:T(8,128)(2,1)} %bitcast.16, bf16[4,32,2048]{2,1,0:T(8,128)(2,1)} %bitcast.17, bf16[1024,128]{1,0:T(8,128)(2,1)} %get-tuple-element.26.weight_ref), custom_call_target="tpu_custom_call" | custom-call | tf_op jit(solution)/shard_map/pallas_call | solution.py:767
  77.9 1.2 %reshape.30 = bf16[1,32,32,64]{3,2,1,0:T(8,128)(2,1)S(1)} reshape(bf16[1,32,2048]{2,1,0:T(8,128)(2,1)} %get-tuple-element.28) | data formatting | bytes 262144 | tf_op jit(solution)/shard_map/reshape | solution.py:804
  79.1 0.3 copy.17
  79.4 1.2 %reshape.31 = bf16[32,2048]{1,0:T(8,128)(2,1)} reshape(bf16[32,1,64,32]{3,2,0,1:T(8,128)(2,1)S(1)} %bitcast.15) | data formatting | bytes 262144 | tf_op jit(solution)/shard_map/reshape | solution.py:806
  80.6 1.6 %copy.20 = bf16[32,2048]{1,0:T(8,128)(2,1)} copy(bf16[32,2048]{1,0:T(8,128)(2,1)} %get-tuple-element.35) | data formatting | bytes 262144
  82.1 1.9 %copy.21 = f32[1024,128]{1,0:T(8,128)} copy(f32[1024,128]{1,0:T(8,128)} %get-tuple-element.37) | data formatting | bytes 1048576

commit v4 on v3

--- a/solution.py
+++ b/solution.py
@@ -128,8 +128,10 @@
         right_own[0, low:, lanes] = jnp.where(near, pltpu.roll(even, rows, 1), odd).astype(bf16)
     yield
     fold = LANES // size
-    first = jnp.concatenate([first_ref[...]] * fold, axis=1)
-    line_ref[...] = jnp.dot(normed_ref[...], first, preferred_element_type=f32)
+    first = jnp.concatenate([first_ref[...]] * fold, axis=0)
+    line_ref[...] = lax.dot_general(
+        normed_ref[...], first, (((1,), (1,)), ((), ())), preferred_element_type=f32
+    )
     place = lax.broadcasted_iota(jnp.int32, (share, LANES), 1) // size
     for g in range(rows // fold):
         total = line_ref[pl.ds(g * fold, share, stride=rows), :]
@@ -319,141 +321,33 @@
             twin_copy(block(right_out, peer), peer).wait_send()
 
 
-def pair_kernel(
-    tile, cols, seqs,
-    labels_ref,
-    left_ref, right_ref, table_ref, inverse_ref, grad_ref, scaled, weight_t_ref, bias_ref,
-    pair_ref, left_grad_ref, right_grad_ref, weight_grad_ref,
-    kept, kept_t, spread, outer, acc, left_acc, right_acc, weight_acc, slots,
+def core_kernel(
+    n_row, n_col, ratio, rows, cols, tile,
+    labels_ref, left_in_ref, right_in_ref, table_ref, inverse_ref, grad_hbm, scaled_hbm,
+    weight_t_ref, bias_ref,
+    pair_out, left_out, right_out, weight_out,
+    grad, scaled, spread, outer, outer_more, left_more, slots, left_tiles, inverses, label_lanes, right_t, keep, keep_t,
+    weight_acc, left_ref, right_ref, weight_ref, local_sem,
+    left_in, right_twin, right_half, right_mid, right_sum,
+    weight_twin, weight_half, weight_mid, weight_sum, weight_in, weight_part,
+    up_send, down_send, left_recv, twin_send, twin_recv, mid_send, mid_recv,
+    right_send, right_recv, own_sem,
+    w1_send, w1_recv, w2_send, w2_recv, w3_send, w3_recv, around_send, hop_send, last_send,
+    all_recv,
 ):
-    step = pl.program_id(0)
+    f32, bf16 = jnp.float32, jnp.bfloat16
     size = PROJECTED_SIZE
     inner = LANES // cols
     blocks = size // inner
+    steps = rows // tile
+    span = tile * size
+    seqs = left_in_ref.shape[0]
+    share = seqs // n_col
     width = 2 * LANES if blocks % 2 == 0 else LANES
-    f32, bf16 = jnp.float32, jnp.bfloat16
-    seq = lax.broadcasted_iota(jnp.int32, (seqs, LANES), 0).astype(f32)
-
-    @pl.when(step == 0)
-    def _():
-        spread[...] = jnp.zeros_like(spread)
-        right_acc[...] = jnp.zeros_like(right_acc)
-        weight_acc[...] = jnp.zeros_like(weight_acc)
-
-        def fill(chain, carry):
-            keep = jnp.where(seq < table_ref[pl.ds(chain, 1), :], 1.0, 0.0).astype(bf16)
-            for b in range(blocks):
-                lanes = slice(b * LANES, (b + 1) * LANES)
-                piece = right_ref[:, lanes] * keep
-                kept[chain, :, lanes] = piece
-                kept_t[chain, lanes, :] = piece.T
-            return carry
-
-        extent = pl.num_programs(0) * tile
-        first = lax.axis_index("row") * extent
-        lax.fori_loop(labels_ref[first], labels_ref[first + extent - 1] + 2, fill, 0)
-
-    for i in range(tile):
-        grad = grad_ref[i * cols : (i + 1) * cols, :]
-        for e in range(inner):
-            spread[i * LANES + e * cols : i * LANES + (e + 1) * cols, e * CZ : (e + 1) * CZ] = grad
-    inverse = [inverse_ref[i : i + 1, :] for i in range(tile)]
-    offset = lax.axis_index("row") * (pl.num_programs(0) * tile)
-    label = [labels_ref[offset + step * tile + i] for i in range(tile)]
-    place = lax.broadcasted_iota(jnp.int32, (1, tile * size), 1) // size
-    lane = jnp.zeros((1, tile * size), jnp.int32)
-    for i in range(tile):
-        lane = jnp.where(place == i, label[i], lane)
-    low, high = label[0], label[tile - 1]
-
-    def chain_pair(first, chain):
-        left = left_ref[...]
-        for k in range(2):
-            slots[k * seqs : (k + 1) * seqs, :] = left * jnp.where(
-                lane == chain + k, 1.0, 0.0
-            ).astype(bf16)
-        both = slots[...]
-        both_t = both.T
-        keep = [seq < table_ref[pl.ds(chain + k, 1), :] for k in range(2)]
-        for start in range(0, blocks * LANES, width):
-            lanes = slice(start, start + width)
-            right = kept[pl.ds(chain, 2), :, lanes].reshape(2 * seqs, width)
-            prod = jnp.dot(both_t, right, preferred_element_type=f32)
-            if first:
-                acc[:, lanes] = prod
-            else:
-                acc[:, lanes] += prod
-            out = jnp.dot(both, scaled[:, lanes], preferred_element_type=f32)
-            for b in range(width // LANES):
-                part = slice(b * LANES, (b + 1) * LANES)
-                right_acc[:, start + b * LANES : start + (b + 1) * LANES] += jnp.where(
-                    keep[0], out[:seqs, part], 0.0
-                ) + jnp.where(keep[1], out[seqs:, part], 0.0)
-        right_t = jnp.concatenate([kept_t[chain], kept_t[chain + 1]], axis=1)
-        out = jnp.dot(scaled[...], right_t, preferred_element_type=f32)
-        for i in range(tile):
-            rows = slice(i * size, (i + 1) * size)
-            part = jnp.where(label[i] == chain, out[rows, :seqs], 0.0) + jnp.where(
-                label[i] == chain + 1, out[rows, seqs:], 0.0
-            )
-            if first:
-                left_acc[rows, :] = part
-            else:
-                left_acc[rows, :] += part
-
-    chain_pair(True, low)
-
-    def more(p, carry):
-        chain_pair(False, low + 2 * p)
-        return carry
-
-    lax.fori_loop(1, (high - low) // 2 + 1, more, 0)
-    left_grad_ref[...] = left_acc[...].T.astype(bf16)
-    for i in range(tile):
-        for b in range(blocks):
-            outer[b * size : (b + 1) * size, i * LANES : (i + 1) * LANES] = (
-                acc[i * size : (i + 1) * size, b * LANES : (b + 1) * LANES] * inverse[i]
-            ).astype(bf16)
-    group = lax.broadcasted_iota(jnp.int32, (CZ, LANES), 1) // cols
-    for i in range(0, tile, 2):
-        both = jnp.dot(
-            weight_t_ref[...], outer[:, i * LANES : (i + 2) * LANES], preferred_element_type=f32
-        )
-        for k in range(2):
-            lanes = slice(k * LANES, (k + 1) * LANES)
-            total = both[:CZ, lanes]
-            for e in range(1, inner):
-                total = jnp.where(group == e, both[e * CZ : (e + 1) * CZ, lanes], total)
-            turned = total.T
-            pair = turned[:cols]
-            for e in range(1, inner):
-                pair = pair + turned[e * cols : (e + 1) * cols]
-            pair_ref[(i + k) * cols : (i + k + 1) * cols, :] = (pair + bias_ref[...]).astype(bf16)
-    weight_acc[...] += jnp.dot(outer[...], spread[...], preferred_element_type=f32)
-
-    @pl.when(step == pl.num_programs(0) - 1)
-    def _():
-        right_grad_ref[...] = right_acc[...].astype(bf16)
-        rows = blocks * size
-        for e in range(inner):
-            weight_grad_ref[e * rows : (e + 1) * rows, :] = weight_acc[
-                :, e * CZ : (e + 1) * CZ
-            ].astype(bf16)
-
-
-def sum_kernel(
-    n_row, n_col, ratio, blocks,
-    left_ref, right_ref, weight_ref,
-    left_out, right_out, weight_out,
-    left_in, right_twin, right_half, right_mid, right_sum, right_in,
-    weight_mid, weight_sum, weight_in, weight_part, weight_all,
-    up_send, down_send, left_recv, twin_send, twin_recv, mid_send, mid_recv,
-    right_send, right_recv,
-    w1_send, w1_recv, w2_send, w2_recv, w3_send, w3_recv, w4_send, w4_recv,
-):
-    f32, bf16 = jnp.float32, jnp.bfloat16
+    chunks = blocks * LANES // width
+    extras = outer_more.shape[0] - 1
     row, col = lax.axis_index("row"), lax.axis_index("col")
-    greet(n_row, n_col, row * n_col + col)()
+    ready = greet(n_row, n_col, row * n_col + col)
     chips = n_row // 2
     chip, side = row // 2, row % 2
     twin = row + 1 - 2 * side
@@ -466,17 +360,21 @@
     owner, slot = col // ratio, col % ratio
     rows_of = lambda index, extent: pl.ds(pl.multiple_of(index * extent, extent), extent)
     mine = side * chips + chip
-
-    def w1_copy(off):
-        peer = (row + off) % n_row
-        return to(
-            weight_ref.at[rows_of(peer, quarter)], weight_mid.at[row], w1_send.at[off],
-            w1_recv.at[row], peer, col,
-        )
-
+    add = lambda *terms: functools.reduce(lambda a, b: a + b, [t.astype(f32) for t in terms])
+
+    w1_copy = to(
+        weight_ref.at[rows_of(1 - side, chips * quarter)], weight_twin, w1_send, w1_recv, twin, col
+    )
     twin_copy = to(
         right_ref.at[rows_of(1 - side, half)], right_twin, twin_send, twin_recv, twin, col
     )
+
+    def w2_copy(off):
+        peer = (chip + off) % chips
+        return to(
+            weight_half.at[rows_of(peer, quarter)], weight_mid.at[chip], w2_send.at[off],
+            w2_recv.at[chip], 2 * peer + side, col,
+        )
 
     def mid_copy(off):
         peer = (chip + off) % chips
@@ -487,7 +385,7 @@
 
     def right_copy(b):
         return to(
-            right_sum.at[b], right_in.at[slot], right_send.at[b], right_recv.at[slot],
+            right_sum.at[b], right_out.at[slot], right_send.at[b], right_recv.at[slot],
             owner, mine * many + b,
         )
 
@@ -506,117 +404,408 @@
         for on, copy in left_copies(d, h):
             pl.when(on)(copy.start)
 
-    def w2_copy(off):
-        peer = (col + off) % n_col
-        return to(
-            weight_sum.at[rows_of(peer, piece)], weight_in.at[col], w2_send.at[off],
-            w2_recv.at[col], row, peer,
-        )
-
     def w3_copy(off):
         peer = (col + off) % n_col
         return to(
-            weight_part, weight_all.at[rows_of(row * n_col + col, piece)], w3_send.at[off],
+            weight_sum.at[rows_of(peer, piece)], weight_in.at[col], w3_send.at[off],
             w3_recv.at[col], row, peer,
         )
 
-    def w4_copy(off):
-        peer = (row + off) % n_row
-        own = weight_all.at[rows_of(row, quarter)]
-        return to(own, own, w4_send.at[off], w4_recv.at[row], peer, col)
-
-    for off in range(1, n_row):
-        w1_copy(off).start()
-    twin_copy.start()
-    for h in range(parts):
-        left_start(1, h)
-    left_start(2, 0)
-
-    arrived(right_twin, twin_recv)
-    right_half[...] = (
-        right_ref[rows_of(side, half)].astype(f32) + right_twin[...].astype(f32)
-    ).astype(bf16)
-    for off in range(1, chips):
-        mid_copy(off).start()
-
-    own = weight_ref[rows_of(row, quarter), :].astype(f32)
-    for off in range(1, n_row):
-        peer = (row + off) % n_row
-        arrived(weight_mid.at[peer], w1_recv.at[peer])
-        own = own + weight_mid[peer].astype(f32)
-    weight_sum[...] = own.astype(bf16)
-    for off in range(1, n_col):
-        w2_copy(off).start()
-    for h in range(1, parts):
-        left_start(2, h)
-
-    total = right_half[rows_of(chip, many)].astype(f32)
-    for off in range(1, chips):
+    def cell(group, index):
+        return weight_out.at[rows_of(group * n_col + index, piece)]
+
+    def spread_copy(send, group, index, to_row, to_col, source=None):
+        there = cell(group, index)
+        return to(
+            there if source is None else source, there, send, all_recv.at[group, index],
+            to_row, to_col,
+        )
+
+    def around_copy(off):
+        return spread_copy(around_send.at[off], mine, col, row, (col + off) % n_col, weight_part)
+
+    def hop_copy(index, off, source=None):
         peer = (chip + off) % chips
-        arrived(right_mid.at[peer], mid_recv.at[peer])
-        total = total + right_mid[peer].astype(f32)
-    right_sum[...] = total.astype(bf16)
-    for b in range(many):
-        here = jnp.logical_and(owner == row, mine * many + b == col)
-        pl.when(jnp.logical_not(here))(right_copy(b).start)
-        pl.when(here)(
-            pltpu.make_async_copy(right_sum.at[b], right_in.at[slot], right_recv.at[slot]).start
-        )
-
-    own = weight_sum[rows_of(col, piece), :].astype(f32)
-    for off in range(1, n_col):
-        peer = (col + off) % n_col
-        arrived(weight_in.at[peer], w2_recv.at[peer])
-        own = own + weight_in[peer].astype(f32)
-    weight_part[...] = own.astype(bf16)
-    weight_all[rows_of(row * n_col + col, piece), :] = own.astype(bf16)
-    for off in range(1, n_col):
-        w3_copy(off).start()
-    for d in range(3, n_col):
-        for h in range(parts):
-            left_start(d, h)
-
-    for off in range(1, n_col):
-        peer = (col + off) % n_col
-        arrived(weight_all.at[rows_of(row * n_col + peer, piece)], w3_recv.at[peer])
-    for off in range(1, n_row):
-        w4_copy(off).start()
-
-    total = left_ref[col].astype(f32)
-    for off in range(1, n_col):
-        peer = (col + off) % n_col
-        for h in range(parts):
-            arrived(left_in.at[peer, :, h * part : (h + 1) * part], left_recv.at[peer, h])
-        total = total + left_in[peer].astype(f32)
-    left_out[...] = total.astype(bf16)
-    for t in range(ratio):
-        arrived(right_in.at[t], right_recv.at[t])
-        right_out[t] = right_in[t]
-    for off in range(1, n_row):
-        peer = (row + off) % n_row
-        arrived(weight_all.at[rows_of(peer, quarter)], w4_recv.at[peer])
+        return spread_copy(hop_send.at[index, off], mine, index, 2 * peer + side, col, source)
+
+    def last_copy(group, index, source=None):
+        return spread_copy(last_send.at[group, index], group, index, twin, col, source)
+
+    def group_of(off):
+        return side * chips + (chip + off) % chips
+
+    def here(b):
+        return jnp.logical_and(owner == row, mine * many + b == col)
+
+
+    own_piece = pltpu.make_async_copy(weight_part, cell(mine, col), own_sem)
+
+    def after_left_extra():
+        arrived(weight_twin, w1_recv)
+        weight_half[...] = add(
+            weight_ref[rows_of(side, chips * quarter), :], weight_twin[...]
+        ).astype(bf16)
+        for off in range(1, chips):
+            w2_copy(off).start()
+
+    def first_left():
+        for d in range(1, n_col):
+            left_start(d, 0)
+
+    def after_left():
+        total = weight_half[rows_of(chip, quarter), :].astype(f32)
+        for off in range(1, chips):
+            peer = (chip + off) % chips
+            arrived(weight_mid.at[peer], w2_recv.at[peer])
+            total = add(total, weight_mid[peer])
+        weight_sum[...] = total.astype(bf16)
+        for off in range(1, n_col):
+            w3_copy(off).start()
+
+    def during_right():
+        total = weight_sum[rows_of(col, piece), :].astype(f32)
+        for off in range(1, n_col):
+            peer = (col + off) % n_col
+            arrived(weight_in.at[peer], w3_recv.at[peer])
+            total = add(total, weight_in[peer])
+        weight_part[...] = total.astype(bf16)
+        own_piece.start()
+        for off in range(1, n_col):
+            around_copy(off).start()
+        for off in range(1, chips):
+            hop_copy(col, off, weight_part).start()
+        last_copy(mine, col, weight_part).start()
+        for h in range(1, parts):
+            for d in range(1, n_col):
+                left_start(d, h)
+
+    def after_right():
+        twin_copy.start()
+
+    def pair_first():
+        arrived(right_twin, twin_recv)
+        right_half[...] = add(right_ref[rows_of(side, half)], right_twin[...]).astype(bf16)
+        for off in range(1, chips):
+            mid_copy(off).start()
+
+    def pair_second():
+        for off in range(1, n_col):
+            peer = (col + off) % n_col
+            arrived(cell(mine, peer), all_recv.at[mine, peer])
+            for hop in range(1, chips):
+                hop_copy(peer, hop).start()
+            last_copy(mine, peer).start()
+
+    def pair_third():
+        total = right_half[rows_of(chip, many)].astype(f32)
+        for off in range(1, chips):
+            peer = (chip + off) % chips
+            arrived(right_mid.at[peer], mid_recv.at[peer])
+            total = add(total, right_mid[peer])
+        right_sum[...] = total.astype(bf16)
+        for b in range(many):
+            pl.when(jnp.logical_not(here(b)))(right_copy(b).start)
+            own = pltpu.make_async_copy(right_sum.at[b], right_out.at[slot], right_recv.at[slot])
+            pl.when(here(b))(own.start)
+
+    def finish():
+        for off in range(n_col):
+            peer = (col + off) % n_col
+            for hop in range(1, chips):
+                arrived(cell(group_of(hop), peer), all_recv.at[group_of(hop), peer])
+                last_copy(group_of(hop), peer).start()
+
+        total = left_ref[col].astype(f32)
+        for off in range(1, n_col):
+            peer = (col + off) % n_col
+            for h in range(parts):
+                arrived(left_in.at[peer, :, h * part : (h + 1) * part], left_recv.at[peer, h])
+            total = add(total, left_in[peer])
+        left_out[...] = total.astype(bf16)
+        for t in range(ratio):
+            arrived(right_out.at[t], right_recv.at[t])
+        for off in range(n_col):
+            peer = (col + off) % n_col
+            for other in range(chips):
+                group = (1 - side) * chips + other
+                arrived(cell(group, peer), all_recv.at[group, peer])
+
+        own_piece.wait()
+        w1_copy.wait_send()
+        twin_copy.wait_send()
+        for off in range(1, chips):
+            w2_copy(off).wait_send()
+            mid_copy(off).wait_send()
+        for off in range(1, n_col):
+            w3_copy(off).wait_send()
+            around_copy(off).wait_send()
+            for h in range(parts):
+                for on, copy in left_copies(off, h):
+                    pl.when(on)(copy.wait_send)
+        for index in range(n_col):
+            for off in range(1, chips):
+                hop_copy(index, off).wait_send()
+            for off in range(chips):
+                last_copy(group_of(off), index).wait_send()
+        for b in range(many):
+            pl.when(jnp.logical_not(here(b)))(right_copy(b).wait_send)
+    grad_copies = [
+        pltpu.make_async_copy(
+            grad_hbm.at[pl.ds(t * tile * cols, tile * cols)], grad.at[t], local_sem.at[0, t]
+        )
+        for t in range(steps)
+    ]
+    scaled_copies = [
+        pltpu.make_async_copy(
+            scaled_hbm.at[pl.ds(t * span, span)], scaled.at[t], local_sem.at[1, t]
+        )
+        for t in range(steps)
+    ]
+    for copy in grad_copies + scaled_copies:
+        copy.start()
+
+    place_of = lax.broadcasted_iota(jnp.int32, (tile, span), 1) // size
+    seq = lax.broadcasted_iota(jnp.int32, (seqs, LANES), 0).astype(f32)
+    for chain in range(keep.shape[0]):
+        kept = jnp.where(seq < table_ref[chain : chain + 1, :], 1.0, 0.0)
+        keep[chain] = kept.astype(bf16)
+        keep_t[chain] = kept.T.astype(bf16)
+    for b in range(blocks):
+        right_t[b * LANES : (b + 1) * LANES, :] = right_in_ref[:, b * LANES : (b + 1) * LANES].T
+    for t in range(steps):
+        left_tiles[t] = left_in_ref[:, t * span : (t + 1) * span]
+        inverses[t] = inverse_ref[t * tile : (t + 1) * tile, :]
+        line = jnp.zeros((tile, span), jnp.int32)
+        for i in range(tile):
+            line = jnp.where(place_of == i, labels_ref[row * rows + t * tile + i], line)
+        label_lanes[t] = line
+    spread[...] = jnp.zeros_like(spread)
+    weight_acc[...] = jnp.zeros_like(weight_acc)
+    outer_more[0] = jnp.zeros(outer_more.shape[1:], bf16)
+    left_more[0] = jnp.zeros(left_more.shape[1:], f32)
+
+    offset = row * rows
+    label_of = lambda t, i: labels_ref[offset + t * tile + i]
+    lows = [label_of(t, 0) for t in range(steps)]
+    more = [lax.div(label_of(t, tile - 1) - lows[t], jnp.int32(2)) for t in range(steps)]
+    ends, end = [], 0
+    for t in range(steps):
+        end = end + more[t]
+        ends.append(end)
+
+    flag = lambda test: test.astype(jnp.int32)
+
+    def extra_of(u):
+        t = sum([flag(ends[k] <= u) for k in range(steps)])
+        chain = flag(t == steps) * CHAINS
+        for k in range(steps):
+            chain = chain + flag(t == k) * (lows[k] + 2 * (u - ends[k] + more[k] + 1))
+        return t - flag(t == steps), chain
+
+    def slot_of(t):
+        return sum([flag(t == k) * flag(more[k] > 0) * ends[k] for k in range(steps)])
+
+    def same_of(u):
+        return flag(extra_of(u)[0] == extra_of(u - 1)[0]).astype(f32)
+
+    def build(t, chain, place):
+        lane = label_lanes[t][:1]
+        left = left_tiles[t]
+        for k in range(2):
+            slots[place, k * seqs : (k + 1) * seqs, :] = left * jnp.where(
+                lane == chain + k, 1.0, 0.0
+            ).astype(bf16)
+        return slots[place]
+
+    def forward(t, chain, place, store):
+        both_t = build(t, chain, place).T
+        inverse = inverses[t]
+        kept = [jnp.concatenate([keep[chain + k]] * (width // LANES), axis=1) for k in range(2)]
+        for c in range(chunks):
+            lanes = slice(c * width, (c + 1) * width)
+            right = right_in_ref[:, lanes]
+            right = jnp.concatenate([right * kept[0], right * kept[1]], axis=0)
+            prod = jnp.dot(both_t, right, preferred_element_type=f32)
+            for i in range(tile):
+                for b in range(width // LANES):
+                    first = (c * (width // LANES) + b) * size
+                    store(
+                        slice(first, first + size), slice(i * LANES, (i + 1) * LANES),
+                        (
+                            prod[i * size : (i + 1) * size, b * LANES : (b + 1) * LANES]
+                            * inverse[i : i + 1]
+                        ).astype(bf16),
+                    )
+
+    def forward_more(u, carry):
+        t, chain = extra_of(u)
+        same = jnp.full((size, LANES), same_of(u), f32).astype(bf16)
+
+        def store(where, lanes, value):
+            outer_more[u + 1, where, lanes] = value + outer_more[u, where, lanes] * same
+
+        forward(t, chain, steps + u, store)
+        return carry
+
+    lax.fori_loop(0, extras, forward_more, 0)
+    for copy in grad_copies:
+        copy.wait()
+
+    def forward_main(t, carry):
+        slot = slot_of(t)
+
+        def store(where, lanes, value):
+            outer[t, where, lanes] = value + outer_more[slot, where, lanes]
+
+        forward(t, label_of(t, 0), t, store)
+        for i in range(tile):
+            part = grad[t, i * cols : (i + 1) * cols, :]
+            for e in range(inner):
+                spread[i * LANES + e * cols : i * LANES + (e + 1) * cols, e * CZ : (e + 1) * CZ] = (
+                    part
+                )
+        weight_acc[...] += jnp.dot(outer[t], spread[...], preferred_element_type=f32)
+        return carry
+
+    lax.fori_loop(0, steps, forward_main, 0)
+    extent = blocks * size
+    for e in range(inner):
+        weight_ref[e * extent : (e + 1) * extent, :] = weight_acc[
+            :, e * CZ : (e + 1) * CZ
+        ].astype(bf16)
+    ready()
+    w1_copy.start()
+    for copy in scaled_copies:
+        copy.wait()
+
+    def left_part(t, chain):
+        tall = jnp.zeros((span, 2 * seqs), f32)
+        for c in range(chunks):
+            lanes = slice(c * width, (c + 1) * width)
+            kept = [
+                jnp.concatenate([keep_t[chain + k]] * (width // LANES), axis=0) for k in range(2)
+            ]
+            right = right_t[lanes, :]
+            right = jnp.concatenate([right * kept[0], right * kept[1]], axis=1)
+            tall = tall + jnp.dot(scaled[t, :, lanes], right, preferred_element_type=f32)
+        turned = tall.T
+        lane = label_lanes[t][:1]
+        return jnp.where(lane == chain, turned[:seqs], 0.0) + jnp.where(
+            lane == chain + 1, turned[seqs:], 0.0
+        )
+
+    def left_extra(u, carry):
+        t, chain = extra_of(u)
+        left_more[u + 1] = left_part(t, chain) + left_more[u] * same_of(u)
+        return carry
+
+    lax.fori_loop(0, extras, left_extra, 0)
+    after_left_extra()
+
+    def left_main(t, carry):
+        slot = slot_of(t)
+        turned = left_part(t, label_of(t, 0)) + left_more[slot]
+        lanes = pl.ds(pl.multiple_of(t * span, span), span)
+        for q in range(n_col):
+            left_ref[q, :, lanes] = turned[q * share : (q + 1) * share].astype(bf16)
+        pl.when(t == steps // parts - 1)(first_left)
+        return carry
+
+    lax.fori_loop(0, steps, left_main, 0)
+    after_left()
+    pairs = [(t, label_of(t, 0), t) for t in range(steps)]
+    for u in range(extras):
+        pairs.append((*extra_of(jnp.int32(u)), steps + u))
+
+    def right_main(c, carry):
+        lanes = pl.ds(pl.multiple_of(c * width, width), width)
+        total = [jnp.zeros((seqs, LANES), f32) for _ in range(width // LANES)]
+        for t, chain, place in pairs:
+            out = jnp.dot(slots[place], scaled[t, :, lanes], preferred_element_type=f32)
+            kept = [seq < table_ref[pl.ds(chain + k, 1), :] for k in range(2)]
+            for b in range(width // LANES):
+                part = slice(b * LANES, (b + 1) * LANES)
+                total[b] = total[b] + (
+                    jnp.where(kept[0], out[:seqs, part], 0.0)
+                    + jnp.where(kept[1], out[seqs:, part], 0.0)
+                )
+        whole = jnp.concatenate(total, axis=1)
+        for q in range(n_col):
+            right_ref[q, :, lanes] = whole[q * share : (q + 1) * share].astype(bf16)
+        pl.when(c == chunks * 3 // 4)(during_right)
+        return carry
+
+    lax.fori_loop(0, chunks, right_main, 0)
+    after_right()
+    group = lax.broadcasted_iota(jnp.int32, (CZ, LANES), 1) // cols
+
+    def pairs_of(t, carry):
+        for i in range(0, tile, 2):
+            both = jnp.dot(
+                weight_t_ref[...], outer[t, :, i * LANES : (i + 2) * LANES],
+                preferred_element_type=f32,
+            )
+            for k in range(2):
+                lanes = slice(k * LANES, (k + 1) * LANES)
+                total = both[:CZ, lanes]
+                for e in range(1, inner):
+                    total = jnp.where(group == e, both[e * CZ : (e + 1) * CZ, lanes], total)
+                turned = total.T
+                pair = turned[:cols]
+                for e in range(1, inner):
+                    pair = pair + turned[e * cols : (e + 1) * cols]
+                first = pl.multiple_of((t * tile + i + k) * cols, cols)
+                pair_out[pl.ds(first, cols), :] = (pair + bias_ref[...]).astype(bf16)
+        pl.when(t == min(1, steps - 1))(pair_first)
+        pl.when(t == steps // 2)(pair_second)
+        pl.when(t == steps - 1)(pair_third)
+        return carry
+
+    lax.fori_loop(0, steps, pairs_of, 0)
+    finish()
+
+
+def finish_kernel(fused, blocks, left_ref, right_ref, weight_ref, *refs):
+    f32, bf16 = jnp.float32, jnp.bfloat16
     size = PROJECTED_SIZE
+    left_out, right_out, weight_out = refs[:3]
+    left_out[...] = left_ref[...]
     for g in range(size):
         e = (g % blocks) * (size // blocks) + g // blocks
-        weight_out[pl.ds(e, size, stride=size), :] = weight_all[
+        weight_out[pl.ds(e, size, stride=size), :] = weight_ref[
             g * size : (g + 1) * size, :
         ].astype(f32) * (1.0 / WINDOW_AMINOS)
-
-    twin_copy.wait_send()
-    for off in range(1, chips):
-        mid_copy(off).wait_send()
-    for off in range(1, n_row):
-        w1_copy(off).wait_send()
-        w4_copy(off).wait_send()
-    for off in range(1, n_col):
-        w2_copy(off).wait_send()
-        w3_copy(off).wait_send()
-        for h in range(parts):
-            for on, copy in left_copies(off, h):
-                pl.when(on)(copy.wait_send)
-    for b in range(many):
-        here = jnp.logical_and(owner == row, mine * many + b == col)
-        pl.when(jnp.logical_not(here))(right_copy(b).wait_send)
+    if not fused:
+        right_out[...] = right_ref[...]
+        return
+    turn_ref, line_ref = refs[3:]
+    share = right_ref.shape[1]
+    low = share // 2
+    rows = line_ref.shape[0] // share
+    near = lax.broadcasted_iota(jnp.int32, (low, LANES), 1) < rows
+    for b in range(size // 2):
+        lanes = slice(b * LANES, (b + 1) * LANES)
+        above = right_ref[0, :low, lanes].astype(f32)
+        below = right_ref[0, low:, lanes].astype(f32)
+        turn_ref[pl.ds(2 * b, low, stride=size), :] = jnp.where(
+            near, above, pltpu.roll(below, rows, 1)
+        )
+        turn_ref[pl.ds(2 * b + 1, low, stride=size), :] = jnp.where(
+            near, pltpu.roll(above, rows, 1), below
+        )
+    fold = LANES // size
+    for p in range(low):
+        turned = jnp.concatenate([turn_ref[p * size : (p + 1) * size, :]] * fold, axis=0).T
+        line_ref[p * rows : (p + 1) * rows, :] = turned[:rows]
+        line_ref[(p + low) * rows : (p + low + 1) * rows, :] = turned[rows:]
+    place = lax.broadcasted_iota(jnp.int32, (share, LANES), 1) // size
+    for g in range(rows // fold):
+        total = line_ref[pl.ds(g * fold, share, stride=rows), :]
+        for k in range(1, fold):
+            total = jnp.where(
+                place == k, line_ref[pl.ds(g * fold + k, share, stride=rows), :], total
+            )
+        right_out[:, g * LANES : (g + 1) * LANES] = total.astype(bf16)
 
 
 def shards(
@@ -650,7 +839,7 @@
     if fused:
         sources = (
             alignment_tensor, standardizer_scaling[None, :], standardizer_offset[None, :],
-            first_projector, second_projector.T,
+            first_projector.T, second_projector.T,
         )
         extra = [
             pltpu.VMEM((share * rows, feats), bf16),
@@ -706,48 +895,61 @@
         ),
     )(amino_strand_label, matched_strand_count, final_projector, flat_grad, *sources)
 
-    whole = lambda shape: pl.BlockSpec(shape, lambda g, labels: (0,) * len(shape))
-    pair, left_grad, right_grad, weight_part = pl.pallas_call(
-        functools.partial(pair_kernel, tile, cols, seqs),
-        grid_spec=pltpu.PrefetchScalarGridSpec(
-            num_scalar_prefetch=1,
-            grid=(steps,),
-            in_specs=[
-                pl.BlockSpec((seqs, tile * size), lambda g, labels: (0, g)),
-                whole((seqs, wide)),
-                whole((2 * CHAINS, LANES)),
-                pl.BlockSpec((tile, LANES), lambda g, labels: (g, 0)),
-                pl.BlockSpec((tile * cols, CZ), lambda g, labels: (g, 0)),
-                pl.BlockSpec((tile * size, wide), lambda g, labels: (g, 0)),
-                whole((inner * CZ, blocks * size)),
-                whole((1, CZ)),
-            ],
-            out_specs=[
-                pl.BlockSpec((tile * cols, CZ), lambda g, labels: (g, 0)),
-                pl.BlockSpec((seqs, tile * size), lambda g, labels: (0, g)),
-                whole((seqs, wide)),
-                whole((size * size, CZ)),
-            ],
-            scratch_shapes=[
-                pltpu.VMEM((CHAINS + 1, seqs, wide), bf16),
-                pltpu.VMEM((CHAINS + 1, wide, seqs), bf16),
-                pltpu.VMEM((tile * LANES, inner * CZ), bf16),
-                pltpu.VMEM((blocks * size, tile * LANES), bf16),
-                pltpu.VMEM((tile * size, wide), f32),
-                pltpu.VMEM((tile * size, seqs), f32),
-                pltpu.VMEM((seqs, wide), f32),
-                pltpu.VMEM((blocks * size, inner * CZ), f32),
-                pltpu.VMEM((2 * seqs, tile * size), bf16),
-            ],
-        ),
+    many = n_col // n_row
+    quarter = size * size // n_row
+    piece = quarter // n_col
+    extras = min(CHAINS - 1, rows - 1) // 2
+    pair, left_sum, right_sum, weight_total = pl.pallas_call(
+        functools.partial(core_kernel, n_row, n_col, ratio, rows, cols, tile),
+        in_specs=[smem] + [vmem] * 4 + [hbm] * 2 + [vmem] * 2,
+        out_specs=[vmem] * 4,
         out_shape=[
             jax.ShapeDtypeStruct((rows * cols, CZ), bf16),
-            jax.ShapeDtypeStruct((seqs, rows * size), bf16),
-            jax.ShapeDtypeStruct((seqs, wide), bf16),
+            jax.ShapeDtypeStruct((share, rows * size), bf16),
+            jax.ShapeDtypeStruct((ratio, share, wide), bf16),
             jax.ShapeDtypeStruct((size * size, CZ), bf16),
         ],
+        scratch_shapes=[
+            pltpu.VMEM((steps, tile * cols, CZ), bf16),
+            pltpu.VMEM((steps, tile * size, wide), bf16),
+            pltpu.VMEM((tile * LANES, inner * CZ), bf16),
+            pltpu.VMEM((steps, blocks * size, tile * LANES), bf16),
+            pltpu.VMEM((extras + 1, blocks * size, tile * LANES), bf16),
+            pltpu.VMEM((extras + 1, seqs, tile * size), f32),
+            pltpu.VMEM((steps + extras, 2 * seqs, tile * size), bf16),
+            pltpu.VMEM((steps, seqs, tile * size), bf16),
+            pltpu.VMEM((steps, tile, LANES), f32),
+            pltpu.VMEM((steps, tile, tile * size), jnp.int32),
+            pltpu.VMEM((wide, seqs), bf16),
+            pltpu.VMEM((CHAINS + 2, seqs, LANES), bf16),
+            pltpu.VMEM((CHAINS + 2, LANES, seqs), bf16),
+            pltpu.VMEM((blocks * size, inner * CZ), f32),
+            pltpu.VMEM((n_col, share, rows * size), bf16),
+            pltpu.VMEM((n_col, share, wide), bf16),
+            pltpu.VMEM((size * size, CZ), bf16),
+            dma((2, steps)),
+            pltpu.VMEM((n_col, share, rows * size), bf16),
+            pltpu.VMEM((n_col // 2, share, wide), bf16),
+            pltpu.VMEM((n_col // 2, share, wide), bf16),
+            pltpu.VMEM((n_row // 2, many, share, wide), bf16),
+            pltpu.VMEM((many, share, wide), bf16),
+            pltpu.VMEM((n_row // 2 * quarter, CZ), bf16),
+            pltpu.VMEM((n_row // 2 * quarter, CZ), bf16),
+            pltpu.VMEM((n_row // 2, quarter, CZ), bf16),
+            pltpu.VMEM((quarter, CZ), bf16),
+            pltpu.VMEM((n_col, piece, CZ), bf16),
+            pltpu.VMEM((piece, CZ), bf16),
+            dma((n_col, 2)), dma((n_col, 2)), dma((n_col, 2)),
+            dma, dma,
+            dma((n_row // 2,)), dma((n_row // 2,)),
+            dma((many,)), dma((ratio,)), dma,
+            dma, dma,
+            dma((n_row // 2,)), dma((n_row // 2,)),
+            dma((n_col,)), dma((n_col,)), dma((n_col,)),
+            dma((n_col, n_row // 2)), dma((n_row, n_col)), dma((n_row, n_col)),
+        ],
         compiler_params=pltpu.CompilerParams(
-            dimension_semantics=("arbitrary",), vmem_limit_bytes=56 * 1024 * 1024
+            collective_id=1, has_side_effects=True, vmem_limit_bytes=58 * 1024 * 1024
         ),
     )(
         amino_strand_label,
@@ -761,51 +963,29 @@
         final_offset[None, :],
     )
     pair_update = pair.reshape(rows, cols, CZ)
-    many = n_col // n_row
-    quarter = size * size // n_row
-    piece = quarter // n_col
-    adjoint_first_factor, right_sum, weight_total = pl.pallas_call(
-        functools.partial(sum_kernel, n_row, n_col, ratio, blocks),
+    adjoint_first_factor, grad_right, grad_w_out = pl.pallas_call(
+        functools.partial(finish_kernel, fused, blocks),
         in_specs=[vmem] * 3,
         out_specs=[vmem] * 3,
         out_shape=[
             jax.ShapeDtypeStruct((share, rows * size), bf16),
-            jax.ShapeDtypeStruct((ratio, share, wide), bf16),
+            jax.ShapeDtypeStruct((share, rows * size) if fused else (ratio, share, wide), bf16),
             jax.ShapeDtypeStruct((size * size, CZ), f32),
         ],
         scratch_shapes=[
-            pltpu.VMEM((n_col, share, rows * size), bf16),
-            pltpu.VMEM((n_col // 2, share, wide), bf16),
-            pltpu.VMEM((n_col // 2, share, wide), bf16),
-            pltpu.VMEM((n_row // 2, many, share, wide), bf16),
-            pltpu.VMEM((many, share, wide), bf16),
-            pltpu.VMEM((ratio, share, wide), bf16),
-            pltpu.VMEM((n_row, quarter, CZ), bf16),
-            pltpu.VMEM((quarter, CZ), bf16),
-            pltpu.VMEM((n_col, piece, CZ), bf16),
-            pltpu.VMEM((piece, CZ), bf16),
-            pltpu.VMEM((size * size, CZ), bf16),
-            dma((n_col, 2)), dma((n_col, 2)), dma((n_col, 2)),
-            dma, dma,
-            dma((n_row // 2,)), dma((n_row // 2,)),
-            dma((many,)), dma((ratio,)),
-            dma((n_row,)), dma((n_row,)),
-            dma((n_col,)), dma((n_col,)),
-            dma((n_col,)), dma((n_col,)),
-            dma((n_row,)), dma((n_row,)),
-        ],
-        compiler_params=pltpu.CompilerParams(collective_id=1, has_side_effects=True),
-    )(
-        left_grad.reshape(n_col, share, rows * size),
-        right_grad.reshape(n_col, share, wide),
-        weight_part,
-    )
-    grad_right = (
-        right_sum.reshape(ratio, share, size, cols)
-        .transpose(1, 0, 3, 2)
-        .reshape(share, rows * size)
-    )
-    return (pair_update, adjoint_first_factor, grad_right, weight_total)
+            pltpu.VMEM((share // 2 * size, LANES), f32),
+            pltpu.VMEM((share * rows, LANES), f32),
+        ]
+        if fused
+        else [],
+    )(left_sum, right_sum, weight_total)
+    if not fused:
+        grad_right = (
+            grad_right.reshape(ratio, share, size, cols)
+            .transpose(1, 0, 3, 2)
+            .reshape(share, rows * size)
+        )
+    return (pair_update, adjoint_first_factor, grad_right, grad_w_out)
 
 
 def solution(mesh):

time: 84.7 us -> 73.5 us (0.87)
  Pallas kernels: 75.8 us -> 70.4 us
  local copies, waits for them, and re-layouts: 7.54 us -> 2.26 us
    pallas_call x2, Pallas kernels: 50.4 us -> 44.9 us  [the longest x1 41.2 us: shards(): pl.pallas_call(functools.partial(core_kernel, n_row, n_col, ratio, rows,...]
    reshape x3 -> x0, local copies, waits for them, and re-layouts: 2.65 us -> none  [the longest x2 1.46 us: shards(): right_sum.reshape(ratio, share, size, cols).transpose(1, 0, 3, 2)]
    unnamed x3 -> x1, local copies, waits for them, and re-layouts: 4.89 us -> 2.26 us
where the time goes in v4:
time: 73.5 us; the launch traced here: 73.3 us
  Pallas kernels  70.4 us (96%)
  local copies, waits for them, and re-layouts  2.26 us (3%)
    pallas_call x1, Pallas kernels, shards(): pl.pallas_call(functools.partial(core_kernel, n_row, n_col, ratio, rows,...  41.2 us
    pallas_call x1, Pallas kernels, shards(): pl.pallas_call(functools.partial(gather_kernel, n_row, n_col, ratio, rows...  25.5 us
    pallas_call x1, Pallas kernels, shards(): pl.pallas_call(functools.partial(finish_kernel, fused, blocks), in_specs=...  3.65 us
    unnamed x1, local copies, waits for them, and re-layouts  2.26 us

profile of v4, /device:TPU:1, one launch (start us, length us, event | category | flops | bytes accessed | tf_op | source)
XLA Modules:
  0.0 73.3 jit_solution(7707713037084884143)
XLA Ops:
  0.6 25.5 %shard_map.129 = (bf16[128,2048]{1,0:T(8,128)(2,1)}, bf16[128,2048]{1,0:T(8,128)(2,1)}, f32[16,128]{1,0:T(8,128)}, f32[64,128]{1,0:T(8,128)}, bf16[512,256]{1,0:...) custom-call(s32[256]{0:T(256)} %labels_ref.1, s32[8,8]{1,0:T(8,128)} %refs_1_.1, ...), custom_call_target="tpu_custom_call" | custom-call | tf_op jit(solution)/shard_map/pallas_call | solution.py:871
  26.1 41.2 %shard_map.130 = (bf16[4096,128]{1,0:T(8,128)(2,1)}, bf16[32,2048]{1,0:T(8,128)(2,1)}, bf16[1,32,2048]{2,1,0:T(8,128)(2,1)}, bf16[1024,128]{1,0:T(8,128)(2,1)}) custom-call(s32[256]{0:T(256)} %labels_ref.1, bf16[128,2048]{1,0:T(8,128)(2,1)} %get-tuple-element.17.left_in_ref, bf16[128,2048]{1,0:T(8,128)(2,1)} %get-tuple-element.18.right_in_ref, ...), custom_call_target="tpu_custom_call" | custom-call | tf_op jit(solution)/shard_map/pallas_call | solution.py:902
  67.4 3.7 %shard_map.131 = (bf16[32,2048]{1,0:T(8,128)(2,1)}, bf16[32,2048]{1,0:T(8,128)(2,1)}, f32[1024,128]{1,0:T(8,128)}) custom-call(bf16[32,2048]{1,0:T(8,128)(2,1)} %get-tuple-element.24.left_ref, bf16[1,32,2048]{2,1,0:T(8,128)(2,1)} %get-tuple-element.25.right_ref, bf16[1024,128]{1,0:T(8,128)(2,1)} %get-tuple-element.26.weight_ref), custom_call_target="tpu_custom_call" | custom-call | tf_op jit(solution)/shard_map/pallas_call | solution.py:966
  71.0 2.3 %copy.15 = bf16[64,64,128]{2,1,0:T(8,128)(2,1)} copy(bf16[64,64,128]{2,1,0:T(8,128)(2,1)} %bitcast.9) | data formatting | bytes 2097152

commit v5 on v4

--- a/solution.py
+++ b/solution.py
@@ -57,7 +57,9 @@
     return lambda: pl.semaphore_wait(barrier, peers - 1)
 
 
-def fill_tables(rows, cols, labels_ref, counts_ref, row, col, table_ref, inverse_ref):
+def fill_tables(
+    rows, cols, labels_ref, counts_ref, row, col, table_ref, inverse_ref, over_ref
+):
     f32 = jnp.float32
     inner = LANES // cols
     lane = lax.broadcasted_iota(jnp.int32, (1, LANES), 1) % cols
@@ -71,11 +73,9 @@
             line = jnp.where(label == b, counts_ref[a, b], line)
         table_ref[a : a + 1, :] = line.astype(f32)
 
-    def divide(i, carry):
-        inverse_ref[pl.ds(i, 1), :] = 1.0 / table_ref[pl.ds(labels_ref[row * rows + i], 1), :]
-        return carry
-
-    lax.fori_loop(0, rows, divide, 0)
+    over_ref[...] = 1.0 / jnp.maximum(table_ref[...], 1.0)
+    for i in range(rows):
+        inverse_ref[i : i + 1, :] = over_ref[pl.ds(labels_ref[row * rows + i], 1), :]
 
 
 def fill_weights(blocks, final_ref, wide_ref, weight_ref, weight_t_ref):
@@ -139,215 +139,56 @@
             total = jnp.where(
                 place == k, line_ref[pl.ds(g * fold + k, share, stride=rows), :], total
             )
-        left_own[:, g * LANES : (g + 1) * LANES] = total.astype(bf16)
+        span = left_own.shape[2]
+        lanes = slice(g * LANES % span, g * LANES % span + LANES)
+        left_own[g * LANES // span, :, lanes] = total.astype(bf16)
     yield
 
 
-def gather_kernel(
-    n_row, n_col, ratio, rows, cols, tile, fused, *refs
-):
-    f32, bf16 = jnp.float32, jnp.bfloat16
-    size = PROJECTED_SIZE
-    inner = LANES // cols
-    blocks = size // inner
-    labels_ref, counts_ref, final_ref, grad_ref = refs[:4]
-    count = 9 if fused else 6
-    source_refs = refs[4:count]
-    left_out, right_out, table_ref, inverse_ref, weight_ref, weight_t_ref, scaled_out = refs[
-        count : count + 7
-    ]
-    grad, spread, scaled, wide_ref = refs[count + 7 : count + 11]
-    refs = refs[count + 11 :]
-    if fused:
-        normed_ref, line_ref, turn_ref, left_ref, right_ref = refs[:5]
-        refs = refs[5:]
-    else:
-        left_ref, right_ref = source_refs
-    (
-        left_send, left_recv, right_send, right_recv, hop_send, twin_send, own_sem, grad_sem,
-        scaled_sem,
-    ) = refs
-    row, col = lax.axis_index("row"), lax.axis_index("col")
-    share = left_ref.shape[0]
-    ready = greet(n_row, n_col, row * n_col + col)
-    grad_copy = pltpu.make_async_copy(grad_ref, grad, grad_sem)
-    grad_copy.start()
-    block = lambda ref, index: ref.at[pl.ds(pl.multiple_of(index * share, share), share)]
-    owner = col // ratio
-    twin = row + 1 - 2 * (row % 2)
-    chips = n_row // 2
-    is_owner = row == owner
-    same_side = row % 2 == owner % 2
-
-    def right_copy(t):
-        return to(
-            right_ref.at[t], block(right_out, col), right_send.at[t], right_recv.at[col],
-            row, row * ratio + t,
-        )
-
-    def left_copy(off):
-        peer = (col + off) % n_col
-        return to(left_ref, block(left_out, col), left_send.at[off], left_recv.at[col], row, peer)
-
-    def hop_copy(source, index, hop):
-        return to(
-            source, block(right_out, index), hop_send.at[index, hop], right_recv.at[index],
-            (row + 2 * hop) % n_row, col,
-        )
-
-    def twin_copy(source, index):
-        return to(
-            source, block(right_out, index), twin_send.at[index], right_recv.at[index], twin, col
-        )
-
-    work = project(share, rows, *source_refs, *((normed_ref, line_ref, turn_ref, left_ref, right_ref))) if fused else None
-    if fused:
-        next(work)
-    ready()
-    for t in range(ratio):
-        pl.when(row * ratio + t != col)(right_copy(t).start)
-    mine = right_ref.at[col % ratio]
-    own_right = pltpu.make_async_copy(mine, block(right_out, col), own_sem.at[1])
-
-    @pl.when(is_owner)
-    def _():
-        own_right.start()
-        for hop in range(1, chips):
-            hop_copy(mine, col, hop).start()
-        twin_copy(mine, col).start()
-
-    if fused:
-        next(work)
-    own_left = pltpu.make_async_copy(left_ref, block(left_out, col), own_sem.at[0])
-    own_left.start()
-    for off in range(1, n_col):
-        left_copy(off).start()
-
-    def pass_right(off):
-        peer = (col + off) % n_col
-        source = block(right_out, peer)
-        if off:
-            arrived(source, right_recv.at[peer])
-
-            @pl.when(is_owner)
-            def _():
-                for hop in range(1, chips):
-                    hop_copy(source, peer, hop).start()
-
-            pl.when(same_side)(twin_copy(source, peer).start)
-        else:
-
-            @pl.when(jnp.logical_not(is_owner))
-            def _():
-                arrived(source, right_recv.at[peer])
-
-            pl.when(jnp.logical_and(same_side, jnp.logical_not(is_owner)))(
-                twin_copy(source, peer).start
-            )
-
-    fill_weights(blocks, final_ref, wide_ref, weight_ref, weight_t_ref)
-    fill_tables(rows, cols, labels_ref, counts_ref, row, col, table_ref, inverse_ref)
-    spread[...] = jnp.zeros_like(spread)
-    grad_copy.wait()
-    steps = rows // tile
-
-    def scaled_copy(step, slot):
-        extent = tile * size
-        return pltpu.make_async_copy(
-            scaled.at[slot],
-            scaled_out.at[pl.ds(pl.multiple_of(step * extent, extent), extent)],
-            scaled_sem.at[slot],
-        )
-
-    def scale(step, carry):
-        slot = step % 2
-        first = pl.multiple_of(step * tile * cols, tile * cols)
-        part = grad[pl.ds(first, tile * cols), :]
-        for i in range(tile):
-            for e in range(inner):
-                spread[i * LANES + e * cols : i * LANES + (e + 1) * cols, e * CZ : (e + 1) * CZ] = (
-                    part[i * cols : (i + 1) * cols]
-                )
-        inverse = inverse_ref[pl.ds(pl.multiple_of(step * tile, tile), tile), :]
-
-        @pl.when(step >= 2)
-        def _():
-            scaled_copy(step - 2, slot).wait()
-
-        for i in range(0, tile, 2):
-            back = lax.dot_general(
-                weight_ref[...], spread[i * LANES : (i + 2) * LANES, :], (((1,), (1,)), ((), ())),
-                preferred_element_type=f32,
-            )
-            for k in range(2):
-                piece = (
-                    back[:, k * LANES : (k + 1) * LANES] * inverse[i + k : i + k + 1]
-                ).astype(bf16)
-                for b in range(blocks):
-                    scaled[
-                        slot, (i + k) * size : (i + k + 1) * size, b * LANES : (b + 1) * LANES
-                    ] = piece[b * size : (b + 1) * size]
-        scaled_copy(step, slot).start()
-        for off in range(n_col - 1):
-            pl.when(step == min(2 * off + 1, steps - 1))(functools.partial(pass_right, off))
-        return carry
-
-    lax.fori_loop(0, steps, scale, 0)
-    pass_right(n_col - 1)
-    for step in range(max(0, steps - 2), steps):
-        scaled_copy(step, step % 2).wait()
-
-    own_left.wait()
-    pl.when(is_owner)(own_right.wait)
-    for off in range(1, n_col):
-        peer = (col + off) % n_col
-        arrived(block(left_out, peer), left_recv.at[peer])
-    for off in range(1, n_col):
-        left_copy(off).wait_send()
-    for t in range(ratio):
-        pl.when(row * ratio + t != col)(right_copy(t).wait_send)
-
-    @pl.when(is_owner)
-    def _():
-        for off in range(n_col):
-            peer = (col + off) % n_col
-            for hop in range(1, chips):
-                hop_copy(block(right_out, peer), peer, hop).wait_send()
-
-    @pl.when(same_side)
-    def _():
-        for off in range(n_col):
-            peer = (col + off) % n_col
-            twin_copy(block(right_out, peer), peer).wait_send()
-
-
-def core_kernel(
-    n_row, n_col, ratio, rows, cols, tile,
-    labels_ref, left_in_ref, right_in_ref, table_ref, inverse_ref, grad_hbm, scaled_hbm,
-    weight_t_ref, bias_ref,
-    pair_out, left_out, right_out, weight_out,
-    grad, scaled, spread, outer, outer_more, left_more, slots, left_tiles, inverses, label_lanes, right_t, keep, keep_t,
-    weight_acc, left_ref, right_ref, weight_ref, local_sem,
-    left_in, right_twin, right_half, right_mid, right_sum,
-    weight_twin, weight_half, weight_mid, weight_sum, weight_in, weight_part,
-    up_send, down_send, left_recv, twin_send, twin_recv, mid_send, mid_recv,
-    right_send, right_recv, own_sem,
-    w1_send, w1_recv, w2_send, w2_recv, w3_send, w3_recv, around_send, hop_send, last_send,
-    all_recv,
-):
+def core_kernel(n_row, n_col, ratio, rows, cols, tile, fused, *refs):
     f32, bf16 = jnp.float32, jnp.bfloat16
     size = PROJECTED_SIZE
     inner = LANES // cols
     blocks = size // inner
     steps = rows // tile
     span = tile * size
-    seqs = left_in_ref.shape[0]
+    labels_ref, counts_ref, final_ref, bias_ref, grad_hbm = refs[:5]
+    count = 10 if fused else 7
+    source_refs = refs[5:count]
+    pair_out, left_out, right_out, weight_out = refs[count : count + 4]
+    refs = refs[count + 4 :]
+    if fused:
+        normed_ref, line_ref, turn_ref, left_own, right_own = refs[:5]
+        refs = refs[5:]
+    else:
+        left_own, right_own = source_refs
+    (
+        table_ref, over_ref, inverse_ref, wide_ref, weight_w, weight_t_ref, left_tiles, right_panel,
+        g_left_send, g_left_recv, g_right_send, g_right_recv, g_hop_send, g_twin_send, g_own_sem,
+        grad, scaled, spread, outer, outer_own, outer_more, left_more, slots, inverses, label_lanes,
+        right_t, keep, keep_t, weight_acc, left_ref, right_ref, weight_ref, local_sem,
+        left_in, right_twin, right_half, right_mid, right_sum,
+        weight_twin, weight_half, weight_mid, weight_sum, weight_in, weight_part,
+        up_send, down_send, left_recv, twin_send, twin_recv, mid_send, mid_recv,
+        right_send, right_recv, own_sem,
+        w1_send, w1_recv, w2_send, w2_recv, w3_send, w3_recv, around_send, hop_send, last_send,
+        all_recv,
+    ) = refs
+    row, col = lax.axis_index("row"), lax.axis_index("col")
+    ready = greet(n_row, n_col, row * n_col + col)
+    grad_copies = [
+        pltpu.make_async_copy(
+            grad_hbm.at[pl.ds(t * tile * cols, tile * cols)], grad.at[t], local_sem.at[t]
+        )
+        for t in range(steps)
+    ]
+    for copy in grad_copies:
+        copy.start()
+    seqs, wide = right_panel.shape
     share = seqs // n_col
     width = 2 * LANES if blocks % 2 == 0 else LANES
     chunks = blocks * LANES // width
     extras = outer_more.shape[0] - 1
-    row, col = lax.axis_index("row"), lax.axis_index("col")
-    ready = greet(n_row, n_col, row * n_col + col)
     chips = n_row // 2
     chip, side = row // 2, row % 2
     twin = row + 1 - 2 * side
@@ -549,31 +390,97 @@
                 last_copy(group_of(off), index).wait_send()
         for b in range(many):
             pl.when(jnp.logical_not(here(b)))(right_copy(b).wait_send)
-    grad_copies = [
-        pltpu.make_async_copy(
-            grad_hbm.at[pl.ds(t * tile * cols, tile * cols)], grad.at[t], local_sem.at[0, t]
-        )
-        for t in range(steps)
-    ]
-    scaled_copies = [
-        pltpu.make_async_copy(
-            scaled_hbm.at[pl.ds(t * span, span)], scaled.at[t], local_sem.at[1, t]
-        )
-        for t in range(steps)
-    ]
-    for copy in grad_copies + scaled_copies:
-        copy.start()
-
+    is_owner = row == owner
+    same_side = row % 2 == owner % 2
+    group = steps // parts
+    seq_rows = lambda index: pl.ds(pl.multiple_of(index * share, share), share)
+    block = lambda index: right_panel.at[seq_rows(index)]
+    tiles_of = lambda index, h: left_tiles.at[h * group : (h + 1) * group, seq_rows(index)]
+
+    def out_right(t):
+        return to(
+            right_own.at[t], block(col), g_right_send.at[t], g_right_recv.at[col],
+            row, row * ratio + t,
+        )
+
+    def out_left(d, h):
+        for k, step in enumerate((d, -d)):
+            there = col + step
+            copy = to(
+                left_own.at[h * group : (h + 1) * group], tiles_of(col, h),
+                g_left_send.at[k, d, h], g_left_recv.at[col, h], row, there % n_col,
+            )
+            yield jnp.logical_and(there >= 0, there < n_col), copy
+
+    def pass_hop(source, index, hop):
+        return to(
+            source, block(index), g_hop_send.at[index, hop], g_right_recv.at[index],
+            (row + 2 * hop) % n_row, col,
+        )
+
+    def pass_twin(source, index):
+        return to(source, block(index), g_twin_send.at[index], g_right_recv.at[index], twin, col)
+
+    if fused:
+        work = project(
+            share, rows, *source_refs, normed_ref, line_ref, turn_ref, left_own, right_own
+        )
+        next(work)
+    ready()
+    for t in range(ratio):
+        pl.when(row * ratio + t != col)(out_right(t).start)
+    own_block = right_own.at[col % ratio]
+    own_right = pltpu.make_async_copy(own_block, block(col), g_own_sem.at[1])
+
+    @pl.when(is_owner)
+    def _():
+        own_right.start()
+        for hop in range(1, chips):
+            pass_hop(own_block, col, hop).start()
+        pass_twin(own_block, col).start()
+
+    if fused:
+        next(work)
+    own_left = pltpu.make_async_copy(left_own, left_tiles.at[:, seq_rows(col)], g_own_sem.at[0])
+    own_left.start()
+    for h in range(parts):
+        for d in range(1, n_col):
+            for on, copy in out_left(d, h):
+                pl.when(on)(copy.start)
+
+    def pass_right(off):
+        peer = (col + off) % n_col
+        source = block(peer)
+        if off:
+            arrived(source, g_right_recv.at[peer])
+
+            @pl.when(is_owner)
+            def _():
+                for hop in range(1, chips):
+                    pass_hop(source, peer, hop).start()
+
+            pl.when(same_side)(pass_twin(source, peer).start)
+        else:
+
+            @pl.when(jnp.logical_not(is_owner))
+            def _():
+                arrived(source, g_right_recv.at[peer])
+
+            pl.when(jnp.logical_and(same_side, jnp.logical_not(is_owner)))(
+                pass_twin(source, peer).start
+            )
+
+    fill_weights(blocks, final_ref, wide_ref, weight_w, weight_t_ref)
+    fill_tables(
+        rows, cols, labels_ref, counts_ref, row, col, table_ref, inverse_ref, over_ref
+    )
     place_of = lax.broadcasted_iota(jnp.int32, (tile, span), 1) // size
     seq = lax.broadcasted_iota(jnp.int32, (seqs, LANES), 0).astype(f32)
     for chain in range(keep.shape[0]):
         kept = jnp.where(seq < table_ref[chain : chain + 1, :], 1.0, 0.0)
         keep[chain] = kept.astype(bf16)
         keep_t[chain] = kept.T.astype(bf16)
-    for b in range(blocks):
-        right_t[b * LANES : (b + 1) * LANES, :] = right_in_ref[:, b * LANES : (b + 1) * LANES].T
     for t in range(steps):
-        left_tiles[t] = left_in_ref[:, t * span : (t + 1) * span]
         inverses[t] = inverse_ref[t * tile : (t + 1) * tile, :]
         line = jnp.zeros((tile, span), jnp.int32)
         for i in range(tile):
@@ -583,6 +490,43 @@
     weight_acc[...] = jnp.zeros_like(weight_acc)
     outer_more[0] = jnp.zeros(outer_more.shape[1:], bf16)
     left_more[0] = jnp.zeros(left_more.shape[1:], f32)
+    for copy in grad_copies:
+        copy.wait()
+
+    def fill_spread(t):
+        for i in range(tile):
+            part = grad[t, i * cols : (i + 1) * cols, :]
+            for e in range(inner):
+                spread[i * LANES + e * cols : i * LANES + (e + 1) * cols, e * CZ : (e + 1) * CZ] = (
+                    part
+                )
+
+    def scale(step, carry):
+        fill_spread(step)
+        inverse = inverses[step]
+        for i in range(0, tile, 2):
+            back = lax.dot_general(
+                weight_w[...], spread[i * LANES : (i + 2) * LANES, :], (((1,), (1,)), ((), ())),
+                preferred_element_type=f32,
+            )
+            for k in range(2):
+                value = (
+                    back[:, k * LANES : (k + 1) * LANES] * inverse[i + k : i + k + 1]
+                ).astype(bf16)
+                for b in range(blocks):
+                    scaled[
+                        step, (i + k) * size : (i + k + 1) * size, b * LANES : (b + 1) * LANES
+                    ] = value[b * size : (b + 1) * size]
+        for off in range(n_col - 1):
+            pl.when(step == min(2 * off + 1, steps - 1))(functools.partial(pass_right, off))
+        return carry
+
+    lax.fori_loop(0, steps, scale, 0)
+    pass_right(n_col - 1)
+    pl.when(is_owner)(own_right.wait)
+    own_left.wait()
+    for b in range(blocks):
+        right_t[b * LANES : (b + 1) * LANES, :] = right_panel[:, b * LANES : (b + 1) * LANES].T
 
     offset = row * rows
     label_of = lambda t, i: labels_ref[offset + t * tile + i]
@@ -623,7 +567,7 @@
         kept = [jnp.concatenate([keep[chain + k]] * (width // LANES), axis=1) for k in range(2)]
         for c in range(chunks):
             lanes = slice(c * width, (c + 1) * width)
-            right = right_in_ref[:, lanes]
+            right = right_panel[:, lanes]
             right = jnp.concatenate([right * kept[0], right * kept[1]], axis=0)
             prod = jnp.dot(both_t, right, preferred_element_type=f32)
             for i in range(tile):
@@ -637,46 +581,41 @@
                         ).astype(bf16),
                     )
 
+    def forward_main(t, carry):
+        def store(where, lanes, value):
+            outer[t, where, lanes] = value
+
+        forward(t, label_of(t, 0), t, store)
+        fill_spread(t)
+        weight_acc[...] += jnp.dot(outer[t], spread[...], preferred_element_type=f32)
+        return carry
+
+    for h in range(parts):
+        for off in range(1, n_col):
+            peer = (col + off) % n_col
+            arrived(tiles_of(peer, h), g_left_recv.at[peer, h])
+        lax.fori_loop(h * group, (h + 1) * group, forward_main, 0)
+
     def forward_more(u, carry):
         t, chain = extra_of(u)
         same = jnp.full((size, LANES), same_of(u), f32).astype(bf16)
 
         def store(where, lanes, value):
+            outer_own[where, lanes] = value
             outer_more[u + 1, where, lanes] = value + outer_more[u, where, lanes] * same
 
         forward(t, chain, steps + u, store)
+        fill_spread(t)
+        weight_acc[...] += jnp.dot(outer_own[...], spread[...], preferred_element_type=f32)
         return carry
 
     lax.fori_loop(0, extras, forward_more, 0)
-    for copy in grad_copies:
-        copy.wait()
-
-    def forward_main(t, carry):
-        slot = slot_of(t)
-
-        def store(where, lanes, value):
-            outer[t, where, lanes] = value + outer_more[slot, where, lanes]
-
-        forward(t, label_of(t, 0), t, store)
-        for i in range(tile):
-            part = grad[t, i * cols : (i + 1) * cols, :]
-            for e in range(inner):
-                spread[i * LANES + e * cols : i * LANES + (e + 1) * cols, e * CZ : (e + 1) * CZ] = (
-                    part
-                )
-        weight_acc[...] += jnp.dot(outer[t], spread[...], preferred_element_type=f32)
-        return carry
-
-    lax.fori_loop(0, steps, forward_main, 0)
     extent = blocks * size
     for e in range(inner):
         weight_ref[e * extent : (e + 1) * extent, :] = weight_acc[
             :, e * CZ : (e + 1) * CZ
         ].astype(bf16)
-    ready()
     w1_copy.start()
-    for copy in scaled_copies:
-        copy.wait()
 
     def left_part(t, chain):
         tall = jnp.zeros((span, 2 * seqs), f32)
@@ -737,19 +676,21 @@
 
     lax.fori_loop(0, chunks, right_main, 0)
     after_right()
-    group = lax.broadcasted_iota(jnp.int32, (CZ, LANES), 1) // cols
+    lane_group = lax.broadcasted_iota(jnp.int32, (CZ, LANES), 1) // cols
 
     def pairs_of(t, carry):
+        slot = slot_of(t)
         for i in range(0, tile, 2):
+            lanes = slice(i * LANES, (i + 2) * LANES)
             both = jnp.dot(
-                weight_t_ref[...], outer[t, :, i * LANES : (i + 2) * LANES],
+                weight_t_ref[...], outer[t, :, lanes] + outer_more[slot, :, lanes],
                 preferred_element_type=f32,
             )
             for k in range(2):
                 lanes = slice(k * LANES, (k + 1) * LANES)
                 total = both[:CZ, lanes]
                 for e in range(1, inner):
-                    total = jnp.where(group == e, both[e * CZ : (e + 1) * CZ, lanes], total)
+                    total = jnp.where(lane_group == e, both[e * CZ : (e + 1) * CZ, lanes], total)
                 turned = total.T
                 pair = turned[:cols]
                 for e in range(1, inner):
@@ -763,49 +704,95 @@
 
     lax.fori_loop(0, steps, pairs_of, 0)
     finish()
-
-
-def finish_kernel(fused, blocks, left_ref, right_ref, weight_ref, *refs):
+    for t in range(ratio):
+        pl.when(row * ratio + t != col)(out_right(t).wait_send)
+    for h in range(parts):
+        for d in range(1, n_col):
+            for on, copy in out_left(d, h):
+                pl.when(on)(copy.wait_send)
+
+    @pl.when(is_owner)
+    def _():
+        for index in range(n_col):
+            for hop in range(1, chips):
+                pass_hop(block(index), index, hop).wait_send()
+
+    @pl.when(same_side)
+    def _():
+        for index in range(n_col):
+            pass_twin(block(index), index).wait_send()
+
+
+def finish_kernel(
+    fused, blocks,
+    left_in, right_in, weight_in, pair_in,
+    left_out, right_out, weight_out, pair_out,
+    left, right, weight, pair, right_done, weight_done, in_sem, out_sem, *more,
+):
     f32, bf16 = jnp.float32, jnp.bfloat16
     size = PROJECTED_SIZE
-    left_out, right_out, weight_out = refs[:3]
-    left_out[...] = left_ref[...]
+    takes = [
+        pltpu.make_async_copy(source, target, in_sem.at[k])
+        for k, (source, target) in enumerate(
+            ((weight_in, weight), (right_in, right), (left_in, left), (pair_in, pair))
+        )
+    ]
+    gives = [
+        pltpu.make_async_copy(source, target, out_sem.at[k])
+        for k, (source, target) in enumerate(
+            (
+                (weight_done, weight_out),
+                (right_done if fused else right, right_out),
+                (left, left_out),
+                (pair, pair_out),
+            )
+        )
+    ]
+    for copy in takes:
+        copy.start()
+    takes[0].wait()
     for g in range(size):
         e = (g % blocks) * (size // blocks) + g // blocks
-        weight_out[pl.ds(e, size, stride=size), :] = weight_ref[
+        weight_done[pl.ds(e, size, stride=size), :] = weight[
             g * size : (g + 1) * size, :
         ].astype(f32) * (1.0 / WINDOW_AMINOS)
-    if not fused:
-        right_out[...] = right_ref[...]
-        return
-    turn_ref, line_ref = refs[3:]
-    share = right_ref.shape[1]
-    low = share // 2
-    rows = line_ref.shape[0] // share
-    near = lax.broadcasted_iota(jnp.int32, (low, LANES), 1) < rows
-    for b in range(size // 2):
-        lanes = slice(b * LANES, (b + 1) * LANES)
-        above = right_ref[0, :low, lanes].astype(f32)
-        below = right_ref[0, low:, lanes].astype(f32)
-        turn_ref[pl.ds(2 * b, low, stride=size), :] = jnp.where(
-            near, above, pltpu.roll(below, rows, 1)
-        )
-        turn_ref[pl.ds(2 * b + 1, low, stride=size), :] = jnp.where(
-            near, pltpu.roll(above, rows, 1), below
-        )
-    fold = LANES // size
-    for p in range(low):
-        turned = jnp.concatenate([turn_ref[p * size : (p + 1) * size, :]] * fold, axis=0).T
-        line_ref[p * rows : (p + 1) * rows, :] = turned[:rows]
-        line_ref[(p + low) * rows : (p + low + 1) * rows, :] = turned[rows:]
-    place = lax.broadcasted_iota(jnp.int32, (share, LANES), 1) // size
-    for g in range(rows // fold):
-        total = line_ref[pl.ds(g * fold, share, stride=rows), :]
-        for k in range(1, fold):
-            total = jnp.where(
-                place == k, line_ref[pl.ds(g * fold + k, share, stride=rows), :], total
+    gives[0].start()
+    takes[1].wait()
+    for k in range(2, 4):
+        takes[k].wait()
+        gives[k].start()
+    if fused:
+        turn_ref, line_ref = more
+        share = right.shape[1]
+        low = share // 2
+        rows = line_ref.shape[0] // share
+        near = lax.broadcasted_iota(jnp.int32, (low, LANES), 1) < rows
+        for b in range(size // 2):
+            lanes = slice(b * LANES, (b + 1) * LANES)
+            above = right[0, :low, lanes].astype(f32)
+            below = right[0, low:, lanes].astype(f32)
+            turn_ref[pl.ds(2 * b, low, stride=size), :] = jnp.where(
+                near, above, pltpu.roll(below, rows, 1)
             )
-        right_out[:, g * LANES : (g + 1) * LANES] = total.astype(bf16)
+            turn_ref[pl.ds(2 * b + 1, low, stride=size), :] = jnp.where(
+                near, pltpu.roll(above, rows, 1), below
+            )
+        fold = LANES // size
+        for p in range(low):
+            turned = jnp.concatenate([turn_ref[p * size : (p + 1) * size, :]] * fold, axis=0).T
+            line_ref[p * rows : (p + 1) * rows, :] = turned[:rows]
+            line_ref[(p + low) * rows : (p + low + 1) * rows, :] = turned[rows:]
+        place = lax.broadcasted_iota(jnp.int32, (share, LANES), 1) // size
+        for g in range(rows // fold):
+            total = line_ref[pl.ds(g * fold, share, stride=rows), :]
+            for k in range(1, fold):
+                total = jnp.where(
+                    place == k, line_ref[pl.ds(g * fold + k, share, stride=rows), :], total
+                )
+            right_done[:, g * LANES : (g + 1) * LANES] = total.astype(bf16)
+    gives[1].start()
+    for copy in gives:
+        copy.wait()
 
 
 def shards(
@@ -836,6 +823,7 @@
     tile = 8
     steps = rows // tile
     fused = ratio == 1 and 2 * rows == LANES and share % 16 == 0
+    span = tile * size
     if fused:
         sources = (
             alignment_tensor, standardizer_scaling[None, :], standardizer_offset[None, :],
@@ -845,7 +833,7 @@
             pltpu.VMEM((share * rows, feats), bf16),
             pltpu.VMEM((share * rows, LANES), f32),
             pltpu.VMEM((share // 2 * size, LANES), f32),
-            pltpu.VMEM((share, rows * size), bf16),
+            pltpu.VMEM((steps, share, span), bf16),
             pltpu.VMEM((ratio, share, wide), bf16),
         ]
     else:
@@ -857,7 +845,7 @@
             jnp.concatenate([first_projector, second_projector], axis=1),
             preferred_element_type=f32,
         ).astype(bf16)
-        left_own = both[:, :size].reshape(share, rows * size)
+        left_own = both[:, :size].reshape(share, steps, span).transpose(1, 0, 2)
         right_own = (
             both[:, size:]
             .reshape(share, ratio, cols, size)
@@ -868,40 +856,14 @@
     flat_grad = couple_delta_adjoint.reshape(-1, CZ)
     smem = pl.BlockSpec(memory_space=pltpu.SMEM)
     hbm = pl.BlockSpec(memory_space=pl.ANY)
-    left_panel, right_panel, table, inverse, weight, weight_t, scaled = pl.pallas_call(
-        functools.partial(gather_kernel, n_row, n_col, ratio, rows, cols, tile, fused),
-        in_specs=[smem, smem, vmem, hbm] + [vmem] * len(sources),
-        out_specs=[vmem] * 6 + [hbm],
-        out_shape=[
-            jax.ShapeDtypeStruct((seqs, rows * size), bf16),
-            jax.ShapeDtypeStruct((seqs, wide), bf16),
-            jax.ShapeDtypeStruct((2 * CHAINS, LANES), f32),
-            jax.ShapeDtypeStruct((rows, LANES), f32),
-            jax.ShapeDtypeStruct((blocks * size, inner * CZ), bf16),
-            jax.ShapeDtypeStruct((inner * CZ, blocks * size), bf16),
-            jax.ShapeDtypeStruct((rows * size, wide), bf16),
-        ],
-        scratch_shapes=[
-            pltpu.VMEM((rows * cols, CZ), bf16),
-            pltpu.VMEM((tile * LANES, inner * CZ), bf16),
-            pltpu.VMEM((2, tile * size, wide), bf16),
-            pltpu.VMEM((size * size, CZ), f32),
-            *extra,
-            dma((n_col,)), dma((n_col,)), dma((ratio,)), dma((n_col,)),
-            dma((n_col, n_row // 2)), dma((n_col,)), dma((2,)), dma, dma((2,)),
-        ],
-        compiler_params=pltpu.CompilerParams(
-            collective_id=0, has_side_effects=True, vmem_limit_bytes=56 * 1024 * 1024
-        ),
-    )(amino_strand_label, matched_strand_count, final_projector, flat_grad, *sources)
-
+    chips = n_row // 2
     many = n_col // n_row
     quarter = size * size // n_row
     piece = quarter // n_col
     extras = min(CHAINS - 1, rows - 1) // 2
     pair, left_sum, right_sum, weight_total = pl.pallas_call(
-        functools.partial(core_kernel, n_row, n_col, ratio, rows, cols, tile),
-        in_specs=[smem] + [vmem] * 4 + [hbm] * 2 + [vmem] * 2,
+        functools.partial(core_kernel, n_row, n_col, ratio, rows, cols, tile, fused),
+        in_specs=[smem, smem, vmem, vmem, hbm] + [vmem] * len(sources),
         out_specs=[vmem] * 4,
         out_shape=[
             jax.ShapeDtypeStruct((rows * cols, CZ), bf16),
@@ -910,16 +872,27 @@
             jax.ShapeDtypeStruct((size * size, CZ), bf16),
         ],
         scratch_shapes=[
+            *extra,
+            pltpu.VMEM((2 * CHAINS, LANES), f32),
+            pltpu.VMEM((2 * CHAINS, LANES), f32),
+            pltpu.VMEM((rows, LANES), f32),
+            pltpu.VMEM((size * size, CZ), f32),
+            pltpu.VMEM((blocks * size, inner * CZ), bf16),
+            pltpu.VMEM((inner * CZ, blocks * size), bf16),
+            pltpu.VMEM((steps, seqs, span), bf16),
+            pltpu.VMEM((seqs, wide), bf16),
+            dma((2, n_col, 2)), dma((n_col, 2)), dma((ratio,)), dma((n_col,)),
+            dma((n_col, chips)), dma((n_col,)), dma((2,)),
             pltpu.VMEM((steps, tile * cols, CZ), bf16),
-            pltpu.VMEM((steps, tile * size, wide), bf16),
+            pltpu.VMEM((steps, span, wide), bf16),
             pltpu.VMEM((tile * LANES, inner * CZ), bf16),
             pltpu.VMEM((steps, blocks * size, tile * LANES), bf16),
+            pltpu.VMEM((blocks * size, tile * LANES), bf16),
             pltpu.VMEM((extras + 1, blocks * size, tile * LANES), bf16),
-            pltpu.VMEM((extras + 1, seqs, tile * size), f32),
-            pltpu.VMEM((steps + extras, 2 * seqs, tile * size), bf16),
-            pltpu.VMEM((steps, seqs, tile * size), bf16),
+            pltpu.VMEM((extras + 1, seqs, span), f32),
+            pltpu.VMEM((steps + extras, 2 * seqs, span), bf16),
             pltpu.VMEM((steps, tile, LANES), f32),
-            pltpu.VMEM((steps, tile, tile * size), jnp.int32),
+            pltpu.VMEM((steps, tile, span), jnp.int32),
             pltpu.VMEM((wide, seqs), bf16),
             pltpu.VMEM((CHAINS + 2, seqs, LANES), bf16),
             pltpu.VMEM((CHAINS + 2, LANES, seqs), bf16),
@@ -927,58 +900,64 @@
             pltpu.VMEM((n_col, share, rows * size), bf16),
             pltpu.VMEM((n_col, share, wide), bf16),
             pltpu.VMEM((size * size, CZ), bf16),
-            dma((2, steps)),
+            dma((steps,)),
             pltpu.VMEM((n_col, share, rows * size), bf16),
             pltpu.VMEM((n_col // 2, share, wide), bf16),
             pltpu.VMEM((n_col // 2, share, wide), bf16),
-            pltpu.VMEM((n_row // 2, many, share, wide), bf16),
+            pltpu.VMEM((chips, many, share, wide), bf16),
             pltpu.VMEM((many, share, wide), bf16),
-            pltpu.VMEM((n_row // 2 * quarter, CZ), bf16),
-            pltpu.VMEM((n_row // 2 * quarter, CZ), bf16),
-            pltpu.VMEM((n_row // 2, quarter, CZ), bf16),
+            pltpu.VMEM((chips * quarter, CZ), bf16),
+            pltpu.VMEM((chips * quarter, CZ), bf16),
+            pltpu.VMEM((chips, quarter, CZ), bf16),
             pltpu.VMEM((quarter, CZ), bf16),
             pltpu.VMEM((n_col, piece, CZ), bf16),
             pltpu.VMEM((piece, CZ), bf16),
             dma((n_col, 2)), dma((n_col, 2)), dma((n_col, 2)),
             dma, dma,
-            dma((n_row // 2,)), dma((n_row // 2,)),
+            dma((chips,)), dma((chips,)),
             dma((many,)), dma((ratio,)), dma,
             dma, dma,
-            dma((n_row // 2,)), dma((n_row // 2,)),
+            dma((chips,)), dma((chips,)),
             dma((n_col,)), dma((n_col,)), dma((n_col,)),
-            dma((n_col, n_row // 2)), dma((n_row, n_col)), dma((n_row, n_col)),
+            dma((n_col, chips)), dma((n_row, n_col)), dma((n_row, n_col)),
         ],
         compiler_params=pltpu.CompilerParams(
-            collective_id=1, has_side_effects=True, vmem_limit_bytes=58 * 1024 * 1024
+            collective_id=0, has_side_effects=True, vmem_limit_bytes=60 * 1024 * 1024
         ),
     )(
         amino_strand_label,
-        left_panel,
-        right_panel,
-        table,
-        inverse,
+        matched_strand_count,
+        final_projector,
+        final_offset[None, :],
         flat_grad,
-        scaled,
-        weight_t,
-        final_offset[None, :],
+        *sources,
     )
-    pair_update = pair.reshape(rows, cols, CZ)
-    adjoint_first_factor, grad_right, grad_w_out = pl.pallas_call(
+    adjoint_first_factor, grad_right, grad_w_out, pair = pl.pallas_call(
         functools.partial(finish_kernel, fused, blocks),
-        in_specs=[vmem] * 3,
-        out_specs=[vmem] * 3,
+        in_specs=[hbm] * 4,
+        out_specs=[hbm] * 4,
         out_shape=[
             jax.ShapeDtypeStruct((share, rows * size), bf16),
             jax.ShapeDtypeStruct((share, rows * size) if fused else (ratio, share, wide), bf16),
             jax.ShapeDtypeStruct((size * size, CZ), f32),
+            jax.ShapeDtypeStruct((rows * cols, CZ), bf16),
         ],
         scratch_shapes=[
-            pltpu.VMEM((share // 2 * size, LANES), f32),
-            pltpu.VMEM((share * rows, LANES), f32),
+            pltpu.VMEM((share, rows * size), bf16),
+            pltpu.VMEM((ratio, share, wide), bf16),
+            pltpu.VMEM((size * size, CZ), bf16),
+            pltpu.VMEM((rows * cols, CZ), bf16),
+            pltpu.VMEM((share, rows * size), bf16),
+            pltpu.VMEM((size * size, CZ), f32),
+            dma((4,)), dma((4,)),
         ]
-        if fused
-        else [],
-    )(left_sum, right_sum, weight_total)
+        + (
+            [pltpu.VMEM((share // 2 * size, LANES), f32), pltpu.VMEM((share * rows, LANES), f32)]
+            if fused
+            else []
+        ),
+    )(left_sum, right_sum, weight_total, pair)
+    pair_update = pair.reshape(rows, cols, CZ)
     if not fused:
         grad_right = (
             grad_right.reshape(ratio, share, size, cols)

time: 73.5 us -> 65.9 us (0.90)
  Pallas kernels: 70.4 us -> 65.1 us
  local copies, waits for them, and re-layouts: 2.26 us -> 0 us
    pallas_call x1 -> x0, Pallas kernels: 25.5 us -> none  [shards(): pl.pallas_call(functools.partial(gather_kernel, n_row, n_col, ratio, rows...]
    pallas_call x1, Pallas kernels: 41.2 us -> 61.7 us  [shards(): pl.pallas_call(functools.partial(core_kernel, n_row, n_col, ratio, rows,...]
    unnamed x1 -> x0, local copies, waits for them, and re-layouts: 2.26 us -> none
where the time goes in v5:
time: 65.9 us; the launch traced here: 65.8 us
  Pallas kernels  65.1 us (99%)
    pallas_call x1, Pallas kernels, shards(): pl.pallas_call(functools.partial(core_kernel, n_row, n_col, ratio, rows,...  61.7 us
    pallas_call x1, Pallas kernels, shards(): pl.pallas_call(functools.partial(finish_kernel, fused, blocks), in_specs=...  3.44 us

profile of v5, /device:TPU:1, one launch (start us, length us, event | category | flops | bytes accessed | tf_op | source)
XLA Modules:
  0.0 65.8 jit_solution(12142585828783613486)
XLA Ops:
  0.6 61.7 %shard_map.129 = (bf16[4096,128]{1,0:T(8,128)(2,1)}, bf16[32,2048]{1,0:T(8,128)(2,1)}, bf16[1,32,2048]{2,1,0:T(8,128)(2,1)}, bf16[1024,128]{1,0:T(8,128)(2,1)}) custom-call(s32[256]{0:T(256)} %refs_0_.1, s32[8,8]{1,0:T(8,128)} %refs_1_.1, bf16[1024,128]{1,0:T(8,128)(2,1)} %refs_2_.1, f32[1,128]{1,0:T(1,128)} %bitcast.12, bf16[4096,128]{1,0:T(8,128)(2,1)} %bitcast.7, ...), custom_call_target="tpu_custom_call" | custom-call | tf_op jit(solution)/shard_map/pallas_call | solution.py:864
  62.3 3.4 %shard_map.130 = (bf16[32,2048]{1,0:T(8,128)(2,1)}, bf16[32,2048]{1,0:T(8,128)(2,1)}, f32[1024,128]{1,0:T(8,128)}, bf16[4096,128]{1,0:T(8,128)(2,1)}) custom-call(bf16[32,2048]{1,0:T(8,128)(2,1)} %get-tuple-element.12.left_in, bf16[1,32,2048]{2,1,0:T(8,128)(2,1)} %get-tuple-element.13.right_in, bf16[1024,128]{1,0:T(8,128)(2,1)} %get-tuple-element.14.weight_in, ...), custom_call_target="tpu_custom_call" | custom-call | tf_op jit(solution)/shard_map/pallas_call | solution.py:935

commit v6 on v5

--- a/solution.py
+++ b/solution.py
@@ -206,9 +206,15 @@
     w1_copy = to(
         weight_ref.at[rows_of(1 - side, chips * quarter)], weight_twin, w1_send, w1_recv, twin, col
     )
-    twin_copy = to(
-        right_ref.at[rows_of(1 - side, half)], right_twin, twin_send, twin_recv, twin, col
-    )
+    right_parts = twin_recv.shape[0]
+    right_part = right_twin.shape[2] // right_parts
+    right_lanes = lambda h: slice(h * right_part, (h + 1) * right_part)
+
+    def twin_copy(h):
+        return to(
+            right_ref.at[rows_of(1 - side, half), :, right_lanes(h)],
+            right_twin.at[:, :, right_lanes(h)], twin_send.at[h], twin_recv.at[h], twin, col,
+        )
 
     def w2_copy(off):
         peer = (chip + off) % chips
@@ -217,17 +223,18 @@
             w2_recv.at[chip], 2 * peer + side, col,
         )
 
-    def mid_copy(off):
+    def mid_copy(off, h):
         peer = (chip + off) % chips
         return to(
-            right_half.at[rows_of(peer, many)], right_mid.at[chip], mid_send.at[off],
-            mid_recv.at[chip], 2 * peer + side, col,
-        )
-
-    def right_copy(b):
+            right_half.at[rows_of(peer, many), :, right_lanes(h)],
+            right_mid.at[chip, :, :, right_lanes(h)], mid_send.at[off, h],
+            mid_recv.at[chip, h], 2 * peer + side, col,
+        )
+
+    def right_copy(b, h):
         return to(
-            right_sum.at[b], right_out.at[slot], right_send.at[b], right_recv.at[slot],
-            owner, mine * many + b,
+            right_sum.at[b, :, right_lanes(h)], right_out.at[slot, :, right_lanes(h)],
+            right_send.at[b, h], right_recv.at[slot, h], owner, mine * many + b,
         )
 
     def left_copies(d, h):
@@ -302,6 +309,9 @@
         weight_sum[...] = total.astype(bf16)
         for off in range(1, n_col):
             w3_copy(off).start()
+        for h in range(1, parts):
+            for d in range(1, n_col):
+                left_start(d, h)
 
     def during_right():
         total = weight_sum[rows_of(col, piece), :].astype(f32)
@@ -316,18 +326,33 @@
         for off in range(1, chips):
             hop_copy(col, off, weight_part).start()
         last_copy(mine, col, weight_part).start()
-        for h in range(1, parts):
-            for d in range(1, n_col):
-                left_start(d, h)
-
-    def after_right():
-        twin_copy.start()
-
-    def pair_first():
-        arrived(right_twin, twin_recv)
-        right_half[...] = add(right_ref[rows_of(side, half)], right_twin[...]).astype(bf16)
+
+    def right_first(h):
+        twin_copy(h).start()
+
+    def right_second(h):
+        lanes = right_lanes(h)
+        arrived(right_twin.at[:, :, lanes], twin_recv.at[h])
+        right_half[:, :, lanes] = add(
+            right_ref[rows_of(side, half), :, lanes], right_twin[:, :, lanes]
+        ).astype(bf16)
         for off in range(1, chips):
-            mid_copy(off).start()
+            mid_copy(off, h).start()
+
+    def right_third(h):
+        lanes = right_lanes(h)
+        total = right_half[rows_of(chip, many), :, lanes].astype(f32)
+        for off in range(1, chips):
+            peer = (chip + off) % chips
+            arrived(right_mid.at[peer, :, :, lanes], mid_recv.at[peer, h])
+            total = add(total, right_mid[peer, :, :, lanes])
+        right_sum[:, :, lanes] = total.astype(bf16)
+        for b in range(many):
+            pl.when(jnp.logical_not(here(b)))(right_copy(b, h).start)
+            own = pltpu.make_async_copy(
+                right_sum.at[b, :, lanes], right_out.at[slot, :, lanes], right_recv.at[slot, h]
+            )
+            pl.when(here(b))(own.start)
 
     def pair_second():
         for off in range(1, n_col):
@@ -336,18 +361,6 @@
             for hop in range(1, chips):
                 hop_copy(peer, hop).start()
             last_copy(mine, peer).start()
-
-    def pair_third():
-        total = right_half[rows_of(chip, many)].astype(f32)
-        for off in range(1, chips):
-            peer = (chip + off) % chips
-            arrived(right_mid.at[peer], mid_recv.at[peer])
-            total = add(total, right_mid[peer])
-        right_sum[...] = total.astype(bf16)
-        for b in range(many):
-            pl.when(jnp.logical_not(here(b)))(right_copy(b).start)
-            own = pltpu.make_async_copy(right_sum.at[b], right_out.at[slot], right_recv.at[slot])
-            pl.when(here(b))(own.start)
 
     def finish():
         for off in range(n_col):
@@ -364,7 +377,8 @@
             total = add(total, left_in[peer])
         left_out[...] = total.astype(bf16)
         for t in range(ratio):
-            arrived(right_out.at[t], right_recv.at[t])
+            for h in range(right_parts):
+                arrived(right_out.at[t, :, right_lanes(h)], right_recv.at[t, h])
         for off in range(n_col):
             peer = (col + off) % n_col
             for other in range(chips):
@@ -373,10 +387,12 @@
 
         own_piece.wait()
         w1_copy.wait_send()
-        twin_copy.wait_send()
+        for h in range(right_parts):
+            twin_copy(h).wait_send()
         for off in range(1, chips):
             w2_copy(off).wait_send()
-            mid_copy(off).wait_send()
+            for h in range(right_parts):
+                mid_copy(off, h).wait_send()
         for off in range(1, n_col):
             w3_copy(off).wait_send()
             around_copy(off).wait_send()
@@ -389,7 +405,8 @@
             for off in range(chips):
                 last_copy(group_of(off), index).wait_send()
         for b in range(many):
-            pl.when(jnp.logical_not(here(b)))(right_copy(b).wait_send)
+            for h in range(right_parts):
+                pl.when(jnp.logical_not(here(b)))(right_copy(b, h).wait_send)
     is_owner = row == owner
     same_side = row % 2 == owner % 2
     group = steps // parts
@@ -671,11 +688,13 @@
         whole = jnp.concatenate(total, axis=1)
         for q in range(n_col):
             right_ref[q, :, lanes] = whole[q * share : (q + 1) * share].astype(bf16)
+        pl.when(c == chunks // 2 - 1)(functools.partial(right_first, 0))
+        pl.when(c == max(chunks - 2, chunks // 2))(functools.partial(right_second, 0))
         pl.when(c == chunks * 3 // 4)(during_right)
         return carry
 
     lax.fori_loop(0, chunks, right_main, 0)
-    after_right()
+    right_first(1)
     lane_group = lax.broadcasted_iota(jnp.int32, (CZ, LANES), 1) // cols
 
     def pairs_of(t, carry):
@@ -697,9 +716,10 @@
                     pair = pair + turned[e * cols : (e + 1) * cols]
                 first = pl.multiple_of((t * tile + i + k) * cols, cols)
                 pair_out[pl.ds(first, cols), :] = (pair + bias_ref[...]).astype(bf16)
-        pl.when(t == min(1, steps - 1))(pair_first)
+        pl.when(t == min(3, steps - 1))(functools.partial(right_second, 1))
         pl.when(t == steps // 2)(pair_second)
-        pl.when(t == steps - 1)(pair_third)
+        pl.when(t == steps * 5 // 8)(functools.partial(right_third, 0))
+        pl.when(t == steps - 1)(functools.partial(right_third, 1))
         return carry
 
     lax.fori_loop(0, steps, pairs_of, 0)
@@ -913,9 +933,9 @@
             pltpu.VMEM((n_col, piece, CZ), bf16),
             pltpu.VMEM((piece, CZ), bf16),
             dma((n_col, 2)), dma((n_col, 2)), dma((n_col, 2)),
-            dma, dma,
-            dma((chips,)), dma((chips,)),
-            dma((many,)), dma((ratio,)), dma,
+            dma((2,)), dma((2,)),
+            dma((chips, 2)), dma((chips, 2)),
+            dma((many, 2)), dma((ratio, 2)), dma,
             dma, dma,
             dma((chips,)), dma((chips,)),
             dma((n_col,)), dma((n_col,)), dma((n_col,)),

time: 65.9 us -> 64.8 us (0.983)
  Pallas kernels: 65.1 us -> 64 us
    pallas_call x1, Pallas kernels: 61.7 us -> 60.5 us  [shards(): pl.pallas_call(functools.partial(core_kernel, n_row, n_col, ratio, rows,...]
where the time goes in v6:
time: 64.8 us; the launch traced here: 64.6 us
  Pallas kernels  64 us (99%)
    pallas_call x1, Pallas kernels, shards(): pl.pallas_call(functools.partial(core_kernel, n_row, n_col, ratio, rows,...  60.5 us
    pallas_call x1, Pallas kernels, shards(): pl.pallas_call(functools.partial(finish_kernel, fused, blocks), in_specs=...  3.44 us

profile of v6, /device:TPU:1, one launch (start us, length us, event | category | flops | bytes accessed | tf_op | source)
XLA Modules:
  0.0 64.6 jit_solution(3318563004362461521)
XLA Ops:
  0.6 60.5 %shard_map.129 = (bf16[4096,128]{1,0:T(8,128)(2,1)}, bf16[32,2048]{1,0:T(8,128)(2,1)}, bf16[1,32,2048]{2,1,0:T(8,128)(2,1)}, bf16[1024,128]{1,0:T(8,128)(2,1)}) custom-call(s32[256]{0:T(256)} %refs_0_.1, s32[8,8]{1,0:T(8,128)} %refs_1_.1, bf16[1024,128]{1,0:T(8,128)(2,1)} %refs_2_.1, f32[1,128]{1,0:T(1,128)} %bitcast.12, bf16[4096,128]{1,0:T(8,128)(2,1)} %bitcast.7, ...), custom_call_target="tpu_custom_call" | custom-call | tf_op jit(solution)/shard_map/pallas_call | solution.py:884
  61.2 3.4 %shard_map.130 = (bf16[32,2048]{1,0:T(8,128)(2,1)}, bf16[32,2048]{1,0:T(8,128)(2,1)}, f32[1024,128]{1,0:T(8,128)}, bf16[4096,128]{1,0:T(8,128)(2,1)}) custom-call(bf16[32,2048]{1,0:T(8,128)(2,1)} %get-tuple-element.12.left_in, bf16[1,32,2048]{2,1,0:T(8,128)(2,1)} %get-tuple-element.13.right_in, bf16[1024,128]{1,0:T(8,128)(2,1)} %get-tuple-element.14.weight_in, ...), custom_call_target="tpu_custom_call" | custom-call | tf_op jit(solution)/shard_map/pallas_call | solution.py:955

commit v7 on v6

--- a/solution.py
+++ b/solution.py
@@ -656,7 +656,6 @@
         return carry
 
     lax.fori_loop(0, extras, left_extra, 0)
-    after_left_extra()
 
     def left_main(t, carry):
         slot = slot_of(t)
@@ -664,11 +663,11 @@
         lanes = pl.ds(pl.multiple_of(t * span, span), span)
         for q in range(n_col):
             left_ref[q, :, lanes] = turned[q * share : (q + 1) * share].astype(bf16)
+        pl.when(t == min(1, steps - 1))(after_left_extra)
         pl.when(t == steps // parts - 1)(first_left)
         return carry
 
     lax.fori_loop(0, steps, left_main, 0)
-    after_left()
     pairs = [(t, label_of(t, 0), t) for t in range(steps)]
     for u in range(extras):
         pairs.append((*extra_of(jnp.int32(u)), steps + u))
@@ -688,9 +687,9 @@
         whole = jnp.concatenate(total, axis=1)
         for q in range(n_col):
             right_ref[q, :, lanes] = whole[q * share : (q + 1) * share].astype(bf16)
+        pl.when(c == min(1, chunks - 1))(after_left)
         pl.when(c == chunks // 2 - 1)(functools.partial(right_first, 0))
         pl.when(c == max(chunks - 2, chunks // 2))(functools.partial(right_second, 0))
-        pl.when(c == chunks * 3 // 4)(during_right)
         return carry
 
     lax.fori_loop(0, chunks, right_main, 0)
@@ -716,13 +715,14 @@
                     pair = pair + turned[e * cols : (e + 1) * cols]
                 first = pl.multiple_of((t * tile + i + k) * cols, cols)
                 pair_out[pl.ds(first, cols), :] = (pair + bias_ref[...]).astype(bf16)
+        pl.when(t == min(1, steps - 1))(during_right)
         pl.when(t == min(3, steps - 1))(functools.partial(right_second, 1))
-        pl.when(t == steps // 2)(pair_second)
         pl.when(t == steps * 5 // 8)(functools.partial(right_third, 0))
         pl.when(t == steps - 1)(functools.partial(right_third, 1))
         return carry
 
     lax.fori_loop(0, steps, pairs_of, 0)
+    pair_second()
     finish()
     for t in range(ratio):
         pl.when(row * ratio + t != col)(out_right(t).wait_send)

time: 64.8 us -> 62.3 us (0.961)
  Pallas kernels: 64 us -> 61.4 us
    pallas_call x1, Pallas kernels: 60.5 us -> 57.9 us  [shards(): pl.pallas_call(functools.partial(core_kernel, n_row, n_col, ratio, rows,...]
where the time goes in v7:
time: 62.3 us; the launch traced here: 62 us
  Pallas kernels  61.4 us (99%)
  between operations  0.64 us (1%)
    pallas_call x1, Pallas kernels, shards(): pl.pallas_call(functools.partial(core_kernel, n_row, n_col, ratio, rows,...  57.9 us
    pallas_call x1, Pallas kernels, shards(): pl.pallas_call(functools.partial(finish_kernel, fused, blocks), in_specs=...  3.44 us

profile of v7, /device:TPU:1, one launch (start us, length us, event | category | flops | bytes accessed | tf_op | source)
XLA Modules:
  0.0 62.0 jit_solution(9825520974797350896)
XLA Ops:
  0.6 57.9 %shard_map.129 = (bf16[4096,128]{1,0:T(8,128)(2,1)}, bf16[32,2048]{1,0:T(8,128)(2,1)}, bf16[1,32,2048]{2,1,0:T(8,128)(2,1)}, bf16[1024,128]{1,0:T(8,128)(2,1)}) custom-call(s32[256]{0:T(256)} %refs_0_.1, s32[8,8]{1,0:T(8,128)} %refs_1_.1, bf16[1024,128]{1,0:T(8,128)(2,1)} %refs_2_.1, f32[1,128]{1,0:T(1,128)} %bitcast.12, bf16[4096,128]{1,0:T(8,128)(2,1)} %bitcast.7, ...), custom_call_target="tpu_custom_call" | custom-call | tf_op jit(solution)/shard_map/pallas_call | solution.py:884
  58.6 3.4 %shard_map.130 = (bf16[32,2048]{1,0:T(8,128)(2,1)}, bf16[32,2048]{1,0:T(8,128)(2,1)}, f32[1024,128]{1,0:T(8,128)}, bf16[4096,128]{1,0:T(8,128)(2,1)}) custom-call(bf16[32,2048]{1,0:T(8,128)(2,1)} %get-tuple-element.12.left_in, bf16[1,32,2048]{2,1,0:T(8,128)(2,1)} %get-tuple-element.13.right_in, bf16[1024,128]{1,0:T(8,128)(2,1)} %get-tuple-element.14.weight_in, ...), custom_call_target="tpu_custom_call" | custom-call | tf_op jit(solution)/shard_map/pallas_call | solution.py:955
